TPU v7x, 128 devices: a whole 4x4x4 slice. The times are simulated.
128 devices in a mesh: kpt: 1, col: 16 (over z, y), row: 8 (over x, core).
Axes of the slice: x: 4, y: 4, z: 4, core: 2. Of those that a mesh axis runs over, the one named last changes fastest.
Arguments:
- v_panels: float32 [8192, 8192], P(('kpt', 'row'), 'col')
- t_fac: float32 [128, 64, 64], P('kpt')
- z_in: float32 [8192, 8192], P(('kpt', 'row'), 'col')
- l_chol: float32 [8192, 8192], P(('kpt', 'row'), 'col')
Outputs:
- output: float32 [8192, 8192], P(('kpt', 'row'), 'col')
All inputs are finite; a program needn't handle non-finite values.
Results may differ from a plain program's by a relative error of at most 0.001.
Values sent between devices are 32-bit elements.
A program may use at most 1 GiB of HBM per device.

v0:
```python
import jax
import jax.numpy as jnp
from jax import lax
from jax.sharding import PartitionSpec as P

PREC_HIGH = lax.Precision.HIGHEST
CONTRACT_ROWS = (((0,), (0,)), ((), ()))


def solution(mesh):
    row_devs = mesh.shape['row']
    col_devs = mesh.shape['col']
    mat_spec = P(('kpt', 'row'), 'col')
    fac_spec = P('kpt', None, None)

    def local_work(v_loc, t_loc, z_loc, l_loc):
        block_len = t_loc.shape[-1]
        slot_count = v_loc.shape[1] // block_len
        row_idx = lax.axis_index('row')

        def house_group(step_id, z_cur):
            slot_pos = slot_count - 1 - step_id
            v_mine = lax.dynamic_slice_in_dim(v_loc, slot_pos * block_len, block_len, axis=1)
            v_group = lax.all_gather(v_mine, 'col', axis=1, tiled=True)
            t_group = lax.dynamic_slice_in_dim(t_loc, slot_pos * col_devs, col_devs, axis=0)

            def house_one(inner_pos, z_acc):
                col_owner = col_devs - 1 - inner_pos
                v_cur = lax.dynamic_slice_in_dim(v_group, col_owner * block_len, block_len, axis=1)
                t_cur = lax.dynamic_index_in_dim(t_group, col_owner, keepdims=False)
                s_part = lax.dot_general(v_cur, z_acc, CONTRACT_ROWS, precision=PREC_HIGH, preferred_element_type=jnp.float32)
                s_sum = lax.psum(s_part, 'row')
                w_part = lax.dot_general(t_cur, s_sum, CONTRACT_ROWS, precision=PREC_HIGH, preferred_element_type=jnp.float32)
                return z_acc - jnp.dot(v_cur, w_part, precision=PREC_HIGH, preferred_element_type=jnp.float32)

            return lax.fori_loop(0, col_devs, house_one, z_cur)

        y_loc = lax.fori_loop(0, slot_count, house_group, z_loc)

        def solve_group(step_id, x_cur):
            slot_pos = slot_count - 1 - step_id
            l_mine = lax.dynamic_slice_in_dim(l_loc, slot_pos * block_len, block_len, axis=1)
            l_group = lax.all_gather(l_mine, 'col', axis=1, tiled=True)

            def solve_one(inner_pos, x_acc):
                col_owner = col_devs - 1 - inner_pos
                panel_id = slot_pos * col_devs + col_owner
                row_slot = panel_id // row_devs
                l_cur = lax.dynamic_slice_in_dim(l_group, col_owner * block_len, block_len, axis=1)
                s_part = lax.dot_general(l_cur, x_acc, CONTRACT_ROWS, precision=PREC_HIGH, preferred_element_type=jnp.float32)
                s_sum = lax.psum(s_part, 'row')
                l_diag = lax.dynamic_slice_in_dim(l_cur, row_slot * block_len, block_len, axis=0)
                y_blk = lax.dynamic_slice_in_dim(y_loc, row_slot * block_len, block_len, axis=0)
                x_blk = lax.linalg.triangular_solve(l_diag, y_blk - s_sum, left_side=True, lower=True, transpose_a=True)
                old_blk = lax.dynamic_slice_in_dim(x_acc, row_slot * block_len, block_len, axis=0)
                new_blk = jnp.where(row_idx == panel_id % row_devs, x_blk, old_blk)
                return lax.dynamic_update_slice_in_dim(x_acc, new_blk, row_slot * block_len, axis=0)

            return lax.fori_loop(0, col_devs, solve_one, x_cur)

        return lax.fori_loop(0, slot_count, solve_group, jnp.zeros_like(y_loc))

    return jax.shard_map(local_work, mesh=mesh, in_specs=(mat_spec, fac_spec, mat_spec, mat_spec), out_specs=mat_spec, check_vma=False)
```

profile of v0, /device:TPU:1, one launch (start us, length us, event | category | flops | bytes accessed | tf_op | source)
XLA Modules:
  0.0 17714.1 jit_solution(4297017765894734616)
XLA Ops:
  15.6 8933.2 %while.89 = (s32[]{:T(128)}, f32[1024,512]{1,0:T(8,128)S(1)}, f32[1024,512]{0,1:T(8,128)}, f32[128,64,64]{2,1,0:T(8,128)}, s32[]{:T(128)}, /*index=5*/s32[]{:T(1...) while((s32[]{:T(128)}, f32[1024,512]{1,0:T(8,128)S(1)}, ...), condition=%wide.region_4.5_spmd, body=%wide.region_0.4_spmd.sunk | while | flops 831029248 | bytes 22577792 | solution.py:38
  72.8 1061.4 %while.92 = (s32[]{:T(128)}, f32[1024,512]{1,0:T(8,128)S(1)}, f32[1024,1024]{0,1:T(8,128)}, f32[16,64,64]{2,1,0:T(8,128)S(1)}, s32[]{:T(128)}, /*index=5*/s32[]{:T(128)}, s32[]{:T(128)}, s32[]{:T(128)}, s32[]{:T(128)}, s32[]{:T(128)}) while((s32[]{:T(128)}, f32[1024,512]{1,0:T(8,128)S(1)}, f32[1024,1024]{0,1:T(8,128)}, ...), condition=%wide.region_3.3_spmd, body=%wide.region_1.2_spmd.sunk | while | flops 831029248 | bytes 8159477 | solution.py:36
  472.8 58.9 all-reduce.5.cloned.1.call-done
  1189.0 1061.3 %while.92 = (s32[]{:T(128)}, f32[1024,512]{1,0:T(8,128)S(1)}, f32[1024,1024]{0,1:T(8,128)}, f32[16,64,64]{2,1,0:T(8,128)S(1)}, s32[]{:T(128)}, /*index=5*/s32[]{:T(128)}, s32[]{:T(128)}, s32[]{:T(128)}, s32[]{:T(128)}, s32[]{:T(128)}) while((s32[]{:T(128)}, f32[1024,512]{1,0:T(8,128)S(1)}, f32[1024,1024]{0,1:T(8,128)}, ...), condition=%wide.region_3.3_spmd, body=%wide.region_1.2_spmd.sunk | while | flops 831029248 | bytes 8159477 | solution.py:36
  2187.0 58.9 all-reduce.5.cloned.1.call-done
  2305.5 1061.3 %while.92 = (s32[]{:T(128)}, f32[1024,512]{1,0:T(8,128)S(1)}, f32[1024,1024]{0,1:T(8,128)}, f32[16,64,64]{2,1,0:T(8,128)S(1)}, s32[]{:T(128)}, /*index=5*/s32[]{:T(128)}, s32[]{:T(128)}, s32[]{:T(128)}, s32[]{:T(128)}, s32[]{:T(128)}) while((s32[]{:T(128)}, f32[1024,512]{1,0:T(8,128)S(1)}, f32[1024,1024]{0,1:T(8,128)}, ...), condition=%wide.region_3.3_spmd, body=%wide.region_1.2_spmd.sunk | while | flops 831029248 | bytes 8159477 | solution.py:36
  2639.0 58.9 all-reduce.5.cloned.1.call-done
  3422.0 1061.4 %while.92 = (s32[]{:T(128)}, f32[1024,512]{1,0:T(8,128)S(1)}, f32[1024,1024]{0,1:T(8,128)}, f32[16,64,64]{2,1,0:T(8,128)S(1)}, s32[]{:T(128)}, /*index=5*/s32[]{:T(128)}, s32[]{:T(128)}, s32[]{:T(128)}, s32[]{:T(128)}, s32[]{:T(128)}) while((s32[]{:T(128)}, f32[1024,512]{1,0:T(8,128)S(1)}, f32[1024,1024]{0,1:T(8,128)}, ...), condition=%wide.region_3.3_spmd, body=%wide.region_1.2_spmd.sunk | while | flops 831029248 | bytes 8159477 | solution.py:36
  3954.9 58.9 all-reduce.5.cloned.1.call-done
  4220.7 58.9 all-reduce.5.cloned.1.call-done
  4538.5 1061.4 %while.92 = (s32[]{:T(128)}, f32[1024,512]{1,0:T(8,128)S(1)}, f32[1024,1024]{0,1:T(8,128)}, f32[16,64,64]{2,1,0:T(8,128)S(1)}, s32[]{:T(128)}, /*index=5*/s32[]{:T(128)}, s32[]{:T(128)}, s32[]{:T(128)}, s32[]{:T(128)}, s32[]{:T(128)}) while((s32[]{:T(128)}, f32[1024,512]{1,0:T(8,128)S(1)}, f32[1024,1024]{0,1:T(8,128)}, ...), condition=%wide.region_3.3_spmd, body=%wide.region_1.2_spmd.sunk | while | flops 831029248 | bytes 8159477 | solution.py:36
  5137.9 58.9 all-reduce.5.cloned.1.call-done
  5270.8 58.9 all-reduce.5.cloned.1.call-done
  5536.6 58.9 all-reduce.5.cloned.1.call-done
  5654.8 1061.3 %while.92 = (s32[]{:T(128)}, f32[1024,512]{1,0:T(8,128)S(1)}, f32[1024,1024]{0,1:T(8,128)}, f32[16,64,64]{2,1,0:T(8,128)S(1)}, s32[]{:T(128)}, /*index=5*/s32[]{:T(128)}, s32[]{:T(128)}, s32[]{:T(128)}, s32[]{:T(128)}, s32[]{:T(128)}) while((s32[]{:T(128)}, f32[1024,512]{1,0:T(8,128)S(1)}, f32[1024,1024]{0,1:T(8,128)}, ...), condition=%wide.region_3.3_spmd, body=%wide.region_1.2_spmd.sunk | while | flops 831029248 | bytes 8159477 | solution.py:36
  6586.3 58.9 all-reduce.5.cloned.1.call-done
  6771.0 1061.3 %while.92 = (s32[]{:T(128)}, f32[1024,512]{1,0:T(8,128)S(1)}, f32[1024,1024]{0,1:T(8,128)}, f32[16,64,64]{2,1,0:T(8,128)S(1)}, s32[]{:T(128)}, /*index=5*/s32[]{:T(128)}, s32[]{:T(128)}, s32[]{:T(128)}, s32[]{:T(128)}, s32[]{:T(128)}) while((s32[]{:T(128)}, f32[1024,512]{1,0:T(8,128)S(1)}, f32[1024,1024]{0,1:T(8,128)}, ...), condition=%wide.region_3.3_spmd, body=%wide.region_1.2_spmd.sunk | while | flops 831029248 | bytes 8159477 | solution.py:36
  7171.0 58.9 all-reduce.5.cloned.1.call-done
  7303.8 58.9 all-reduce.5.cloned.1.call-done
  7436.7 58.9 all-reduce.5.cloned.1.call-done
  7887.5 1061.4 %while.92 = (s32[]{:T(128)}, f32[1024,512]{1,0:T(8,128)S(1)}, f32[1024,1024]{0,1:T(8,128)}, f32[16,64,64]{2,1,0:T(8,128)S(1)}, s32[]{:T(128)}, /*index=5*/s32[]{:T(128)}, s32[]{:T(128)}, s32[]{:T(128)}, s32[]{:T(128)}, s32[]{:T(128)}) while((s32[]{:T(128)}, f32[1024,512]{1,0:T(8,128)S(1)}, f32[1024,1024]{0,1:T(8,128)}, ...), condition=%wide.region_3.3_spmd, body=%wide.region_1.2_spmd.sunk | while | flops 831029248 | bytes 8159477 | solution.py:36
  8354.0 58.9 all-reduce.5.cloned.1.call-done
  8553.3 58.9 all-reduce.5.cloned.1.call-done
  8953.4 8754.2 %while.91 = (s32[]{:T(128)}, f32[1024,512]{1,0:T(8,128)}, f32[1024,512]{0,1:T(8,128)}, s32[]{:T(128)}, f32[1024,512]{1,0:T(8,128)S(1)}, /*index=5*/s32[]{:T(128)...) while((s32[]{:T(128)}, f32[1024,512]{1,0:T(8,128)}, ...), condition=%wide.region_9.10_spmd, body=%wide.region_5.9_spmd.sunk | while | flops 427925536 | bytes 26413528 | solution.py:61
  9013.9 1033.7 %while.93 = (s32[]{:T(128)}, f32[1024,512]{1,0:T(8,128)}, s32[]{:T(128)}, s32[]{:T(128)}, f32[1024,1024]{1,0:T(8,128)}, /*index=5*/f32[1024,512]{1,0:T(8,128)S(1...) while((s32[]{:T(128)}, f32[1024,512]{1,0:T(8,128)}, ...), condition=%wide.region_8.8_spmd, body=%wide.region_6.7_spmd.sunk | while | flops 427925536 | bytes 4130849 | solution.py:59
  10107.8 1033.8 %while.93 = (s32[]{:T(128)}, f32[1024,512]{1,0:T(8,128)}, s32[]{:T(128)}, s32[]{:T(128)}, f32[1024,1024]{1,0:T(8,128)}, /*index=5*/f32[1024,512]{1,0:T(8,128)S(1...) while((s32[]{:T(128)}, f32[1024,512]{1,0:T(8,128)}, ...), condition=%wide.region_8.8_spmd, body=%wide.region_6.7_spmd.sunk | while | flops 427925536 | bytes 4130849 | solution.py:59
  11202.2 1033.9 %while.93 = (s32[]{:T(128)}, f32[1024,512]{1,0:T(8,128)}, s32[]{:T(128)}, s32[]{:T(128)}, f32[1024,1024]{1,0:T(8,128)}, /*index=5*/f32[1024,512]{1,0:T(8,128)S(1...) while((s32[]{:T(128)}, f32[1024,512]{1,0:T(8,128)}, ...), condition=%wide.region_8.8_spmd, body=%wide.region_6.7_spmd.sunk | while | flops 427925536 | bytes 4130849 | solution.py:59
  12296.6 1033.8 %while.93 = (s32[]{:T(128)}, f32[1024,512]{1,0:T(8,128)}, s32[]{:T(128)}, s32[]{:T(128)}, f32[1024,1024]{1,0:T(8,128)}, /*index=5*/f32[1024,512]{1,0:T(8,128)S(1...) while((s32[]{:T(128)}, f32[1024,512]{1,0:T(8,128)}, ...), condition=%wide.region_8.8_spmd, body=%wide.region_6.7_spmd.sunk | while | flops 427925536 | bytes 4130849 | solution.py:59
  13390.9 1033.9 %while.93 = (s32[]{:T(128)}, f32[1024,512]{1,0:T(8,128)}, s32[]{:T(128)}, s32[]{:T(128)}, f32[1024,1024]{1,0:T(8,128)}, /*index=5*/f32[1024,512]{1,0:T(8,128)S(1...) while((s32[]{:T(128)}, f32[1024,512]{1,0:T(8,128)}, ...), condition=%wide.region_8.8_spmd, body=%wide.region_6.7_spmd.sunk | while | flops 427925536 | bytes 4130849 | solution.py:59
  14485.3 1033.9 %while.93 = (s32[]{:T(128)}, f32[1024,512]{1,0:T(8,128)}, s32[]{:T(128)}, s32[]{:T(128)}, f32[1024,1024]{1,0:T(8,128)}, /*index=5*/f32[1024,512]{1,0:T(8,128)S(1...) while((s32[]{:T(128)}, f32[1024,512]{1,0:T(8,128)}, ...), condition=%wide.region_8.8_spmd, body=%wide.region_6.7_spmd.sunk | while | flops 427925536 | bytes 4130849 | solution.py:59
  15579.7 1033.8 %while.93 = (s32[]{:T(128)}, f32[1024,512]{1,0:T(8,128)}, s32[]{:T(128)}, s32[]{:T(128)}, f32[1024,1024]{1,0:T(8,128)}, /*index=5*/f32[1024,512]{1,0:T(8,128)S(1...) while((s32[]{:T(128)}, f32[1024,512]{1,0:T(8,128)}, ...), condition=%wide.region_8.8_spmd, body=%wide.region_6.7_spmd.sunk | while | flops 427925536 | bytes 4130849 | solution.py:59
  16673.8 1033.8 %while.93 = (s32[]{:T(128)}, f32[1024,512]{1,0:T(8,128)}, s32[]{:T(128)}, s32[]{:T(128)}, f32[1024,1024]{1,0:T(8,128)}, /*index=5*/f32[1024,512]{1,0:T(8,128)S(1...) while((s32[]{:T(128)}, f32[1024,512]{1,0:T(8,128)}, ...), condition=%wide.region_8.8_spmd, body=%wide.region_6.7_spmd.sunk | while | flops 427925536 | bytes 4130849 | solution.py:59
  (1738 shorter events, 16860.0 us)
Async XLA Ops:
  9529.9 62.8 all-reduce.3.cloned.1.call-start
  9594.6 62.8 all-reduce.3.cloned.1.call-start
  10235.7 62.8 all-reduce.3.cloned.1.call-start
  10300.5 62.8 all-reduce.3.cloned.1.call-start
  10365.2 62.8 all-reduce.3.cloned.1.call-start
  10429.9 62.8 all-reduce.3.cloned.1.call-start
  10494.6 62.8 all-reduce.3.cloned.1.call-start
  10559.3 62.8 all-reduce.3.cloned.1.call-start
  10624.0 62.8 all-reduce.3.cloned.1.call-start
  10688.7 62.8 all-reduce.3.cloned.1.call-start
  10753.4 62.8 all-reduce.3.cloned.1.call-start
  10818.1 62.8 all-reduce.3.cloned.1.call-start
  10882.8 62.8 all-reduce.3.cloned.1.call-start
  10947.5 62.8 all-reduce.3.cloned.1.call-start
  11012.2 62.8 all-reduce.3.cloned.1.call-start
  11076.9 62.8 all-reduce.3.cloned.1.call-start
  11330.1 62.8 all-reduce.3.cloned.1.call-start
  11394.8 62.8 all-reduce.3.cloned.1.call-start
  12424.5 62.8 all-reduce.3.cloned.1.call-start
  12489.2 62.8 all-reduce.3.cloned.1.call-start
  12553.9 62.8 all-reduce.3.cloned.1.call-start
  12618.6 62.8 all-reduce.3.cloned.1.call-start
  12683.3 62.8 all-reduce.3.cloned.1.call-start
  12748.0 62.8 all-reduce.3.cloned.1.call-start
  12812.7 62.8 all-reduce.3.cloned.1.call-start
  12877.5 62.8 all-reduce.3.cloned.1.call-start
  12942.2 62.8 all-reduce.3.cloned.1.call-start
  13006.9 62.8 all-reduce.3.cloned.1.call-start
  13071.6 62.8 all-reduce.3.cloned.1.call-start
  13583.6 62.8 all-reduce.3.cloned.1.call-start
  14613.3 62.8 all-reduce.3.cloned.1.call-start
  14678.0 62.8 all-reduce.3.cloned.1.call-start
  (242 other events, 14829.4 us)
Sparse Core Ops, SparseCore 0:
  9533.9 58.7 all-reduce.2
  9598.6 58.7 all-reduce.2
  9663.3 58.7 all-reduce.2
  9728.0 58.7 all-reduce.2
  9792.7 58.7 all-reduce.2
  9857.4 58.7 all-reduce.2
  9922.2 58.7 all-reduce.2
  9986.9 58.7 all-reduce.2
  11334.1 58.7 all-reduce.2
  11398.8 58.7 all-reduce.2
  11463.5 58.7 all-reduce.2
  11528.2 58.7 all-reduce.2
  11592.9 58.7 all-reduce.2
  11657.6 58.7 all-reduce.2
  11722.4 58.7 all-reduce.2
  11787.1 58.7 all-reduce.2
  11851.8 58.7 all-reduce.2
  11916.5 58.7 all-reduce.2
  11981.2 58.7 all-reduce.2
  12045.9 58.7 all-reduce.2
  12110.6 58.7 all-reduce.2
  12175.3 58.7 all-reduce.2
  13587.6 58.7 all-reduce.2
  14617.2 58.7 all-reduce.2
  14682.0 58.7 all-reduce.2
  14746.7 58.7 all-reduce.2
  14811.4 58.7 all-reduce.2
  14876.1 58.7 all-reduce.2
  14940.8 58.7 all-reduce.2
  15005.5 58.7 all-reduce.2
  15070.2 58.7 all-reduce.2
  15134.9 58.7 all-reduce.2
  (240 shorter events, 13967.6 us)
where the time goes:
time: 17700 us
  waiting for transfers between devices  15200 us (86%)
  matrix products  1680 us (9%)
  other arithmetic  749 us (4%)
    psum x128, waiting for transfers between devices, house_one(): s_sum = lax.psum(s_part, 'row')  7530 us
    psum x128, waiting for transfers between devices, solve_one(): s_sum = lax.psum(s_part, 'row')  6780 us
    another operation x256, other arithmetic, solve_one(): lax.linalg.triangular_solve(l_diag, y_blk - s_sum, left_side=True, lower=...  749 us
    dot_general x128, matrix products, solve_one(): lax.dot_general(l_cur, x_acc, CONTRACT_ROWS, precision=PREC_HIGH, preferr...  489 us
    all_gather x8, waiting for transfers between devices, solve_group(): l_group = lax.all_gather(l_mine, 'col', axis=1, tiled=True)  427 us
    all_gather x8, waiting for transfers between devices, house_group(): v_group = lax.all_gather(v_mine, 'col', axis=1, tiled=True)  419 us
    dot_general x128, matrix products, house_one(): jnp.dot(v_cur, w_part, precision=PREC_HIGH, preferred_element_type=jnp.fl...  406 us
    dot_general x128, matrix products, house_one(): lax.dot_general(v_cur, z_acc, CONTRACT_ROWS, precision=PREC_HIGH, preferr...  381 us
  transfers between devices with their start and end apart: 272, of which 272 were waited for; matrix products, arithmetic and copies ran while one was open for 4% of the time, Pallas kernels for 0%

commit v1 on v0

v1 whole, which is shorter than its diff:
```python
import functools

import jax
import jax.numpy as jnp
from jax import lax
from jax.experimental import pallas as pl
from jax.experimental.pallas import tpu as pltpu
from jax.sharding import PartitionSpec as P

PREC_HIGH = lax.Precision.HIGHEST
MESH = pl.DeviceIdType.MESH
EDGE = 64
LANES = 128
STEP = 256


def _dot_nt(a, b):
    return lax.dot_general(a, b, (((1,), (1,)), ((), ())), precision=PREC_HIGH, preferred_element_type=jnp.float32)


def _dot_nn(a, b):
    return lax.dot_general(a, b, (((1,), (0,)), ((), ())), precision=PREC_HIGH, preferred_element_type=jnp.float32)


def _place():
    row, col = lax.axis_index("row"), lax.axis_index("col")
    return row, col, row // 2, row % 2


def _deal_kernel(dims, v_ref, l_ref, vb_ref, ld_ref, v_send, v_recv, d_send, d_recv):
    rows, cols, half = dims
    row, col, x, k = _place()
    chips = rows // 2
    groups = cols // rows
    mine, part = col // rows, col % rows
    sent = []
    for qp in range(half):
        blk = groups * (2 * qp + k) + mine
        here = blk == col
        sent.append((jnp.logical_not(here), pltpu.make_async_remote_copy(
            v_ref.at[qp], vb_ref.at[part], v_send.at[qp], v_recv.at[part],
            device_id={"col": blk, "row": row}, device_id_type=MESH,
        )))

        @pl.when(here)
        def _(qp=qp):
            pltpu.make_async_copy(v_ref.at[qp], vb_ref.at[part], v_recv.at[part]).start()

        src = l_ref.at[qp, :, pl.ds(pl.multiple_of(blk * LANES, LANES), LANES)]
        dst = ld_ref.at[part, :, pl.ds(pl.multiple_of(x * LANES, LANES), LANES)]

        @pl.when(here)
        def _(src=src, dst=dst):
            pltpu.make_async_copy(src, dst, d_recv.at[part, x]).start()

        for d in range(chips):
            x2 = lax.rem(x + d, chips)
            sent.append((jnp.logical_not(here) if d == 0 else None, pltpu.make_async_remote_copy(
                src, dst, d_send.at[qp, d], d_recv.at[part, x],
                device_id={"col": blk, "row": 2 * x2 + k}, device_id_type=MESH,
            )))

    def over_sent(act):
        for cond, copy in sent:
            if cond is None:
                act(copy)
            else:
                pl.when(cond)(functools.partial(act, copy))

    over_sent(lambda c: c.start())

    @pl.when((col // groups) % 2 == k)
    def _():
        for p in range(rows):
            pltpu.make_async_copy(v_ref.at[0], vb_ref.at[p], v_recv.at[p]).wait()
            for x2 in range(chips):
                there = ld_ref.at[p, :, pl.ds(x2 * LANES, LANES)]
                pltpu.make_async_copy(there, there, d_recv.at[p, x2]).wait()

    over_sent(lambda c: c.wait_send())


def _deal(v_own, l_own, rows, cols):
    half, _, lanes = v_own.shape
    chips = rows // 2
    return pl.pallas_call(
        functools.partial(_deal_kernel, (rows, cols, half)),
        out_shape=[
            jax.ShapeDtypeStruct((rows, EDGE, lanes), jnp.float32),
            jax.ShapeDtypeStruct((rows, EDGE, chips * LANES), jnp.float32),
        ],
        in_specs=[pl.BlockSpec(memory_space=pl.ANY)] * 2,
        out_specs=[pl.BlockSpec(memory_space=pl.ANY)] * 2,
        scratch_shapes=[
            pltpu.SemaphoreType.DMA((half,)),
            pltpu.SemaphoreType.DMA((rows,)),
            pltpu.SemaphoreType.DMA((half, chips)),
            pltpu.SemaphoreType.DMA((rows, chips)),
        ],
        compiler_params=pltpu.CompilerParams(has_side_effects=True),
        name="deal",
    )(v_own, l_own)


def _phase_kernel(solve, dims, own_ref, m_ref, in_ref, out_ref, gath, mg, *scratch):
    (blk, mbuf, sbuf, rs, wb, xr, v_send, v_recv, m_send, m_recv, blk_local, blk_send, blk_recv,
     mat_local, mat_send, mat_recv, free, rs_send, rs_recv, ag_send, ag_recv) = scratch
    rows, cols, half, nb, ncol = dims
    row, col, x, k = _place()
    chips = rows // 2
    groups = cols // rows
    size = rows * EDGE
    lanes = nb * LANES
    gcol = ncol // 2
    sl = gcol // chips
    mate = {"row": row + 1 - 2 * k, "col": col}

    def peer(d):
        return lax.rem(x + d, chips)

    def low(qp):
        return 2 * groups * qp * LANES

    def piece(qp, to):
        return own_ref.at[qp, :, pl.ds(low(qp), lanes - low(qp))], gath.at[to, qp, :, pl.ds(low(qp), lanes - low(qp))]

    my_q = col // groups
    my_m = (my_q // 2) * groups + col % groups
    m_mine = my_q % 2 == k

    for qp in reversed(range(half)):
        src, dst = piece(qp, col)
        pltpu.make_async_copy(src, dst, v_recv.at[qp, col]).start()

        def send_slot(d, carry, src=src, dst=dst, qp=qp):
            pltpu.make_async_remote_copy(
                src, dst, v_send.at[qp, d], v_recv.at[qp, col],
                device_id={"row": row, "col": lax.rem(col + d, cols)}, device_id_type=MESH,
            ).start()
            return carry

        lax.fori_loop(1, cols, send_slot, 0)
        if qp == half - 1:

            @pl.when(m_mine)
            def _():
                pltpu.make_async_copy(m_ref, mg.at[my_m], m_recv.at[my_m]).start()

                def send_mat(d, carry):
                    pltpu.make_async_remote_copy(
                        m_ref, mg.at[my_m], m_send.at[d], m_recv.at[my_m],
                        device_id={"row": row, "col": lax.rem(col + d, cols)}, device_id_type=MESH,
                    ).start()
                    return carry

                lax.fori_loop(1, cols, send_mat, 0)

    def owner_of(j):
        return (j // groups) % 2

    def by_class(j, body):
        for qp in range(half):
            pl.when((j // groups) // 2 == qp)(functools.partial(body, qp))

    def blk_copies(j, qp):
        s, h = j % 2, j % groups
        src = gath.at[pl.ds(h * rows, rows), qp, :, pl.ds(low(qp), lanes - low(qp))]
        dst = blk.at[s, :, :, pl.ds(low(qp), lanes - low(qp))]
        here = pltpu.make_async_copy(src, dst, blk_local.at[s])
        there = pltpu.make_async_remote_copy(
            src, dst, blk_send.at[s], blk_recv.at[s], device_id=mate, device_id_type=MESH
        )
        return here, there

    def mat_copies(j):
        s = j % 2
        src = mg.at[((j // groups) // 2) * groups + j % groups]
        here = pltpu.make_async_copy(src, mbuf.at[s], mat_local.at[s])
        there = pltpu.make_async_remote_copy(
            src, mbuf.at[s], mat_send.at[s], mat_recv.at[s], device_id=mate, device_id_type=MESH
        )
        return here, there

    def prefetch(j, first):
        @pl.when(owner_of(j) == k)
        def _():
            h, q = j % groups, j // groups

            def arrived(qp):
                def one(p, carry):
                    _, dst = piece(qp, h * rows + p)
                    pltpu.make_async_copy(dst, dst, v_recv.at[qp, h * rows + p]).wait()
                    return carry

                lax.fori_loop(0, rows, one, 0)

            by_class(j, arrived)
            slot = (q // 2) * groups + h
            pltpu.make_async_copy(mg.at[slot], mg.at[slot], m_recv.at[slot]).wait()
            if not first:

                @pl.when(owner_of(j) == k)
                def _():
                    pl.semaphore_wait(free.at[j % 2], 1)

            def go(qp):
                here, there = blk_copies(j, qp)
                here.start()
                there.start()

            by_class(j, go)
            here, there = mat_copies(j)
            here.start()
            there.start()

    def wait_blk(j):
        mine = owner_of(j) == k

        def one(qp):
            here, there = blk_copies(j, qp)

            @pl.when(mine)
            def _():
                here.wait()

            @pl.when(jnp.logical_not(mine))
            def _():
                there.wait_recv()

        by_class(j, one)
        here, there = mat_copies(j)

        @pl.when(mine)
        def _():
            here.wait()

        @pl.when(jnp.logical_not(mine))
        def _():
            there.wait_recv()

    def release(j):
        @pl.when(owner_of(j) == k)
        def _():
            by_class(j, lambda qp: blk_copies(j, qp)[1].wait_send())
            mat_copies(j)[1].wait_send()

        @pl.when(j >= 2)
        def _():
            @pl.when(owner_of(j - 2) != k)
            def _():
                pl.semaphore_signal(free.at[j % 2], inc=1, device_id=mate, device_id_type=MESH)

            prefetch(j - 2, False)

    def cut(s, i):
        return blk[s, :, :, pl.ds(pl.multiple_of(i * STEP, STEP), STEP)].reshape(size, STEP)

    def rs_copy(par, g, d):
        x2 = peer(d)
        return pltpu.make_async_remote_copy(
            sbuf.at[par, g, pl.ds(pl.multiple_of(x2 * sl, sl), sl)], rs.at[g, d - 1],
            rs_send.at[g, d - 1], rs_recv.at[g, d - 1],
            device_id={"row": 2 * x2 + k, "col": col}, device_id_type=MESH,
        )

    def send_partial(par, g):
        for d in range(1, chips):
            rs_copy(par, g, d).start()

    def gather_sum(par, g):
        for d in range(1, chips):
            rs_copy(par, g, d).wait_recv()
        total = sbuf[par, g, pl.ds(pl.multiple_of(x * sl, sl), sl)]
        for d in range(1, chips):
            total = total + rs[g, d - 1]
        for d in range(1, chips):
            rs_copy(par, g, d).wait_send()
        return total

    def state(ref, g, i):
        return ref[pl.ds(g * gcol, gcol), pl.ds(pl.multiple_of(i * STEP, STEP), STEP)]

    def project(par, g, s, ref, first, limit):
        sbuf[par, g] = jnp.zeros((gcol, size), jnp.float32)

        def one(i, carry):
            sbuf[par, g] += _dot_nt(state(ref, g, i), cut(s, i))
            return carry

        lax.fori_loop(first, limit, one, 0)

    top = nb - 1
    whole = nb * LANES // STEP
    prefetch(top, True)
    prefetch(top - 1, True)

    if not solve:
        out_ref[...] = in_ref[...]
        mine_rows = pl.ds(pl.multiple_of(x * sl, sl), sl)

        def ag_copy(g, d):
            return pltpu.make_async_remote_copy(
                wb.at[g, mine_rows], wb.at[g, mine_rows], ag_send.at[g, d - 1], ag_recv.at[g, d - 1],
                device_id={"row": 2 * peer(d) + k, "col": col}, device_id_type=MESH,
            )

        def ag_wait(g, d):
            rows_of = pl.ds(pl.multiple_of(peer(chips - d) * sl, sl), sl)
            pltpu.make_async_copy(wb.at[g, rows_of], wb.at[g, rows_of], ag_recv.at[g, d - 1]).wait()

        wait_blk(top)
        for g in range(2):
            project(0, g, top % 2, out_ref, top // 2, whole)
            send_partial(0, g)

        def step(i, carry):
            j = top - i
            s = j % 2
            for g in range(2):
                wb[g, mine_rows] = _dot_nn(gather_sum(0, g), mbuf[s])
                for d in range(1, chips):
                    ag_copy(g, d).start()

            @pl.when(j > 0)
            def _():
                wait_blk(j - 1)

            for g in range(2):
                for d in range(1, chips):
                    ag_wait(g, d)

                def apply(n, carry, g=g, s=s):
                    at = pl.ds(g * gcol, gcol), pl.ds(pl.multiple_of(n * STEP, STEP), STEP)
                    out_ref[at] = out_ref[at] - _dot_nn(wb[g], cut(s, n))
                    return carry

                lax.fori_loop(j // 2, whole, apply, 0)
                for d in range(1, chips):
                    ag_copy(g, d).wait_send()

                @pl.when(j > 0)
                def _(g=g):
                    project(0, g, (j - 1) % 2, out_ref, (j - 1) // 2, whole)
                    send_partial(0, g)

            release(j)
            return carry

        lax.fori_loop(0, nb, step, 0)
    else:
        out_ref[...] = jnp.zeros_like(out_ref)

        def right_side(par, g, j):
            sbuf[par, g] = -sbuf[par, g]
            at = pl.ds(pl.multiple_of(x * LANES, LANES), LANES)
            sbuf[par, g, :, at] += in_ref[pl.ds(g * gcol, gcol), pl.ds(pl.multiple_of(j * LANES, LANES), LANES)]

        def aa_copy(g, d):
            x2 = peer(d)
            return pltpu.make_async_remote_copy(
                wb.at[g, pl.ds(0, sl), pl.ds(pl.multiple_of(x2 * LANES, LANES), LANES)],
                xr.at[g, pl.ds(pl.multiple_of(x * sl, sl), sl)], ag_send.at[g, d - 1], ag_recv.at[g, d - 1],
                device_id={"row": 2 * x2 + k, "col": col}, device_id_type=MESH,
            )

        def aa_wait(g, d):
            there = xr.at[g, pl.ds(pl.multiple_of(peer(chips - d) * sl, sl), sl)]
            pltpu.make_async_copy(there, there, ag_recv.at[g, d - 1]).wait()

        wait_blk(top)
        for g in range(2):
            sbuf[top % 2, g] = jnp.zeros((gcol, size), jnp.float32)
            right_side(top % 2, g, top)
            send_partial(top % 2, g)

        def step(i, carry):
            j = top - i
            par, nxt = j % 2, (j + 1) % 2

            @pl.when(j > 0)
            def _():
                wait_blk(j - 1)

            for g in range(2):

                @pl.when(j > 0)
                def _(g=g):
                    project(nxt, g, nxt, out_ref, (j + 1) // 2, whole)

                wb[g, pl.ds(0, sl)] = _dot_nn(gather_sum(par, g), mbuf[par])
                for d in range(1, chips):
                    aa_copy(g, d).start()
                xr[g, pl.ds(pl.multiple_of(x * sl, sl), sl)] = wb[
                    g, pl.ds(0, sl), pl.ds(pl.multiple_of(x * LANES, LANES), LANES)
                ]

            here = pl.ds(pl.multiple_of(j * LANES, LANES), LANES)
            for g in range(2):
                for d in range(1, chips):
                    aa_wait(g, d)
                out_ref[pl.ds(g * gcol, gcol), here] = xr[g]

                @pl.when(j > 0)
                def _(g=g):
                    sbuf[nxt, g] += _dot_nt(xr[g], blk[nxt, :, :, here].reshape(size, LANES))
                    right_side(nxt, g, j - 1)
                    send_partial(nxt, g)

                for d in range(1, chips):
                    aa_copy(g, d).wait_send()

            release(j)
            return carry

        lax.fori_loop(0, nb, step, 0)

    for qp in range(half):
        src, dst = piece(qp, col)

        def sent(d, carry, src=src, dst=dst, qp=qp):
            pltpu.make_async_remote_copy(
                src, dst, v_send.at[qp, d], v_recv.at[qp, col],
                device_id={"row": row, "col": lax.rem(col + d, cols)}, device_id_type=MESH,
            ).wait_send()
            return carry

        lax.fori_loop(1, cols, sent, 0)

    @pl.when(m_mine)
    def _():
        def sent(d, carry):
            pltpu.make_async_remote_copy(
                m_ref, mg.at[my_m], m_send.at[d], m_recv.at[my_m],
                device_id={"row": row, "col": lax.rem(col + d, cols)}, device_id_type=MESH,
            ).wait_send()
            return carry

        lax.fori_loop(1, cols, sent, 0)


def _phase(solve, own, factor, state, rows, cols):
    half, _, lanes = own.shape
    nb = lanes // LANES
    ncol = state.shape[0]
    chips, size, gcol = rows // 2, rows * EDGE, ncol // 2
    sl = gcol // chips
    dma = pltpu.SemaphoreType.DMA
    hbm, vmem = pl.BlockSpec(memory_space=pl.ANY), pl.BlockSpec(memory_space=pltpu.VMEM)
    outs = pl.pallas_call(
        functools.partial(_phase_kernel, solve, (rows, cols, half, nb, ncol)),
        out_shape=[
            jax.ShapeDtypeStruct(state.shape, jnp.float32),
            jax.ShapeDtypeStruct((cols, half, EDGE, lanes), jnp.float32),
            jax.ShapeDtypeStruct((nb // 2, size, size), jnp.float32),
        ],
        in_specs=[hbm, hbm, vmem],
        out_specs=[vmem, hbm, hbm],
        scratch_shapes=[
            pltpu.VMEM((2, rows, EDGE, lanes), jnp.float32),
            pltpu.VMEM((2, size, size), jnp.float32),
            pltpu.VMEM((2 if solve else 1, 2, gcol, size), jnp.float32),
            pltpu.VMEM((2, chips - 1, sl, size), jnp.float32),
            pltpu.VMEM((2, gcol, size), jnp.float32),
            pltpu.VMEM((2, gcol, LANES), jnp.float32),
            dma((half, cols)), dma((half, cols)), dma((cols,)), dma((nb // 2,)),
            dma((2,)), dma((2,)), dma((2,)), dma((2,)), dma((2,)), dma((2,)),
            pltpu.SemaphoreType.REGULAR((2,)),
            dma((2, chips - 1)), dma((2, chips - 1)), dma((2, chips - 1)), dma((2, chips - 1)),
        ],
        compiler_params=pltpu.CompilerParams(has_side_effects=True, vmem_limit_bytes=48 * 1024 * 1024),
        name="solve" if solve else "reflect",
    )(own, factor, state)
    return outs[0]


def _merge(diag, full):
    two, n, b, _ = diag.shape
    while n > 1:
        pairs = diag.reshape(two, n // 2, 2, b, b)
        d1, d2 = pairs[:, :, 0], pairs[:, :, 1]
        c21 = jnp.stack([full[:, (2 * i + 1) * b : (2 * i + 2) * b, 2 * i * b : (2 * i + 1) * b] for i in range(n // 2)], axis=1)
        mid = jnp.einsum("pnij,pnjk->pnik", d2, c21, precision=PREC_HIGH)
        off = -jnp.einsum("pnij,pnjk->pnik", mid, d1, precision=PREC_HIGH)
        zero = jnp.zeros_like(off)
        diag = jnp.concatenate([jnp.concatenate([d1, zero], axis=3), jnp.concatenate([off, d2], axis=3)], axis=2)
        n, b = n // 2, 2 * b
    return diag[:, 0]


def solution(mesh):
    rows, cols = mesh.shape["row"], mesh.shape["col"]
    groups = cols // rows
    mat_spec = P(("kpt", "row"), "col")
    fac_spec = P("kpt", None, None)
    swap = [(r, r + 1 - 2 * (r % 2)) for r in range(rows)]

    def local_work(v_loc, t_loc, z_loc, l_loc):
        nb = v_loc.shape[0] // EDGE
        size = rows * EDGE
        lanes = nb * LANES
        slots = v_loc.shape[1] // EDGE
        row, col = lax.axis_index("row"), lax.axis_index("col")
        k = row % 2

        def chip_rows(keep, send, axis):
            got = lax.ppermute(send, "row", swap)
            return jnp.stack([jnp.where(k == 0, keep, got), jnp.where(k == 0, got, keep)], axis=axis)

        def slots_of(m_loc):
            mt = m_loc.T.reshape(slots // 2, 2, EDGE, nb, EDGE)
            keep = lax.dynamic_index_in_dim(mt, k, 1, keepdims=False)
            send = lax.dynamic_index_in_dim(mt, 1 - k, 1, keepdims=False)
            return chip_rows(keep, send, 3).reshape(slots // 2, EDGE, lanes)

        v_own, l_own = slots_of(v_loc), slots_of(l_loc)
        half_cols = z_loc.shape[1] // 2
        zt = z_loc.T.reshape(2, half_cols, nb, EDGE)
        z_state = chip_rows(
            lax.dynamic_index_in_dim(zt, k, 0, keepdims=False), lax.dynamic_index_in_dim(zt, 1 - k, 0, keepdims=False), 2
        ).reshape(half_cols, lanes)

        v_blk, l_diag = _deal(v_own, l_own, rows, cols)
        held = (col // groups) % 2 == k
        vb = jnp.where(held, v_blk.reshape(size, lanes), 0.0)
        gram = lax.psum(_dot_nt(vb, vb), "row")
        l_blk = jnp.where(held, l_diag.reshape(size, size), jnp.eye(size, dtype=jnp.float32)).T
        t_blk = lax.dynamic_slice_in_dim(t_loc, col * rows, rows, axis=0)
        l_pan = jnp.stack([l_blk[i * EDGE : (i + 1) * EDGE, i * EDGE : (i + 1) * EDGE] for i in range(rows)])
        eye = jnp.broadcast_to(jnp.eye(EDGE, dtype=jnp.float32), l_pan.shape)
        l_inv = lax.linalg.triangular_solve(l_pan, eye, left_side=True, lower=True)
        factors = _merge(jnp.stack([t_blk, l_inv]), jnp.stack([gram, l_blk]))

        y_state = _phase(False, v_own, factors[0], z_state, rows, cols)
        x_state = _phase(True, l_own, factors[1], y_state, rows, cols)

        xs = x_state.reshape(half_cols, nb, 2, EDGE)
        keep = lax.dynamic_index_in_dim(xs, k, 2, keepdims=False).reshape(half_cols, nb * EDGE)
        send = lax.dynamic_index_in_dim(xs, 1 - k, 2, keepdims=False).reshape(half_cols, nb * EDGE)
        got = lax.ppermute(send, "row", swap)
        return jnp.concatenate([jnp.where(k == 0, keep, got), jnp.where(k == 0, got, keep)], axis=0).T

    return jax.shard_map(local_work, mesh=mesh, in_specs=(mat_spec, fac_spec, mat_spec, mat_spec), out_specs=mat_spec, check_vma=False)
```

time: 17700 us -> 1510 us (0.09)
  waiting for transfers between devices: 15200 us -> 70.3 us
  matrix products: 1680 us -> 11.3 us
  Pallas kernels: 0 us -> 1240 us
  other arithmetic: 749 us -> 56.2 us
    psum x256 -> x1, waiting for transfers between devices: 14300 us -> 67.6 us  [local_work(): gram = lax.psum(_dot_nt(vb, vb), 'row')]
    dot_general x512 -> x7, matrix products: 1430 us -> 10.7 us  [the longest x1 7.85 us: _dot_nt(): lax.dot_general(a, b, (((1,), (1,)), ((), ())), precision=PREC_HIGH, pref...]
    pallas_call x0 -> x3, Pallas kernels: none -> 1240 us  [the longest x2 1180 us: _phase(): pl.pallas_call(functools.partial(_phase_kernel, solve, (rows, cols, half,...]
    all_gather x16 -> x0, waiting for transfers between devices: 846 us -> none  [the longest x8 427 us: solve_group(): l_group = lax.all_gather(l_mine, 'col', axis=1, tiled=True)]
    another operation x256 -> x11, other arithmetic: 749 us -> 51.1 us  [the longest x3 39.6 us: local_work(): l_inv = lax.linalg.triangular_solve(l_pan, eye, left_side=True, lower=True)]
    another operation x128 -> x1, matrix products: 243 us -> 0.6 us  [local_work(): l_inv = lax.linalg.triangular_solve(l_pan, eye, left_side=True, lower=True)]
  transfers between devices with their start and end apart: 272 -> 5, of which waited for: 272 -> 2; matrix products, arithmetic and copies ran while one was open for 4% -> 8% of each run, Pallas kernels for 0% -> 0%
where the time goes in v1:
time: 1510 us; the launch traced here: 1490 us
  Pallas kernels  1240 us (82%)
  local copies, waits for them, and re-layouts  92.8 us (6%)
  waiting for transfers between devices  70.3 us (5%)
  other arithmetic  56.2 us (4%)
    pallas_call x2, Pallas kernels, _phase(): pl.pallas_call(functools.partial(_phase_kernel, solve, (rows, cols, half,...  1180 us
    psum x1, waiting for transfers between devices, local_work(): gram = lax.psum(_dot_nt(vb, vb), 'row')  67.6 us
    pallas_call x1, Pallas kernels, _deal(): pl.pallas_call(functools.partial(_deal_kernel, (rows, cols, half)), out_s...  64.2 us
    another operation x3, other arithmetic, local_work(): l_inv = lax.linalg.triangular_solve(l_pan, eye, left_side=True, lower=True)  39.6 us
  transfers between devices with their start and end apart: 5, of which 2 were waited for; matrix products, arithmetic and copies ran while one was open for 8% of the time, Pallas kernels for 0%

profile of v1, /device:TPU:1, one launch (start us, length us, event | category | flops | bytes accessed | tf_op | source)
XLA Modules:
  0.0 1487.5 jit_solution(10699135514506776255)
XLA Ops:
  6.5 3.7 reshape.201
  10.2 4.4 constant_dynamic-slice_fusion.3
  15.7 1.4 collective-permute-start.2
  17.1 6.0 reshape.194
  23.0 6.1 reshape.192
  29.1 14.3 constant_dynamic-slice_fusion.5
  43.4 6.1 copy.25
  49.4 6.1 copy.29
  56.3 1.9 constant_dynamic-slice_fusion.6
  58.2 2.2 copy.57
  60.5 6.3 copy.28
  66.7 4.4 copy.24
  71.2 1.4 select_bitcast_fusion.1
  72.7 1.9 copy.45.in_ref
  74.6 2.5 bitcast_select_fusion.3
  77.1 6.5 pad_maximum_fusion
  83.7 7.0 reshape.193.l_ref.own_ref
  90.7 1.9 fusion
  93.0 5.2 copy.30
  98.3 6.4 reshape.195.v_ref.own_ref
  104.7 64.2 %deal.1 = (f32[8,64,2048]{2,1,0:T(8,128)}, f32[8,64,512]{2,1,0:T(8,128)}) custom-call(f32[4,64,2048]{2,1,0:T(8,128)} %reshape.195.v_ref.own_ref, f32[4,64,2048]{2,1,0:T(8,128)} %reshape.193.l_ref.own_ref), custom_call_target="tpu_custom_call" | custom-call | tf_op jit(solution)/shard_map/deal/pallas_call | solution.py:86
  168.9 1.6 copy.31
  171.1 7.9 convolution_bitcast_fusion
  179.4 39.5 %custom-call.3 = f32[8,1,64,64]{2,3,1,0:T(8,128)S(1)} custom-call(f32[8,1,64,64]{3,2,1,0:T(8,128)S(1)} %broadcast_select_fusion.1), custom_call_target="InvertDiagBlocksLowerTriangular" | custom-call | tf_op jit(solution)/shard_map/triangular_solve | solution.py:530
  219.6 67.6 %all-reduce.5.cloned.1.call-done = f32[1,512,512]{2,1,0:T(8,128)} async-done(((f32[1,512,512]{2,1,0:T(8,128)}), f32[1,512,512]{2,1,0:T(8,128)}) %all-reduce.5.cloned.1.call-update) | async-done | bytes 1048592 | tf_op jit(solution)/shard_map/psum | solution.py:525
  292.5 1.4 copy-done.3
  293.9 590.8 %reflect.1 = (f32[256,2048]{1,0:T(8,128)S(1)}, f32[16,4,64,2048]{3,2,1,0:T(8,128)}, f32[8,512,512]{2,1,0:T(8,128)}) custom-call(f32[4,64,2048]{2,1,0:T(8,128)S(1)} %copy-done.3, f32[512,512]{1,0:T(8,128)S(1)} %get-tuple-element.29.m_ref, f32[256,2048]{1,0:T(8,128)} %copy.45.in_ref), custom_call_target="tpu_custom_call" | custom-call | tf_op jit(solution)/shard_map/reflect/pallas_call | solution.py:449
  886.1 585.6 %solve.1 = (f32[256,2048]{1,0:T(8,128)S(1)}, f32[16,4,64,2048]{3,2,1,0:T(8,128)}, f32[8,512,512]{2,1,0:T(8,128)}) custom-call(f32[4,64,2048]{2,1,0:T(8,128)S(1)} %copy-done.2, f32[512,512]{1,0:T(8,128)S(1)} %get-tuple-element.30.m_ref, f32[256,2048]{1,0:T(8,128)} %copy-done.4), custom_call_target="tpu_custom_call" | custom-call | tf_op jit(solution)/shard_map/solve/pallas_call | solution.py:449
  1471.7 1.8 copy.46
  1473.5 1.7 constant_dynamic-slice_fusion.1
  1475.3 2.6 collective-permute-done.3
  1478.1 1.6 maximum_bitcast_fusion
  (59 shorter events, 11.5 us)
Async XLA Ops:
  6.5 49.7 %copy-start = (f32[128,64,64]{0,2,1:T(8,128)S(1)}, f32[128,64,64]{0,2,1:T(8,128)}, u32[]{:S(2)}) copy-start(f32[128,64,64]{0,2,1:T(8,128)} %param.5) | copy-start | bytes 6291460
  6.5 280.6 %all-reduce.5.cloned.1.call-start = ((), (), s32[]{:S(2)}) async-start(), calls=%async_computation | async-start | bytes 2097152 | tf_op jit(solution)/shard_map/psum | solution.py:525
  15.7 55.5 %collective-permute-start.2 = (f32[256,16,64]{0,2,1:T(8,128)}, f32[256,16,64]{0,2,1:T(8,128)}, u32[]{:S(2)}, u32[]{:S(2)}) collective-permute-start(f32[256,16,64]{0,2,1:T(8,128)} %bitcast.152), channel_id=1, source_target_pairs={{0,1},{1,0},{2,3},{3,2},{4,5},{5,4},{6,7},{7,6},{8,9},{9,8},{10,11... | collective-permute-start | bytes 3145736 | tf_op jit(solution)/shard_map/ppermute | solution.py:506
  49.4 25.1 %collective-permute-start = (f32[4,64,16,64]{3,2,1,0:T(8,128)}, f32[4,64,16,64]{3,2,1,0:T(8,128)}, u32[]{:S(2)}, u32[]{:S(2)}) collective-permute-start(f32[4,64,16,64]{3,2,1,0:T(8,128)} %bitcast.166), channel_id=1, source_target_pairs={{0,1},{1,0},{2,3},{3,2},{4,5},{5,4},{6,7},{7,6},{8,9},{9,8},{10,11... | collective-permute-start | bytes 3145736 | tf_op jit(solution)/shard_map/ppermute | solution.py:506
  55.5 35.2 %collective-permute-start.1 = (f32[4,64,16,64]{3,2,1,0:T(8,128)}, f32[4,64,16,64]{3,2,1,0:T(8,128)}, u32[]{:S(2)}, u32[]{:S(2)}) collective-permute-start(f32[4,64,16,64]{3,2,1,0:T(8,128)} %bitcast.165), channel_id=1, source_target_pairs={{0,1},{1,0},{2,3},{3,2},{4,5},{5,4},{6,7},{7,6},{8,9},{9,8},{10,11... | collective-permute-start | bytes 3145736 | tf_op jit(solution)/shard_map/ppermute | solution.py:506
  60.4 6.3 copy-start.6
  83.7 7.1 copy-start.7
  288.4 1.2 copy-start.5
  292.3 1.6 copy-start.3
  293.9 592.2 %copy-start.2 = (f32[4,64,2048]{2,1,0:T(8,128)S(1)}, f32[4,64,2048]{2,1,0:T(8,128)}, u32[]{:S(2)}) copy-start(f32[4,64,2048]{2,1,0:T(8,128)} %reshape.193.l_ref.own_ref) | copy-start | bytes 6291460
  884.8 1.4 copy-start.4
  1475.2 2.7 collective-permute-start.3
  1478.1 2.3 copy-start.1
Sparse Core Ops, SparseCore 0:
  179.1 108.0 all-reduce.4

commit v2 on v0

v2 whole, which is shorter than its diff:
```python
import functools

import jax
import jax.numpy as jnp
from jax import lax
from jax.experimental import pallas as pl
from jax.experimental.pallas import tpu as pltpu
from jax.sharding import PartitionSpec as P

PREC_HIGH = lax.Precision.HIGHEST
MESH = pl.DeviceIdType.MESH
EDGE = 64
HALF = EDGE // 2
LANES = 128
STEP = 256
RING = 4


def _dot_nt(a, b):
    return lax.dot_general(a, b, (((1,), (1,)), ((), ())), precision=PREC_HIGH, preferred_element_type=jnp.float32)


def _dot_nn(a, b):
    return lax.dot_general(a, b, (((1,), (0,)), ((), ())), precision=PREC_HIGH, preferred_element_type=jnp.float32)


def _place():
    row, col = lax.axis_index("row"), lax.axis_index("col")
    return row, col, row // 2, row % 2


def _at(i, n):
    return pl.ds(pl.multiple_of(i * n, n), n)


def _prep_kernel(dims, v_ref, l_ref, z_ref, own, zs, vb, ld, vt, zt, loc, swap_s, swap_r, v_s, v_r, l_s, l_r):
    rows, cols, slots, pairs = dims
    row, col, x, k = _place()
    chips, groups = rows // 2, cols // rows
    part, grp = col % rows, col // rows
    mate = {"row": row + 1 - 2 * k, "col": col}
    width = pairs * STEP // 2

    def swaps(m, i):
        there = _at(2 * i + k, LANES)
        if m < 2:
            mine, theirs = vt.at[m, :, k, :, _at(i, LANES)], vt.at[m, :, 1 - k, :, _at(i, LANES)]
            dst = own.at[m, :, :, there]
        else:
            mine, theirs = zt.at[k, :, _at(i, LANES)], zt.at[1 - k, :, _at(i, LANES)]
            dst = zs.at[:, there]
        return (
            pltpu.make_async_copy(mine, dst, loc.at[m, i]),
            pltpu.make_async_remote_copy(
                theirs, dst, swap_s.at[m, i], swap_r.at[m, i], device_id=mate, device_id_type=MESH
            ),
        )

    for m, ref in enumerate((v_ref, l_ref, z_ref)):

        def turn(i, carry, m=m, ref=ref):
            block = ref[_at(i, LANES), :].T
            if m < 2:
                vt[m, :, :, :, _at(i, LANES)] = block.reshape(slots, 2, HALF, LANES)
            else:
                zt[:, :, _at(i, LANES)] = block.reshape(2, -1, LANES)
            for c in swaps(m, i):
                c.start()
            return carry

        lax.fori_loop(0, pairs, turn, 0)

    def swapped(m):
        def one(i, carry):
            here, there = swaps(m, i)
            here.wait()
            there.wait_recv()
            return carry

        lax.fori_loop(0, pairs, one, 0)

    def deal_v(q, kk):
        blk = groups * q + grp
        src = own.at[0, q, :, pl.ds(kk * width, width)]
        dst = vb.at[part, pl.ds(pl.multiple_of(k * HALF, HALF), HALF)]
        self_ = jnp.logical_and(blk == col, k == kk)
        here = pltpu.make_async_copy(src, dst, v_r.at[part, k])
        there = pltpu.make_async_remote_copy(
            src, dst, v_s.at[q, kk], v_r.at[part, k], device_id={"col": blk, "row": 2 * x + kk}, device_id_type=MESH
        )
        return self_, here, there

    def deal_l(q, d):
        blk = groups * q + grp
        src = own.at[1, q, :, _at(blk // 2, STEP)]
        dst = ld.at[part, pl.ds(pl.multiple_of(k * HALF, HALF), HALF), _at(x, STEP)]
        self_ = jnp.logical_and(blk == col, d == 0)
        here = pltpu.make_async_copy(src, dst, l_r.at[part, k, x])
        there = pltpu.make_async_remote_copy(
            src, dst, l_s.at[q, d], l_r.at[part, k, x],
            device_id={"col": blk, "row": lax.rem(row + d, rows)}, device_id_type=MESH,
        )
        return self_, here, there

    def send(self_, here, there):
        @pl.when(self_)
        def _():
            here.start()

        @pl.when(jnp.logical_not(self_))
        def _():
            there.start()

    def sent(self_, here, there):
        @pl.when(jnp.logical_not(self_))
        def _():
            there.wait_send()

    def over_v(act):
        def one(q, carry):
            for kk in range(2):
                act(*deal_v(q, kk))
            return carry

        lax.fori_loop(0, slots, one, 0)

    def over_l(act):
        def one(n, carry):
            act(*deal_l(n // rows, n % rows))
            return carry

        lax.fori_loop(0, slots * rows, one, 0)

    swapped(0)
    over_v(send)
    swapped(1)
    over_l(send)
    swapped(2)

    def got(n, carry):
        p, kk = n // 2, n % 2
        there = vb.at[p, pl.ds(pl.multiple_of(kk * HALF, HALF), HALF)]
        pltpu.make_async_copy(there, there, v_r.at[p, kk]).wait()
        for x2 in range(chips):
            there = ld.at[p, pl.ds(pl.multiple_of(kk * HALF, HALF), HALF), pl.ds(x2 * STEP, STEP)]
            pltpu.make_async_copy(there, there, l_r.at[p, kk, x2]).wait()
        return carry

    lax.fori_loop(0, 2 * rows, got, 0)
    over_v(sent)
    over_l(sent)

    def left(i, carry):
        for m in range(3):
            swaps(m, i)[1].wait_send()
        return carry

    lax.fori_loop(0, pairs, left, 0)


def _prep(v_loc, l_loc, z_loc, rows, cols):
    n_row, n_col = v_loc.shape
    slots, pairs = n_col // EDGE, n_row // LANES
    lanes, chips, ncol = 2 * n_row, rows // 2, z_loc.shape[1] // 2
    dma = pltpu.SemaphoreType.DMA
    hbm, vmem = pl.BlockSpec(memory_space=pl.ANY), pl.BlockSpec(memory_space=pltpu.VMEM)
    return pl.pallas_call(
        functools.partial(_prep_kernel, (rows, cols, slots, pairs)),
        out_shape=[
            jax.ShapeDtypeStruct((2, slots, HALF, lanes), jnp.float32),
            jax.ShapeDtypeStruct((ncol, lanes), jnp.float32),
            jax.ShapeDtypeStruct((rows, EDGE, lanes // 2), jnp.float32),
            jax.ShapeDtypeStruct((rows, EDGE, chips * STEP), jnp.float32),
        ],
        in_specs=[vmem] * 3,
        out_specs=[hbm] * 4,
        scratch_shapes=[
            pltpu.VMEM((2, slots, 2, HALF, n_row), jnp.float32),
            pltpu.VMEM((2, ncol, n_row), jnp.float32),
            dma((3, pairs)), dma((3, pairs)), dma((3, pairs)),
            dma((slots, 2)), dma((rows, 2)), dma((slots, rows)), dma((rows, 2, chips)),
        ],
        compiler_params=pltpu.CompilerParams(has_side_effects=True, vmem_limit_bytes=32 * 1024 * 1024),
        name="prep",
    )(v_loc, l_loc, z_loc)


def _main_kernel(dims, own_ref, m_ref, z_ref, out_ref, gath, mg, *scratch):
    (ys, blk, mbuf, sbuf, rs, wb, xr, ag_loc, ag_s, ag_r, blk_loc, blk_s, blk_r, mat_loc, mat_s, mat_r, free,
     rs_s, rs_r, ex_s, ex_r) = scratch
    rows, cols, slots, nb, ncol = dims
    row, col, x, k = _place()
    chips, groups = rows // 2, cols // rows
    size, lanes = rows * EDGE, nb * LANES
    gcol = ncol // 2
    sl = gcol // chips
    mate = {"row": row + 1 - 2 * k, "col": col}
    top, whole = nb - 1, nb // 2
    per = slots + 1
    s_a, s_b = 1 + (RING - 1) * k, RING - (RING - 1) * k
    a, b = (col // s_a) % RING, (col // s_b) % RING

    def plane(da, db):
        aa, bb = lax.rem(a + da, RING), lax.rem(b + db, RING)
        return {"row": row, "col": aa * s_a + bb * s_b}

    def low(q):
        return (groups * q // 2) * STEP

    class Slot:
        def __init__(self, kind, w, n):
            self.kind, self.w, self.n = kind, w, n

        def own(self):
            if self.kind == "m":
                return m_ref.at[self.w]
            return own_ref.at[self.w, self.kind, :, pl.ds(low(self.kind), lanes - low(self.kind))]

        def piece(self, bb, aa, part=None):
            if self.kind == "m":
                return mg.at[self.w, bb, aa] if part is None else mg.at[self.w, bb, aa, pl.ds(part * (size // 4), size // 4)]
            at = pl.ds(low(self.kind), lanes - low(self.kind))
            e = slice(None) if part is None else pl.ds(part * (HALF // 2), HALF // 2)
            return gath.at[self.w, self.kind, bb, aa, e, at]

        def bundle(self, bb, part=None):
            e = slice(None) if part is None else pl.ds(part * (RING // 2), RING // 2)
            if self.kind == "m":
                return mg.at[self.w, bb, e]
            return gath.at[self.w, self.kind, bb, e, :, pl.ds(low(self.kind), lanes - low(self.kind))]

        def copy(self, i):
            plus = i % 2 == 0
            d = 1 if plus else RING - 1
            back = RING - d
            if i < 2:
                src, dst, to = self.own(), self.piece(b, a), plane(d, 0)
            elif i < 4:
                src = dst = self.piece(b, lax.rem(a + back, RING), i % 2)
                to = plane(d, 0)
            elif i < 6:
                src = dst = self.bundle(b)
                to = plane(0, d)
            else:
                src = dst = self.bundle(lax.rem(b + back, RING), i % 2)
                to = plane(0, d)
            return pltpu.make_async_remote_copy(
                src, dst, ag_s.at[self.n, i], ag_r.at[self.n, i], device_id=to, device_id_type=MESH
            )

        def arrived(self, i):
            back = RING - 1 if i % 2 == 0 else 1
            if i < 2:
                dst = self.piece(b, lax.rem(a + back, RING))
            elif i < 4:
                dst = self.piece(b, lax.rem(a + 2, RING), i % 2)
            elif i < 6:
                dst = self.bundle(lax.rem(b + back, RING))
            else:
                dst = self.bundle(lax.rem(b + 2, RING), i % 2)
            pltpu.make_async_copy(dst, dst, ag_r.at[self.n, i]).wait()

        def kept(self):
            return pltpu.make_async_copy(self.own(), self.piece(b, a), ag_loc.at[self.n])

        def stage(self, s):
            if s == 0:
                self.kept().start()
                self.copy(0).start()
                self.copy(1).start()
            elif s == 1:
                for i in range(2):
                    self.arrived(i)
                    self.copy(2 + i).start()
            elif s == 2:
                self.arrived(2)
                self.arrived(3)
                self.kept().wait()
                self.copy(4).start()
                self.copy(5).start()
            elif s == 3:
                for i in range(4, 6):
                    self.arrived(i)
                    self.copy(2 + i).start()
            elif s == 4:
                self.arrived(6)
                self.arrived(7)
            else:
                for i in range(8):
                    self.copy(i).wait_send()

    def tick(t):
        for s in (5, 4, 3, 2, 1, 0):
            n = t - s

            @pl.when(jnp.logical_and(n >= 0, n < 2 * per))
            def _(s=s, n=n):
                w, pos = n // per, n % per
                for q in list(range(slots)) + ["m"]:
                    here = 1 if q == "m" else (0 if q == slots - 1 else slots - q)
                    pl.when(pos == here)(lambda q=q: Slot(q, w, n).stage(s))

    def block_of(n):
        w = n // nb
        j = top - n % nb
        return w, j, j // groups, j % groups, n % 2

    def blk_copies(n, q, p):
        w, j, _, h, s = block_of(n)
        c = h * rows + p
        src = gath.at[w, q, (c // s_b) % RING, (c // s_a) % RING, :, pl.ds(low(q), lanes - low(q))]
        dst = blk.at[s, p, pl.ds(pl.multiple_of(k * HALF, HALF), HALF), pl.ds(low(q), lanes - low(q))]
        here = pltpu.make_async_copy(src, dst, blk_loc.at[s, p])
        there = pltpu.make_async_remote_copy(
            src, dst, blk_s.at[s, p], blk_r.at[s, p], device_id=mate, device_id_type=MESH
        )
        return here, there

    def from_mate(n, q, p):
        s = n % 2
        dst = blk.at[s, p, pl.ds(pl.multiple_of((1 - k) * HALF, HALF), HALF), pl.ds(low(q), lanes - low(q))]
        pltpu.make_async_copy(dst, dst, blk_r.at[s, p]).wait()

    def mat_copies(n):
        w, j, _, _, s = block_of(n)
        src = mg.at[w, (j // s_b) % RING, (j // s_a) % RING]
        dst = mbuf.at[s, _at(k, size // 2)]
        here = pltpu.make_async_copy(src, dst, mat_loc.at[s])
        there = pltpu.make_async_remote_copy(
            src, dst, mat_s.at[s], mat_r.at[s], device_id=mate, device_id_type=MESH
        )
        return here, there

    def per_piece(n, act):
        _, _, q_now, _, _ = block_of(n)
        for q in range(slots):

            @pl.when(q_now == q)
            def _(q=q):
                def one(p, carry):
                    act(q, p)
                    return carry

                lax.fori_loop(0, rows, one, 0)

    def prefetch(n, first):
        if not first:
            pl.semaphore_wait(free.at[n % 2], 1)

        def go(q, p):
            here, there = blk_copies(n, q, p)
            here.start()
            there.start()

        per_piece(n, go)
        for c in mat_copies(n):
            c.start()

    def wait_blk(n):
        def one(q, p):
            blk_copies(n, q, p)[0].wait()
            from_mate(n, q, p)

        per_piece(n, one)
        mat_copies(n)[0].wait()
        there = mbuf.at[n % 2, _at(1 - k, size // 2)]
        pltpu.make_async_copy(there, there, mat_r.at[n % 2]).wait()

    def release(n):
        per_piece(n, lambda q, p: blk_copies(n, q, p)[1].wait_send())
        mat_copies(n)[1].wait_send()

        @pl.when(n + 2 < 2 * nb)
        def _():
            pl.semaphore_signal(free.at[n % 2], inc=1, device_id=mate, device_id_type=MESH)
            prefetch(n + 2, False)

    def cut(s, i):
        return blk[s, :, :, _at(i, STEP)].reshape(size, STEP)

    def peer(d):
        return lax.rem(x + d, chips)

    def at_peer(d):
        return {"row": 2 * peer(d) + k, "col": col}

    def rs_copy(par, g, d):
        return pltpu.make_async_remote_copy(
            sbuf.at[par, g, _at(peer(d), sl)], rs.at[g, d - 1], rs_s.at[g, d - 1], rs_r.at[g, d - 1],
            device_id=at_peer(d), device_id_type=MESH,
        )

    def send_partial(par, g):
        for d in range(1, chips):
            rs_copy(par, g, d).start()

    def gather_sum(par, g):
        for d in range(1, chips):
            rs_copy(par, g, d).wait_recv()
        total = sbuf[par, g, _at(x, sl)]
        for d in range(1, chips):
            total = total + rs[g, d - 1]
        for d in range(1, chips):
            rs_copy(par, g, d).wait_send()
        return total

    def cols_of(g):
        return pl.ds(g * gcol, gcol)

    def project(par, g, s, ref, first):
        sbuf[par, g] = jnp.zeros((gcol, size), jnp.float32)

        def one(i, carry):
            sbuf[par, g] += _dot_nt(ref[cols_of(g), _at(i, STEP)], cut(s, i))
            return carry

        lax.fori_loop(first, whole, one, 0)

    def ex_wait(g, d, ref):
        there = ref.at[g, _at(peer(chips - d), sl)]
        pltpu.make_async_copy(there, there, ex_r.at[g, d - 1]).wait()

    ys[...] = z_ref[...]
    out_ref[...] = jnp.zeros_like(out_ref)
    lead = 6

    def start(t, carry):
        tick(t)
        return carry

    lax.fori_loop(0, lead, start, 0)
    prefetch(0, True)
    prefetch(1, True)

    def w_copy(g, d):
        mine = wb.at[g, _at(x, sl)]
        return pltpu.make_async_remote_copy(
            mine, mine, ex_s.at[g, d - 1], ex_r.at[g, d - 1], device_id=at_peer(d), device_id_type=MESH
        )

    wait_blk(0)
    for g in range(2):
        project(0, g, 0, ys, top // 2)
        send_partial(0, g)

    def reflect(n, carry):
        j, s = top - n, n % 2
        for g in range(2):
            wb[g, _at(x, sl)] = _dot_nn(gather_sum(0, g), mbuf[s])
            for d in range(1, chips):
                w_copy(g, d).start()

        tick(n + lead)

        @pl.when(j > 0)
        def _():
            wait_blk(n + 1)

        for g in range(2):
            for d in range(1, chips):
                ex_wait(g, d, wb)

            def apply(i, carry, g=g):
                at = cols_of(g), _at(i, STEP)
                ys[at] = ys[at] - _dot_nn(wb[g], cut(s, i))
                return carry

            lax.fori_loop(j // 2, whole, apply, 0)
            for d in range(1, chips):
                w_copy(g, d).wait_send()

            @pl.when(j > 0)
            def _(g=g):
                project(0, g, 1 - s, ys, (j - 1) // 2)
                send_partial(0, g)

        release(n)
        return carry

    lax.fori_loop(0, nb, reflect, 0)
    lax.fori_loop(nb + lead, 2 * per + 5, start, 0)

    first_half = lax.broadcasted_iota(jnp.int32, (gcol, LANES), 1) < EDGE

    def take(ref, g, j):
        lo = ref[cols_of(g), pl.ds(pl.multiple_of((j // 2) * STEP, LANES), LANES)]
        hi = ref[cols_of(g), pl.ds(pl.multiple_of((j // 2) * STEP + LANES, LANES), LANES)]
        even = j % 2 == 0
        return jnp.where(
            first_half,
            jnp.where(even, lo, pltpu.roll(lo, EDGE, 1)),
            jnp.where(even, pltpu.roll(hi, EDGE, 1), hi),
        )

    def spread(val, j):
        even = j % 2 == 0
        other = pltpu.roll(val, EDGE, 1)
        zero = jnp.zeros_like(val)
        lo = jnp.where(even, jnp.where(first_half, val, zero), jnp.where(first_half, zero, other))
        hi = jnp.where(even, jnp.where(first_half, other, zero), jnp.where(first_half, zero, val))
        return jnp.concatenate([lo, hi], axis=1)

    def right_side(par, g, j):
        sbuf[par, g] = -sbuf[par, g]
        sbuf[par, g, :, _at(x, LANES)] += take(ys, g, j)

    def x_copy(g, d):
        return pltpu.make_async_remote_copy(
            wb.at[g, pl.ds(0, sl), _at(peer(d), LANES)], xr.at[g, _at(x, sl)], ex_s.at[g, d - 1], ex_r.at[g, d - 1],
            device_id=at_peer(d), device_id_type=MESH,
        )

    wait_blk(nb)
    for g in range(2):
        sbuf[0, g] = jnp.zeros((gcol, size), jnp.float32)
        right_side(0, g, top)
        send_partial(0, g)

    def solve(i, carry):
        n = nb + i
        j = top - i
        par, nxt = n % 2, (n + 1) % 2

        @pl.when(j > 0)
        def _():
            wait_blk(n + 1)

        for g in range(2):

            @pl.when(j > 0)
            def _(g=g):
                project(nxt, g, nxt, out_ref, (j + 1) // 2)

            wb[g, pl.ds(0, sl)] = _dot_nn(gather_sum(par, g), mbuf[par])
            for d in range(1, chips):
                x_copy(g, d).start()
            xr[g, _at(x, sl)] = wb[g, pl.ds(0, sl), _at(x, LANES)]

        for g in range(2):
            for d in range(1, chips):
                ex_wait(g, d, xr)
            solved = spread(xr[g], j)
            out_ref[cols_of(g), _at(j // 2, STEP)] += solved

            @pl.when(j > 0)
            def _(g=g, solved=solved):
                sbuf[nxt, g] += _dot_nt(solved, cut(nxt, j // 2))
                right_side(nxt, g, j - 1)
                send_partial(nxt, g)

            for d in range(1, chips):
                x_copy(g, d).wait_send()

        release(n)
        return carry

    lax.fori_loop(0, nb, solve, 0)


def _main(own, factors, state, rows, cols):
    _, slots, _, lanes = own.shape
    nb, ncol = lanes // LANES, state.shape[0]
    chips, size, gcol = rows // 2, rows * EDGE, ncol // 2
    sl = gcol // chips
    dma = pltpu.SemaphoreType.DMA
    hbm, vmem = pl.BlockSpec(memory_space=pl.ANY), pl.BlockSpec(memory_space=pltpu.VMEM)
    peers = max(chips - 1, 1)
    gathers = 2 * (slots + 1)
    outs = pl.pallas_call(
        functools.partial(_main_kernel, (rows, cols, slots, nb, ncol)),
        out_shape=[
            jax.ShapeDtypeStruct(state.shape, jnp.float32),
            jax.ShapeDtypeStruct((2, slots, RING, RING, HALF, lanes), jnp.float32),
            jax.ShapeDtypeStruct((2, RING, RING, size // 2, size), jnp.float32),
        ],
        in_specs=[vmem] * 3,
        out_specs=[vmem, hbm, hbm],
        scratch_shapes=[
            pltpu.VMEM((ncol, lanes), jnp.float32),
            pltpu.VMEM((2, rows, EDGE, lanes), jnp.float32),
            pltpu.VMEM((2, size, size), jnp.float32),
            pltpu.VMEM((2, 2, gcol, size), jnp.float32),
            pltpu.VMEM((2, peers, sl, size), jnp.float32),
            pltpu.VMEM((2, gcol, size), jnp.float32),
            pltpu.VMEM((2, gcol, LANES), jnp.float32),
            dma((gathers,)), dma((gathers, 8)), dma((gathers, 8)),
            dma((2, rows)), dma((2, rows)), dma((2, rows)), dma((2,)), dma((2,)), dma((2,)),
            pltpu.SemaphoreType.REGULAR((2,)),
            dma((2, peers)), dma((2, peers)), dma((2, peers)), dma((2, peers)),
        ],
        compiler_params=pltpu.CompilerParams(has_side_effects=True, vmem_limit_bytes=56 * 1024 * 1024),
        name="main",
    )(own, factors, state)
    return outs[0]


def _merge(diag, full):
    two, n, b, _ = diag.shape
    while n > 1:
        pairs = diag.reshape(two, n // 2, 2, b, b)
        d1, d2 = pairs[:, :, 0], pairs[:, :, 1]
        c21 = jnp.stack([full[:, (2 * i + 1) * b : (2 * i + 2) * b, 2 * i * b : (2 * i + 1) * b] for i in range(n // 2)], axis=1)
        mid = jnp.einsum("pnij,pnjk->pnik", d2, c21, precision=PREC_HIGH)
        off = -jnp.einsum("pnij,pnjk->pnik", mid, d1, precision=PREC_HIGH)
        zero = jnp.zeros_like(off)
        diag = jnp.concatenate([jnp.concatenate([d1, zero], axis=3), jnp.concatenate([off, d2], axis=3)], axis=2)
        n, b = n // 2, 2 * b
    return diag[:, 0]


def solution(mesh):
    rows, cols = mesh.shape["row"], mesh.shape["col"]
    mat_spec = P(("kpt", "row"), "col")
    fac_spec = P("kpt", None, None)
    swap = [(r, r + 1 - 2 * (r % 2)) for r in range(rows)]

    def local_work(v_loc, t_loc, z_loc, l_loc):
        size, chips = rows * EDGE, rows // 2
        row, col = lax.axis_index("row"), lax.axis_index("col")
        k = row % 2
        own, state, v_blk, l_diag = _prep(v_loc, l_loc, z_loc, rows, cols)

        vb = v_blk.reshape(size, -1)
        gram = lax.psum(_dot_nt(vb, vb), "row")
        l_blk = lax.dynamic_index_in_dim(l_diag.reshape(size, chips, 2, 2, EDGE), col % 2, 3, keepdims=False)
        l_blk = l_blk.reshape(size, size).T
        t_blk = lax.dynamic_slice_in_dim(t_loc, col * rows, rows, axis=0)
        l_pan = jnp.stack([l_blk[i * EDGE : (i + 1) * EDGE, i * EDGE : (i + 1) * EDGE] for i in range(rows)])
        eye = jnp.broadcast_to(jnp.eye(EDGE, dtype=jnp.float32), l_pan.shape)
        l_inv = lax.linalg.triangular_solve(l_pan, eye, left_side=True, lower=True)
        factors = _merge(jnp.stack([t_blk, l_inv]), jnp.stack([gram, l_blk]))
        mine = lax.dynamic_slice_in_dim(factors, k * (size // 2), size // 2, axis=1)

        x_state = _main(own, mine, state, rows, cols)

        ncol, lanes = x_state.shape
        xs = x_state.reshape(ncol, lanes // STEP, 2, LANES)
        keep = lax.dynamic_index_in_dim(xs, k, 2, keepdims=False).reshape(ncol, lanes // 2)
        send = lax.dynamic_index_in_dim(xs, 1 - k, 2, keepdims=False).reshape(ncol, lanes // 2)
        got = lax.ppermute(send, "row", swap)
        return jnp.concatenate([jnp.where(k == 0, keep, got), jnp.where(k == 0, got, keep)], axis=0).T

    return jax.shard_map(local_work, mesh=mesh, in_specs=(mat_spec, fac_spec, mat_spec, mat_spec), out_specs=mat_spec, check_vma=False)
```

time: 17700 us -> 893 us (0.05)
  waiting for transfers between devices: 15200 us -> 17.8 us
  matrix products: 1680 us -> 8.59 us
  Pallas kernels: 0 us -> 759 us
  other arithmetic: 749 us -> 45.1 us
    psum x256 -> x1, waiting for transfers between devices: 14300 us -> 16.5 us  [local_work(): gram = lax.psum(_dot_nt(vb, vb), 'row')]
    dot_general x512 -> x7, matrix products: 1430 us -> 8.01 us  [the longest x1 4.54 us: _dot_nt(): lax.dot_general(a, b, (((1,), (1,)), ((), ())), precision=PREC_HIGH, pref...]
    all_gather x16 -> x0, waiting for transfers between devices: 846 us -> none  [the longest x8 427 us: solve_group(): l_group = lax.all_gather(l_mine, 'col', axis=1, tiled=True)]
    pallas_call x0 -> x2, Pallas kernels: none -> 759 us  [the longest x1 646 us: _main(): pl.pallas_call(functools.partial(_main_kernel, (rows, cols, slots, nb, nc...]
    another operation x256 -> x5, other arithmetic: 749 us -> 41.8 us  [the longest x3 40.9 us: local_work(): l_inv = lax.linalg.triangular_solve(l_pan, eye, left_side=True, lower=True)]
    another operation x128 -> x1, matrix products: 243 us -> 0.59 us  [local_work(): l_inv = lax.linalg.triangular_solve(l_pan, eye, left_side=True, lower=True)]
  transfers between devices with their start and end apart: 272 -> 2, of which waited for: 272 -> 2; matrix products, arithmetic and copies ran while one was open for 4% -> 7% of each run, Pallas kernels for 0% -> 0%
where the time goes in v2:
time: 893 us; the launch traced here: 892 us
  Pallas kernels  759 us (85%)
  local copies, waits for them, and re-layouts  45.7 us (5%)
  other arithmetic  45.1 us (5%)
  waiting for transfers between devices  17.8 us (2%)
  between operations  13.7 us (2%)
    pallas_call x1, Pallas kernels, _main(): pl.pallas_call(functools.partial(_main_kernel, (rows, cols, slots, nb, nc...  646 us
    pallas_call x1, Pallas kernels, _prep(): pl.pallas_call(functools.partial(_prep_kernel, (rows, cols, slots, pairs)...  113 us
    another operation x3, other arithmetic, local_work(): l_inv = lax.linalg.triangular_solve(l_pan, eye, left_side=True, lower=True)  40.9 us
    unnamed x29, local copies, waits for them, and re-layouts  19.8 us
  transfers between devices with their start and end apart: 2, of which 2 were waited for; matrix products, arithmetic and copies ran while one was open for 7% of the time, Pallas kernels for 0%

profile of v2, /device:TPU:1, one launch (start us, length us, event | category | flops | bytes accessed | tf_op | source)
XLA Modules:
  0.0 892.4 jit_solution(16410552680487108648)
XLA Ops:
  6.5 1.7 copy-done.3
  8.3 1.6 copy-done.4
  9.9 1.6 copy-done.5
  11.5 112.6 %prep.1 = (f32[2,8,32,2048]{3,2,1,0:T(8,128)S(1)}, f32[256,2048]{1,0:T(8,128)S(1)}, f32[8,64,1024]{2,1,0:T(8,128)S(1)}, f32[8,64,1024]{2,1,0:T(8,128)S(1)}) custom-call(f32[1024,512]{1,0:T(8,128)S(1)} %copy-done.3, f32[1024,512]{1,0:T(8,128)S(1)} %copy-done.4, f32[1024,512]{1,0:T(8,128)S(1)} %copy-done.5), custom_call_target="tpu_custom_call" | custom-call | tf_op jit(solution)/shard_map/prep/pallas_call | solution.py:167
  124.0 2.0 copy-done.2
  126.0 1.3 copy-done.6
  127.4 1.3 copy-done.7
  128.7 4.5 convolution_bitcast_fusion
  133.3 5.9 reshape.185
  139.2 5.3 constant_dynamic-slice_fusion.2
  144.5 4.5 copy.31
  149.3 0.7 broadcast_select_fusion
  150.1 1.9 constant_dynamic-slice_fusion.3
  152.0 40.2 %custom-call.3 = f32[8,1,64,64]{2,3,1,0:T(8,128)S(1)} custom-call(f32[8,1,64,64]{3,2,1,0:T(8,128)} %broadcast_select_fusion), custom_call_target="InvertDiagBlocksLowerTriangular" | custom-call | tf_op jit(solution)/shard_map/triangular_solve | solution.py:630
  192.2 2.2 copy.30
  195.1 16.5 %all-reduce.5.cloned.1.call-done = f32[1,512,512]{2,1,0:T(8,128)} async-done(((f32[1,512,512]{2,1,0:T(8,128)}), f32[1,512,512]{2,1,0:T(8,128)}) %all-reduce.5.cloned.1.call-update) | async-done | bytes 1048592 | tf_op jit(solution)/shard_map/psum | solution.py:624
  211.6 0.8 maximum_bitcast_fusion.6
  213.4 0.7 fusion.35
  215.1 1.8 copy.34
  216.9 0.8 copy.35
  217.8 1.1 fusion.4
  218.9 1.0 fusion.5
  220.0 0.7 fusion
  220.9 1.3 copy.22
  222.2 646.4 %main.1 = (f32[256,2048]{1,0:T(8,128)}, f32[2,8,4,4,32,2048]{5,4,3,2,1,0:T(8,128)}, f32[2,4,4,256,512]{4,3,2,1,0:T(8,128)}) custom-call(f32[2,8,32,2048]{3,2,1,0:T(8,128)} %copy-done.2, f32[2,256,512]{2,1,0:T(8,128)} %bitcast.120, f32[256,2048]{1,0:T(8,128)} %copy-done.6), custom_call_target="tpu_custom_call" | custom-call | tf_op jit(solution)/shard_map/main/pallas_call | solution.py:569
  868.6 3.3 reshape.182
  871.9 2.8 constant_dynamic-slice_fusion.1
  874.7 3.6 copy.24
  878.2 2.6 collective-permute-start
  880.8 0.9 copy.23
  881.7 1.3 collective-permute-done
  883.3 1.6 maximum_bitcast_fusion
  (35 shorter events, 4.1 us)
Async XLA Ops:
  6.5 143.5 %copy-start = (f32[128,64,64]{0,2,1:T(8,128)S(1)}, f32[128,64,64]{0,2,1:T(8,128)}, u32[]{:S(2)}) copy-start(f32[128,64,64]{0,2,1:T(8,128)} %param.5) | copy-start | bytes 6291460
  6.5 205.1 %all-reduce.5.cloned.1.call-start = ((), (), s32[]{:S(2)}) async-start(), calls=%async_computation | async-start | bytes 2097152 | tf_op jit(solution)/shard_map/psum | solution.py:624
  6.5 1.7 copy-start.3
  8.3 1.6 copy-start.4
  9.9 1.6 copy-start.5
  124.0 2.0 copy-start.2
  126.0 1.3 copy-start.6
  127.4 1.3 copy-start.7
  212.4 1.7 copy-start.8
  878.2 4.8 collective-permute-start
  883.2 2.3 copy-start.1
Sparse Core Ops, SparseCore 0:
  133.4 78.1 all-reduce.4

commit v3 on v0

v3 whole, which is shorter than its diff:
```python
import functools

import jax
import jax.numpy as jnp
from jax import lax
from jax.experimental import pallas as pl
from jax.experimental.pallas import tpu as pltpu
from jax.sharding import PartitionSpec as P

PREC_HIGH = lax.Precision.HIGHEST
MESH = pl.DeviceIdType.MESH
EDGE = 64
HALF = EDGE // 2
LANES = 128
STEP = 256
RING = 4
LEAD = 11


def _dot_nt(a, b):
    return lax.dot_general(a, b, (((1,), (1,)), ((), ())), precision=PREC_HIGH, preferred_element_type=jnp.float32)


def _dot_nn(a, b):
    return lax.dot_general(a, b, (((1,), (0,)), ((), ())), precision=PREC_HIGH, preferred_element_type=jnp.float32)


def _at(i, n):
    return pl.ds(pl.multiple_of(i * n, n), n)


def _loop(lo, hi, body):
    def one(i, carry):
        body(i)
        return carry

    lax.fori_loop(lo, hi, one, 0)


def _gathers(slots):
    early = [(q, 0) for q in range(slots - 1, max(slots - 5, -1), -1)]
    late = [(q, 0) for q in range(slots - 5, -1, -1)]
    rest = [(slots - 1, 1), ("m", 1)] + [(q, 1) for q in range(slots - 2, -1, -1)]
    first = early + [None] * (6 - len(early)) + [("m", 0)] + late
    return first + [None] * (LEAD - len(first)) + rest


def _kernel(dims, v_in, t_in, z_in, l_in, out_ref, gath, mg, *scratch):
    (stage, vt, zt, tb, own, ys, xs, vb, ld, lx, gm, gx, r2, ga, xm, blk, mbuf, sbuf, rs, wb, xr, xf,
     in_sem, swap_l, swap_s, swap_r, v_s, v_r, l_s, l_r, lx_s, lx_r, gx_sem, r2_s, r2_r, ga_s, ga_r, fin_s, fin_r,
     ag_loc, ag_s, ag_r, blk_loc, blk_s, blk_r, mat_loc, mat_s, mat_r, free, rs_s, rs_r, ex_s, ex_r) = scratch
    rows, cols, slots, nb, ncol = dims
    row, col = lax.axis_index("row"), lax.axis_index("col")
    x, k = row // 2, row % 2
    chips, groups = rows // 2, cols // rows
    size, lanes = rows * EDGE, nb * LANES
    hsize = size // 2
    pairs = nb // 2
    gcol = ncol // 2
    sl = gcol // chips
    mate = {"row": row + 1 - 2 * k, "col": col}
    top, whole = nb - 1, nb // 2
    part, grp = col % rows, col // rows
    k_half, m_half = _at(k, HALF), _at(1 - k, HALF)
    s_a, s_b = 1 + (RING - 1) * k, RING - (RING - 1) * k
    a, b = (col // s_a) % RING, (col // s_b) % RING

    def remote(src, dst, ss, rr, to):
        return pltpu.make_async_remote_copy(src, dst, ss, rr, device_id=to, device_id_type=MESH)

    def await_(ref, sem):
        pltpu.make_async_copy(ref, ref, sem).wait()

    def peer(d):
        return lax.rem(x + d, chips)

    def at_peer(d):
        return {"row": 2 * peer(d) + k, "col": col}

    def plane(da, db):
        return {"row": row, "col": lax.rem(a + da, RING) * s_a + lax.rem(b + db, RING) * s_b}

    def low(q):
        return (groups * q // 2) * STEP

    order = _gathers(slots)

    class Slot:
        def __init__(self, kind, w, n):
            self.kind, self.w, self.n = kind, w, n

        def own(self):
            if self.kind == "m":
                return xm.at[self.w, _at(k, hsize)]
            return own.at[self.w, self.kind, :, pl.ds(low(self.kind), lanes - low(self.kind))]

        def piece(self, bb, aa, part=None):
            if self.kind == "m":
                return mg.at[self.w, bb, aa] if part is None else mg.at[self.w, bb, aa, pl.ds(part * (size // 4), size // 4)]
            at = pl.ds(low(self.kind), lanes - low(self.kind))
            e = slice(None) if part is None else pl.ds(part * (HALF // 2), HALF // 2)
            return gath.at[self.w, self.kind, bb, aa, e, at]

        def bundle(self, bb, part=None):
            e = slice(None) if part is None else pl.ds(part * (RING // 2), RING // 2)
            if self.kind == "m":
                return mg.at[self.w, bb, e]
            return gath.at[self.w, self.kind, bb, e, :, pl.ds(low(self.kind), lanes - low(self.kind))]

        def copy(self, i):
            d = 1 if i % 2 == 0 else RING - 1
            back = RING - d
            if i < 2:
                src, dst, to = self.own(), self.piece(b, a), plane(d, 0)
            elif i < 4:
                src = dst = self.piece(b, lax.rem(a + back, RING), i % 2)
                to = plane(d, 0)
            elif i < 6:
                src = dst = self.bundle(b)
                to = plane(0, d)
            else:
                src = dst = self.bundle(lax.rem(b + back, RING), i % 2)
                to = plane(0, d)
            return remote(src, dst, ag_s.at[self.n, i], ag_r.at[self.n, i], to)

        def arrived(self, i):
            back = RING - 1 if i % 2 == 0 else 1
            if i < 2:
                dst = self.piece(b, lax.rem(a + back, RING))
            elif i < 4:
                dst = self.piece(b, lax.rem(a + 2, RING), i % 2)
            elif i < 6:
                dst = self.bundle(lax.rem(b + back, RING))
            else:
                dst = self.bundle(lax.rem(b + 2, RING), i % 2)
            await_(dst, ag_r.at[self.n, i])

        def kept(self):
            return pltpu.make_async_copy(self.own(), self.piece(b, a), ag_loc.at[self.n])

        def stage(self, s):
            if s == 0:
                self.copy(0).start()
                self.copy(1).start()
                self.kept().start()
            elif s == 1:
                for i in range(2):
                    self.arrived(i)
                    self.copy(2 + i).start()
            elif s == 2:
                self.kept().wait()
                self.arrived(2)
                self.arrived(3)
                self.copy(4).start()
                self.copy(5).start()
            elif s == 3:
                for i in range(4, 6):
                    self.arrived(i)
                    self.copy(2 + i).start()
            elif s == 4:
                self.arrived(6)
                self.arrived(7)
            else:
                for i in range(8):
                    self.copy(i).wait_send()

    def tick(t):
        for s in (4, 3, 2, 1, 0, 5):
            n = t - s
            if isinstance(n, int):
                if 0 <= n < len(order) and order[n] is not None:
                    Slot(*order[n], n).stage(s)
                continue
            for kind in list(range(slots)) + ["m"]:
                at_v, at_l = order.index((kind, 0)), order.index((kind, 1))

                @pl.when(jnp.logical_or(n == at_v, n == at_l))
                def _(s=s, n=n, kind=kind, at_l=at_l):
                    Slot(kind, jnp.where(n == at_l, 1, 0), n).stage(s)

    def block_of(n):
        j = top - n % nb
        return n // nb, j, j // groups, j % groups, n % 2

    def blk_copies(n, q, p):
        w, _, _, h, s = block_of(n)
        c = h * rows + p
        at = pl.ds(low(q), lanes - low(q))
        src = gath.at[w, q, (c // s_b) % RING, (c // s_a) % RING, :, at]
        dst = blk.at[s, p, k_half, at]
        return pltpu.make_async_copy(src, dst, blk_loc.at[s, p]), remote(src, dst, blk_s.at[s, p], blk_r.at[s, p], mate)

    def from_mate(n, q, p):
        await_(blk.at[n % 2, p, m_half, pl.ds(low(q), lanes - low(q))], blk_r.at[n % 2, p])

    def mat_copies(n):
        w, j, _, _, s = block_of(n)
        src = mg.at[w, (j // s_b) % RING, (j // s_a) % RING]
        dst = mbuf.at[s, _at(k, hsize)]
        return pltpu.make_async_copy(src, dst, mat_loc.at[s]), remote(src, dst, mat_s.at[s], mat_r.at[s], mate)

    def per_piece(n, act):
        q_now = block_of(n)[2]
        for q in range(slots):

            @pl.when(q_now == q)
            def _(q=q):
                _loop(0, rows, functools.partial(act, q))

    def fetch_blk(n):
        def go(q, p):
            for c in blk_copies(n, q, p):
                c.start()

        per_piece(n, go)

    def fetch_mat(n):
        for c in mat_copies(n):
            c.start()

    def wait_blk(n):
        def one(q, p):
            blk_copies(n, q, p)[0].wait()
            from_mate(n, q, p)

        per_piece(n, one)

    def wait_mat(n):
        mat_copies(n)[0].wait()
        await_(mbuf.at[n % 2, _at(1 - k, hsize)], mat_r.at[n % 2])

    def release(n):
        per_piece(n, lambda q, p: blk_copies(n, q, p)[1].wait_send())
        mat_copies(n)[1].wait_send()

        @pl.when(n + 2 < 2 * nb)
        def _():
            pl.semaphore_signal(free.at[n % 2], inc=1, device_id=mate, device_id_type=MESH)
            pl.semaphore_wait(free.at[n % 2], 1)
            fetch_blk(n + 2)
            fetch_mat(n + 2)

    ins = [
        pltpu.make_async_copy(src, stage.at[i], in_sem.at[i]) for i, src in enumerate((v_in, l_in, z_in))
    ] + [pltpu.make_async_copy(t_in.at[_at(col, rows)], tb, in_sem.at[3])]
    for c in ins:
        c.start()

    def swaps(m, i):
        there = _at(2 * i + k, LANES)
        if m < 2:
            mine, theirs = vt.at[m, :, k, :, _at(i, LANES)], vt.at[m, :, 1 - k, :, _at(i, LANES)]
            dst = own.at[m, :, :, there]
        else:
            mine, theirs = zt.at[k, :, _at(i, LANES)], zt.at[1 - k, :, _at(i, LANES)]
            dst = ys.at[:, there]
        return (
            pltpu.make_async_copy(mine, dst, swap_l.at[m, i]),
            remote(theirs, dst, swap_s.at[m, i], swap_r.at[m, i], mate),
        )

    def arriving(m, i):
        there = _at(2 * i + 1 - k, LANES)
        await_(own.at[m, :, :, there] if m < 2 else ys.at[:, there], swap_r.at[m, i])

    def turn(m):
        ins[m].wait()

        def one(i):
            block = stage[m, _at(i, LANES), :].T
            if m < 2:
                vt[m, :, :, :, _at(i, LANES)] = block.reshape(slots, 2, HALF, LANES)
            else:
                zt[:, :, _at(i, LANES)] = block.reshape(2, ncol, LANES)
            for c in swaps(m, i):
                c.start()

        _loop(0, pairs, one)

    def swapped(m):
        def one(i):
            swaps(m, i)[0].wait()
            arriving(m, i)

        _loop(0, pairs, one)

    width = lanes // 2

    def deal_v(q, kk, act):
        to = groups * q + grp
        src = own.at[0, q, :, pl.ds(kk * width, width)]
        dst = vb.at[part, k_half]
        self_ = jnp.logical_and(to == col, k == kk)
        act(
            self_,
            pltpu.make_async_copy(src, dst, v_r.at[part, k]),
            remote(src, dst, v_s.at[q, kk], v_r.at[part, k], {"col": to, "row": 2 * x + kk}),
        )

    def deal_l(q, kk, act):
        to = groups * q + grp
        src = own.at[1, q, :, _at(to // 2, STEP)]
        dst = ld.at[part, k_half]
        self_ = jnp.logical_and(to == col, k == kk)
        act(
            self_,
            pltpu.make_async_copy(src, dst, l_r.at[part, k]),
            remote(src, dst, l_s.at[q, kk], l_r.at[part, k], {"col": to, "row": 2 * x + kk}),
        )

    def send(self_, here, there):
        pl.when(self_)(here.start)
        pl.when(jnp.logical_not(self_))(there.start)

    def sent(self_, here, there):
        pl.when(jnp.logical_not(self_))(there.wait_send)

    def over_v(act):
        def one(q):
            pl.when(groups * q + grp < nb // 2)(lambda: deal_v(q, 0, act))
            deal_v(q, 1, act)

        _loop(0, slots, one)

    def over_l(act):
        def one(q):
            deal_l(q, 0, act)
            deal_l(q, 1, act)

        _loop(0, slots, one)

    has_v = jnp.logical_or(k == 1, col < nb // 2)

    turn(0)
    swapped(0)
    over_v(send)
    tick(0)
    turn(1)
    tick(1)
    swapped(1)
    over_l(send)
    turn(2)
    tick(2)

    gm[...] = jnp.zeros_like(gm)

    @pl.when(has_v)
    def _():
        def got(n):
            await_(vb.at[n // 2, _at(n % 2, HALF)], v_r.at[n // 2, n % 2])

        _loop(0, 2 * rows, got)

        def chunk(i):
            all_ = vb[:, :, _at(i, STEP)].reshape(size, STEP)
            gm[pl.ds(0, hsize), pl.ds(0, hsize)] += _dot_nt(all_[:hsize], all_[:hsize])
            gm[pl.ds(hsize, hsize), :] += _dot_nt(all_[hsize:], all_)

        _loop(0, width // STEP, chunk)

    mine, theirs = _at(k, hsize), _at(1 - k, hsize)
    to_mate = remote(gm.at[theirs], gx, gx_sem.at[0], gx_sem.at[1], mate)
    to_mate.start()
    tick(3)
    to_mate.wait_recv()
    gm[mine] += gx[...]
    rl = hsize // chips

    def r2_copy(d):
        src = gm.at[pl.ds(pl.multiple_of(k * hsize + peer(d) * rl, rl), rl)]
        return remote(src, r2.at[d - 1], r2_s.at[d - 1], r2_r.at[d - 1], at_peer(d))

    for d in range(1, chips):
        r2_copy(d).start()

    def got_l(n):
        await_(ld.at[n // 2, _at(n % 2, HALF)], l_r.at[n // 2, n % 2])

    _loop(0, 2 * rows, got_l)
    ev = col % 2 == 0
    lo_half = lax.broadcasted_iota(jnp.int32, (size, LANES), 1) < EDGE
    l_lo, l_hi = ld[:, :, pl.ds(0, LANES)].reshape(size, LANES), ld[:, :, pl.ds(LANES, LANES)].reshape(size, LANES)
    lx[x] = jnp.where(
        lo_half,
        jnp.where(ev, l_lo, pltpu.roll(l_lo, EDGE, 1)),
        jnp.where(ev, pltpu.roll(l_hi, EDGE, 1), l_hi),
    )

    def lx_copy(d):
        return remote(lx.at[x], lx.at[x], lx_s.at[d - 1], lx_r.at[d - 1], at_peer(d))

    tick(4)
    for d in range(1, chips):
        r2_copy(d).wait_recv()
    my_rows = pl.ds(pl.multiple_of(k * hsize + x * rl, rl), rl)
    total = gm[my_rows]
    for d in range(1, chips):
        total = total + r2[d - 1]
    ga[my_rows] = total

    def ga_copy(d):
        return remote(ga.at[my_rows], ga.at[my_rows], ga_s.at[d - 1], ga_r.at[d - 1], at_peer(d))

    for d in range(1, chips):
        ga_copy(d).start()
    for d in range(1, chips):
        lx_copy(d).start()
    tick(5)
    for d in range(1, chips):
        await_(ga.at[pl.ds(pl.multiple_of(k * hsize + peer(chips - d) * rl, rl), rl)], ga_r.at[d - 1])
    half_to_mate = remote(ga.at[mine], ga.at[mine], gx_sem.at[2], gx_sem.at[3], mate)
    half_to_mate.start()

    n128 = size // LANES
    r_i = lax.broadcasted_iota(jnp.int32, (LANES, LANES), 0)
    c_i = lax.broadcasted_iota(jnp.int32, (LANES, LANES), 1)

    def tile(i):
        return _at(i, LANES), _at(i, LANES)

    def level_small(w, c_ref, lev):
        pick = jnp.logical_and(
            lax.shift_right_logical(r_i, lev) % 2 == 1,
            lax.shift_right_logical(c_i, lev) + 1 == lax.shift_right_logical(r_i, lev),
        )

        def one(i):
            at = tile(i)
            cur = xm[(w, *at)]
            low_part = jnp.where(pick, c_ref[at], 0.0)
            xm[(w, *at)] = cur - _dot_nn(_dot_nn(cur, low_part), cur)

        _loop(0, n128, one)

    def level_big(w, c_ref):
        width_ = LANES
        while width_ < size:
            for i in range(size // (2 * width_)):
                d1 = pl.ds(2 * i * width_, width_)
                d2 = pl.ds((2 * i + 1) * width_, width_)
                xm[w, d2, d1] = -_dot_nn(_dot_nn(xm[w, d2, d2], c_ref[d2, d1]), xm[w, d1, d1])
            width_ *= 2

    xm[...] = jnp.zeros_like(xm)
    ins[3].wait()
    for p in range(0, rows, 2):
        zero = jnp.zeros((EDGE, EDGE), jnp.float32)
        both = jnp.concatenate(
            [jnp.concatenate([tb[p], zero], axis=1), jnp.concatenate([zero, tb[p + 1]], axis=1)], axis=0
        )
        xm[0, pl.ds(p * EDGE, LANES), pl.ds(p * EDGE, LANES)] = both
    await_(ga.at[theirs], gx_sem.at[3])
    level_small(0, ga, 6)
    level_big(0, ga)
    tick(6)

    fetch_blk(0)
    fetch_blk(1)
    for d in range(1, chips):
        await_(lx.at[peer(chips - d)], lx_r.at[d - 1])
    to_mate.wait_send()
    for d in range(1, chips):
        r2_copy(d).wait_send()
    for i in range(chips):
        gm[_at(i, LANES), :] = lx[i].T
    same = r_i == c_i

    def diag(i):
        d = gm[tile(i)]
        xm[(1, *tile(i))] = jnp.where(same, 1.0 / jnp.where(same, d, 1.0), 0.0)

    _loop(0, n128, diag)
    swapped(2)
    tick(7)
    _loop(0, 3, lambda i: level_small(1, gm, i))
    tick(8)
    _loop(3, 7, lambda i: level_small(1, gm, i))
    tick(9)
    level_big(1, gm)
    tick(10)
    fetch_mat(0)
    fetch_mat(1)

    def cut(s, i):
        return blk[s, :, :, _at(i, STEP)].reshape(size, STEP)

    def rs_copy(par, g, d):
        return remote(sbuf.at[par, g, _at(peer(d), sl)], rs.at[g, d - 1], rs_s.at[g, d - 1], rs_r.at[g, d - 1], at_peer(d))

    def send_partial(par, g):
        for d in range(1, chips):
            rs_copy(par, g, d).start()

    def gather_sum(par, g):
        for d in range(1, chips):
            rs_copy(par, g, d).wait_recv()
        total = sbuf[par, g, _at(x, sl)]
        for d in range(1, chips):
            total = total + rs[g, d - 1]
        for d in range(1, chips):
            rs_copy(par, g, d).wait_send()
        return total

    def cols_of(g):
        return pl.ds(g * gcol, gcol)

    def project(par, g, s, ref, first):
        sbuf[par, g] = jnp.zeros((gcol, size), jnp.float32)

        def one(i):
            sbuf[par, g] += _dot_nt(ref[cols_of(g), _at(i, STEP)], cut(s, i))

        _loop(first, whole, one)

    def ex_wait(g, d, ref):
        await_(ref.at[g, _at(peer(chips - d), sl)], ex_r.at[g, d - 1])

    def w_copy(g, d):
        mine = wb.at[g, _at(x, sl)]
        return remote(mine, mine, ex_s.at[g, d - 1], ex_r.at[g, d - 1], at_peer(d))

    wait_blk(0)
    for g in range(2):
        project(0, g, 0, ys, top // 2)
        send_partial(0, g)
    wait_mat(0)

    def reflect(n):
        j, s = top - n, n % 2
        for g in range(2):
            wb[g, _at(x, sl)] = _dot_nn(gather_sum(0, g), mbuf[s])
            for d in range(1, chips):
                w_copy(g, d).start()

        @pl.when(s == 0)
        def _():
            tick(LEAD + n // 2)

        @pl.when(j > 0)
        def _():
            wait_blk(n + 1)
            wait_mat(n + 1)

        for g in range(2):
            for d in range(1, chips):
                ex_wait(g, d, wb)

            def apply(i, g=g):
                at = cols_of(g), _at(i, STEP)
                ys[at] = ys[at] - _dot_nn(wb[g], cut(s, i))

            _loop(j // 2, whole, apply)
            for d in range(1, chips):
                w_copy(g, d).wait_send()

            @pl.when(j > 0)
            def _(g=g):
                project(0, g, 1 - s, ys, (j - 1) // 2)
                send_partial(0, g)

        release(n)

    _loop(0, nb, reflect)

    xs[...] = jnp.zeros_like(xs)
    first_half = lax.broadcasted_iota(jnp.int32, (gcol, LANES), 1) < EDGE

    def take(ref, g, j):
        lo = ref[cols_of(g), pl.ds(pl.multiple_of((j // 2) * STEP, LANES), LANES)]
        hi = ref[cols_of(g), pl.ds(pl.multiple_of((j // 2) * STEP + LANES, LANES), LANES)]
        even = j % 2 == 0
        return jnp.where(
            first_half,
            jnp.where(even, lo, pltpu.roll(lo, EDGE, 1)),
            jnp.where(even, pltpu.roll(hi, EDGE, 1), hi),
        )

    def spread(val, j):
        even = j % 2 == 0
        other = pltpu.roll(val, EDGE, 1)
        zero = jnp.zeros_like(val)
        lo = jnp.where(even, jnp.where(first_half, val, zero), jnp.where(first_half, zero, other))
        hi = jnp.where(even, jnp.where(first_half, other, zero), jnp.where(first_half, zero, val))
        return jnp.concatenate([lo, hi], axis=1)

    def right_side(par, g, j):
        sbuf[par, g] = -sbuf[par, g]
        sbuf[par, g, :, _at(x, LANES)] += take(ys, g, j)

    def x_copy(g, d):
        src = wb.at[g, pl.ds(0, sl), _at(peer(d), LANES)]
        return remote(src, xr.at[g, _at(x, sl)], ex_s.at[g, d - 1], ex_r.at[g, d - 1], at_peer(d))

    wait_blk(nb)
    wait_mat(nb)
    for g in range(2):
        sbuf[0, g] = jnp.zeros((gcol, size), jnp.float32)
        right_side(0, g, top)
        send_partial(0, g)

    def solve(i):
        n = nb + i
        j = top - i
        par, nxt = n % 2, (n + 1) % 2

        @pl.when(j > 0)
        def _():
            wait_blk(n + 1)
            wait_mat(n + 1)

        for g in range(2):

            @pl.when(j > 0)
            def _(g=g):
                project(nxt, g, nxt, xs, (j + 1) // 2)

            wb[g, pl.ds(0, sl)] = _dot_nn(gather_sum(par, g), mbuf[par])
            for d in range(1, chips):
                x_copy(g, d).start()
            xr[g, _at(x, sl)] = wb[g, pl.ds(0, sl), _at(x, LANES)]

        @pl.when(par == 0)
        def _():
            tick(LEAD + n // 2)

        for g in range(2):
            for d in range(1, chips):
                ex_wait(g, d, xr)
            solved = spread(xr[g], j)
            xs[cols_of(g), _at(j // 2, STEP)] += solved

            @pl.when(j > 0)
            def _(g=g, solved=solved):
                sbuf[nxt, g] += _dot_nt(solved, cut(nxt, j // 2))
                right_side(nxt, g, j - 1)
                send_partial(nxt, g)

            for d in range(1, chips):
                x_copy(g, d).wait_send()

        release(n)

    _loop(0, nb, solve)

    def fin_copy(i):
        return remote(
            xs.at[:, _at(2 * i + 1 - k, LANES)], xf.at[_at(k, ncol), _at(i, LANES)], fin_s.at[i], fin_r.at[i], mate
        )

    _loop(0, pairs, lambda i: fin_copy(i).start())

    def own_cols(i):
        xf[_at(k, ncol), _at(i, LANES)] = xs[:, _at(2 * i + k, LANES)]

    _loop(0, pairs, own_cols)

    def give(i):
        await_(xf.at[_at(1 - k, ncol), _at(i, LANES)], fin_r.at[i])
        out_ref[_at(i, LANES), :] = xf[:, _at(i, LANES)].T

    _loop(0, pairs, give)

    _loop(0, pairs, lambda i: fin_copy(i).wait_send())
    for m in range(3):
        _loop(0, pairs, lambda i, m=m: swaps(m, i)[1].wait_send())
    over_v(sent)
    over_l(sent)
    half_to_mate.wait_send()
    for d in range(1, chips):
        ga_copy(d).wait_send()
        lx_copy(d).wait_send()


def solution(mesh):
    rows, cols = mesh.shape["row"], mesh.shape["col"]
    mat_spec = P(("kpt", "row"), "col")
    fac_spec = P("kpt", None, None)

    def local_work(v_loc, t_loc, z_loc, l_loc):
        n_row, n_col = v_loc.shape
        slots, lanes, chips, size = n_col // EDGE, 2 * n_row, rows // 2, rows * EDGE
        nb, ncol = lanes // LANES, z_loc.shape[1] // 2
        pairs, gcol, peers = nb // 2, ncol // 2, max(chips - 1, 1)
        sl, gathers = gcol // chips, len(_gathers(slots))
        dma = pltpu.SemaphoreType.DMA
        hbm, vmem = pl.BlockSpec(memory_space=pl.ANY), pl.BlockSpec(memory_space=pltpu.VMEM)

        def buf(*shape):
            return pltpu.VMEM(shape, jnp.float32)

        return pl.pallas_call(
            functools.partial(_kernel, (rows, cols, slots, nb, ncol)),
            out_shape=[
                jax.ShapeDtypeStruct(z_loc.shape, jnp.float32),
                jax.ShapeDtypeStruct((2, slots, RING, RING, HALF, lanes), jnp.float32),
                jax.ShapeDtypeStruct((2, RING, RING, size // 2, size), jnp.float32),
            ],
            in_specs=[hbm] * 4,
            out_specs=[vmem, hbm, hbm],
            scratch_shapes=[
                buf(3, n_row, n_col),
                buf(2, slots, 2, HALF, n_row),
                buf(2, ncol, n_row),
                buf(rows, EDGE, EDGE),
                buf(2, slots, HALF, lanes),
                buf(ncol, lanes),
                buf(ncol, lanes),
                buf(rows, EDGE, lanes // 2),
                buf(rows, EDGE, STEP),
                buf(chips, size, LANES),
                buf(size, size),
                buf(size // 2, size),
                buf(peers, size // 2 // chips, size),
                buf(size, size),
                buf(2, size, size),
                buf(2, rows, EDGE, lanes),
                buf(2, size, size),
                buf(2, 2, gcol, size),
                buf(2, peers, sl, size),
                buf(2, gcol, size),
                buf(2, gcol, LANES),
                buf(2 * ncol, n_row),
                dma((4,)),
                dma((3, pairs)), dma((3, pairs)), dma((3, pairs)),
                dma((slots, 2)), dma((rows, 2)),
                dma((slots, 2)), dma((rows, 2)),
                dma((peers,)), dma((peers,)),
                dma((4,)),
                dma((peers,)), dma((peers,)), dma((peers,)), dma((peers,)),
                dma((pairs,)), dma((pairs,)),
                dma((gathers,)), dma((gathers, 8)), dma((gathers, 8)),
                dma((2, rows)), dma((2, rows)), dma((2, rows)),
                dma((2,)), dma((2,)), dma((2,)),
                pltpu.SemaphoreType.REGULAR((2,)),
                dma((2, peers)), dma((2, peers)), dma((2, peers)), dma((2, peers)),
            ],
            compiler_params=pltpu.CompilerParams(has_side_effects=True, vmem_limit_bytes=60 * 1024 * 1024),
            name="eigvec",
        )(v_loc, t_loc, z_loc, l_loc)[0]

    return jax.shard_map(local_work, mesh=mesh, in_specs=(mat_spec, fac_spec, mat_spec, mat_spec), out_specs=mat_spec, check_vma=False)
```

time: 17700 us -> 760 us (0.04)
  waiting for transfers between devices: 15200 us -> 0 us
  matrix products: 1680 us -> 0 us
  Pallas kernels: 0 us -> 751 us
  other arithmetic: 749 us -> 0 us
    psum x256 -> x0, waiting for transfers between devices: 14300 us -> none  [the longest x128 7530 us: house_one(): s_sum = lax.psum(s_part, 'row')]
    dot_general x512 -> x0, matrix products: 1430 us -> none  [the longest x128 489 us: solve_one(): lax.dot_general(l_cur, x_acc, CONTRACT_ROWS, precision=PREC_HIGH, preferr...]
    all_gather x16 -> x0, waiting for transfers between devices: 846 us -> none  [the longest x8 427 us: solve_group(): l_group = lax.all_gather(l_mine, 'col', axis=1, tiled=True)]
    pallas_call x0 -> x1, Pallas kernels: none -> 751 us  [local_work(): pl.pallas_call(functools.partial(_kernel, (rows, cols, slots, nb, ncol)),...]
    another operation x256 -> x0, other arithmetic: 749 us -> none  [solve_one(): lax.linalg.triangular_solve(l_diag, y_blk - s_sum, left_side=True, lower=...]
    another operation x128 -> x0, matrix products: 243 us -> none  [solve_one(): lax.linalg.triangular_solve(l_diag, y_blk - s_sum, left_side=True, lower=...]
  transfers between devices with their start and end apart: 272 -> 0, of which waited for: 272 -> 0; matrix products, arithmetic and copies ran while one was open for 4% -> 0% of each run, Pallas kernels for 0% -> 0%
where the time goes in v3:
time: 760 us; the launch traced here: 759 us
  Pallas kernels  751 us (99%)
  local copies, waits for them, and re-layouts  8.67 us (1%)
    pallas_call x1, Pallas kernels, local_work(): pl.pallas_call(functools.partial(_kernel, (rows, cols, slots, nb, ncol)),...  751 us

profile of v3, /device:TPU:1, one launch (start us, length us, event | category | flops | bytes accessed | tf_op | source)
XLA Modules:
  0.0 759.2 jit_solution(6555821342158512698)
XLA Ops:
  0.0 5.6 copy.5.t_in
  5.6 750.6 %eigvec.1 = (f32[1024,512]{1,0:T(8,128)}, f32[2,8,4,4,32,2048]{5,4,3,2,1,0:T(8,128)}, f32[2,4,4,256,512]{4,3,2,1,0:T(8,128)}) custom-call(f32[1024,512]{1,0:T(8,128)} %v_in.1, f32[128,64,64]{2,1,0:T(8,128)} %copy.5.t_in, f32[1024,512]{1,0:T(8,128)} %z_in.1, f32[1024,512]{1,0:T(8,128)} %l_in.1), custom_call_target="tpu_custom_call" | custom-call | tf_op jit(solution)/shard_map/eigvec/pallas_call | solution.py:691
  756.2 3.1 copy.7

commit v4 on v3

--- a/solution.py
+++ b/solution.py
@@ -14,7 +14,7 @@
 LANES = 128
 STEP = 256
 RING = 4
-LEAD = 11
+LEAD = 9
 
 
 def _dot_nt(a, b):
@@ -38,15 +38,14 @@
 
 
 def _gathers(slots):
-    early = [(q, 0) for q in range(slots - 1, max(slots - 5, -1), -1)]
-    late = [(q, 0) for q in range(slots - 5, -1, -1)]
+    early = [(slots - 1, 0), (slots - 2, 0), None, None, ("m", 0)]
+    first = early + [(q, 0) for q in range(slots - 3, -1, -1)]
     rest = [(slots - 1, 1), ("m", 1)] + [(q, 1) for q in range(slots - 2, -1, -1)]
-    first = early + [None] * (6 - len(early)) + [("m", 0)] + late
     return first + [None] * (LEAD - len(first)) + rest
 
 
-def _kernel(dims, v_in, t_in, z_in, l_in, out_ref, gath, mg, *scratch):
-    (stage, vt, zt, tb, own, ys, xs, vb, ld, lx, gm, gx, r2, ga, xm, blk, mbuf, sbuf, rs, wb, xr, xf,
+def _kernel(dims, v_in, t_in, z_in, l_in, out_ref, gath, *scratch):
+    (stage, vt, zt, tb, own, ys, xs, vb, ld, lx, gm, pk, gx, r2, ga, xm, pm, mg, blk, mbuf, sbuf, rs, wb, xr,
      in_sem, swap_l, swap_s, swap_r, v_s, v_r, l_s, l_r, lx_s, lx_r, gx_sem, r2_s, r2_r, ga_s, ga_r, fin_s, fin_r,
      ag_loc, ag_s, ag_r, blk_loc, blk_s, blk_r, mat_loc, mat_s, mat_r, free, rs_s, rs_r, ex_s, ex_r) = scratch
     rows, cols, slots, nb, ncol = dims
@@ -54,7 +53,7 @@
     x, k = row // 2, row % 2
     chips, groups = rows // 2, cols // rows
     size, lanes = rows * EDGE, nb * LANES
-    hsize = size // 2
+    hsize, qsize, n128 = size // 2, size // 4, size // LANES
     pairs = nb // 2
     gcol = ncol // 2
     sl = gcol // chips
@@ -91,12 +90,12 @@
 
         def own(self):
             if self.kind == "m":
-                return xm.at[self.w, _at(k, hsize)]
+                return pm.at[self.w]
             return own.at[self.w, self.kind, :, pl.ds(low(self.kind), lanes - low(self.kind))]
 
         def piece(self, bb, aa, part=None):
             if self.kind == "m":
-                return mg.at[self.w, bb, aa] if part is None else mg.at[self.w, bb, aa, pl.ds(part * (size // 4), size // 4)]
+                return mg.at[self.w, bb, aa] if part is None else mg.at[self.w, bb, aa, pl.ds(part * HALF, HALF)]
             at = pl.ds(low(self.kind), lanes - low(self.kind))
             e = slice(None) if part is None else pl.ds(part * (HALF // 2), HALF // 2)
             return gath.at[self.w, self.kind, bb, aa, e, at]
@@ -193,11 +192,15 @@
     def from_mate(n, q, p):
         await_(blk.at[n % 2, p, m_half, pl.ds(low(q), lanes - low(q))], blk_r.at[n % 2, p])
 
-    def mat_copies(n):
-        w, j, _, _, s = block_of(n)
-        src = mg.at[w, (j // s_b) % RING, (j // s_a) % RING]
-        dst = mbuf.at[s, _at(k, hsize)]
-        return pltpu.make_async_copy(src, dst, mat_loc.at[s]), remote(src, dst, mat_s.at[s], mat_r.at[s], mate)
+    def mat_copies(n, i):
+        w, j, q, h, s = block_of(n)
+        c = h * rows + q
+        src = mg.at[w, (c // s_b) % RING, (c // s_a) % RING, :, pl.ds(LANES * (i * (i + 1) // 2), LANES * (i + 1))]
+        dst = mbuf.at[s, pl.ds(pl.multiple_of(i * LANES + k * EDGE, EDGE), EDGE), pl.ds(0, LANES * (i + 1))]
+        return (
+            pltpu.make_async_copy(src, dst, mat_loc.at[s, i]),
+            remote(src, dst, mat_s.at[s, i], mat_r.at[s, i], mate),
+        )
 
     def per_piece(n, act):
         q_now = block_of(n)[2]
@@ -215,8 +218,9 @@
         per_piece(n, go)
 
     def fetch_mat(n):
-        for c in mat_copies(n):
-            c.start()
+        for i in range(n128):
+            for c in mat_copies(n, i):
+                c.start()
 
     def wait_blk(n):
         def one(q, p):
@@ -226,12 +230,15 @@
         per_piece(n, one)
 
     def wait_mat(n):
-        mat_copies(n)[0].wait()
-        await_(mbuf.at[n % 2, _at(1 - k, hsize)], mat_r.at[n % 2])
+        for i in range(n128):
+            mat_copies(n, i)[0].wait()
+            there = pl.ds(pl.multiple_of(i * LANES + (1 - k) * EDGE, EDGE), EDGE), pl.ds(0, LANES * (i + 1))
+            await_(mbuf.at[(n % 2, *there)], mat_r.at[n % 2, i])
 
     def release(n):
         per_piece(n, lambda q, p: blk_copies(n, q, p)[1].wait_send())
-        mat_copies(n)[1].wait_send()
+        for i in range(n128):
+            mat_copies(n, i)[1].wait_send()
 
         @pl.when(n + 2 < 2 * nb)
         def _():
@@ -242,7 +249,7 @@
 
     ins = [
         pltpu.make_async_copy(src, stage.at[i], in_sem.at[i]) for i, src in enumerate((v_in, l_in, z_in))
-    ] + [pltpu.make_async_copy(t_in.at[_at(col, rows)], tb, in_sem.at[3])]
+    ] + [pltpu.make_async_copy(t_in.at[_at(groups * part + grp, rows)], tb, in_sem.at[3])]
     for c in ins:
         c.start()
 
@@ -284,22 +291,24 @@
 
         _loop(0, pairs, one)
 
-    width = lanes // 2
-
-    def deal_v(q, kk, act):
-        to = groups * q + grp
-        src = own.at[0, q, :, pl.ds(kk * width, width)]
-        dst = vb.at[part, k_half]
+    my_q, my_h = part, grp
+    my_j = groups * my_q + my_h
+    first_t = my_j // 2
+
+    def deal_v(q, t, act):
+        to, kk = grp * rows + q, t % 2
+        src = own.at[0, q, :, _at(t, STEP)]
+        dst = vb.at[t // 2, part, k_half]
         self_ = jnp.logical_and(to == col, k == kk)
         act(
             self_,
-            pltpu.make_async_copy(src, dst, v_r.at[part, k]),
-            remote(src, dst, v_s.at[q, kk], v_r.at[part, k], {"col": to, "row": 2 * x + kk}),
+            pltpu.make_async_copy(src, dst, v_r.at[t // 2, part, k]),
+            remote(src, dst, v_s.at[q, t], v_r.at[t // 2, part, k], {"col": to, "row": 2 * x + kk}),
         )
 
     def deal_l(q, kk, act):
-        to = groups * q + grp
-        src = own.at[1, q, :, _at(to // 2, STEP)]
+        to = grp * rows + q
+        src = own.at[1, q, :, _at((groups * q + grp) // 2, STEP)]
         dst = ld.at[part, k_half]
         self_ = jnp.logical_and(to == col, k == kk)
         act(
@@ -317,8 +326,7 @@
 
     def over_v(act):
         def one(q):
-            pl.when(groups * q + grp < nb // 2)(lambda: deal_v(q, 0, act))
-            deal_v(q, 1, act)
+            _loop((groups * q + grp) // 2, pairs, lambda t: deal_v(q, t, act))
 
         _loop(0, slots, one)
 
@@ -329,45 +337,53 @@
 
         _loop(0, slots, one)
 
-    has_v = jnp.logical_or(k == 1, col < nb // 2)
-
     turn(0)
     swapped(0)
     over_v(send)
-    tick(0)
     turn(1)
-    tick(1)
     swapped(1)
     over_l(send)
     turn(2)
-    tick(2)
+    mbuf[...] = jnp.zeros_like(mbuf)
 
     gm[...] = jnp.zeros_like(gm)
 
-    @pl.when(has_v)
-    def _():
+    def chunk(i):
         def got(n):
-            await_(vb.at[n // 2, _at(n % 2, HALF)], v_r.at[n // 2, n % 2])
+            await_(vb.at[i, n // 2, _at(n % 2, HALF)], v_r.at[i, n // 2, n % 2])
 
         _loop(0, 2 * rows, got)
-
-        def chunk(i):
-            all_ = vb[:, :, _at(i, STEP)].reshape(size, STEP)
-            gm[pl.ds(0, hsize), pl.ds(0, hsize)] += _dot_nt(all_[:hsize], all_[:hsize])
-            gm[pl.ds(hsize, hsize), :] += _dot_nt(all_[hsize:], all_)
-
-        _loop(0, width // STEP, chunk)
-
-    mine, theirs = _at(k, hsize), _at(1 - k, hsize)
-    to_mate = remote(gm.at[theirs], gx, gx_sem.at[0], gx_sem.at[1], mate)
+        all_ = vb[i].reshape(size, STEP)
+        gm[pl.ds(0, hsize), pl.ds(0, hsize)] += _dot_nt(all_[:hsize], all_[:hsize])
+        gm[pl.ds(hsize, hsize), :] += _dot_nt(all_[hsize:], all_)
+
+    _loop((first_t + 1 - k) // 2, pairs // 2, chunk)
+    tick(0)
+
+    widths = []
+    w_ = hsize
+    while w_ >= EDGE:
+        widths.append(w_)
+        w_ //= 2
+
+    def packed(w_):
+        return pl.ds(size - 2 * w_, w_)
+
+    pk[...] = jnp.zeros_like(pk)
+    for w_ in widths:
+        for i in range(hsize // w_):
+            pk[pl.ds(i * w_, w_), packed(w_)] = gm[pl.ds((2 * i + 1) * w_, w_), pl.ds(2 * i * w_, w_)]
+
+    mine, theirs = _at(k, qsize), _at(1 - k, qsize)
+    to_mate = remote(pk.at[theirs], gx, gx_sem.at[0], gx_sem.at[1], mate)
     to_mate.start()
-    tick(3)
+    tick(1)
     to_mate.wait_recv()
-    gm[mine] += gx[...]
-    rl = hsize // chips
+    pk[mine] += gx[...]
+    rl = qsize // chips
 
     def r2_copy(d):
-        src = gm.at[pl.ds(pl.multiple_of(k * hsize + peer(d) * rl, rl), rl)]
+        src = pk.at[pl.ds(pl.multiple_of(k * qsize + peer(d) * rl, rl), rl)]
         return remote(src, r2.at[d - 1], r2_s.at[d - 1], r2_r.at[d - 1], at_peer(d))
 
     for d in range(1, chips):
@@ -377,7 +393,7 @@
         await_(ld.at[n // 2, _at(n % 2, HALF)], l_r.at[n // 2, n % 2])
 
     _loop(0, 2 * rows, got_l)
-    ev = col % 2 == 0
+    ev = my_j % 2 == 0
     lo_half = lax.broadcasted_iota(jnp.int32, (size, LANES), 1) < EDGE
     l_lo, l_hi = ld[:, :, pl.ds(0, LANES)].reshape(size, LANES), ld[:, :, pl.ds(LANES, LANES)].reshape(size, LANES)
     lx[x] = jnp.where(
@@ -389,11 +405,11 @@
     def lx_copy(d):
         return remote(lx.at[x], lx.at[x], lx_s.at[d - 1], lx_r.at[d - 1], at_peer(d))
 
-    tick(4)
+    tick(2)
     for d in range(1, chips):
         r2_copy(d).wait_recv()
-    my_rows = pl.ds(pl.multiple_of(k * hsize + x * rl, rl), rl)
-    total = gm[my_rows]
+    my_rows = pl.ds(pl.multiple_of(k * qsize + x * rl, rl), rl)
+    total = pk[my_rows]
     for d in range(1, chips):
         total = total + r2[d - 1]
     ga[my_rows] = total
@@ -405,41 +421,41 @@
         ga_copy(d).start()
     for d in range(1, chips):
         lx_copy(d).start()
-    tick(5)
+    tick(3)
     for d in range(1, chips):
-        await_(ga.at[pl.ds(pl.multiple_of(k * hsize + peer(chips - d) * rl, rl), rl)], ga_r.at[d - 1])
+        await_(ga.at[pl.ds(pl.multiple_of(k * qsize + peer(chips - d) * rl, rl), rl)], ga_r.at[d - 1])
     half_to_mate = remote(ga.at[mine], ga.at[mine], gx_sem.at[2], gx_sem.at[3], mate)
     half_to_mate.start()
 
-    n128 = size // LANES
     r_i = lax.broadcasted_iota(jnp.int32, (LANES, LANES), 0)
     c_i = lax.broadcasted_iota(jnp.int32, (LANES, LANES), 1)
 
     def tile(i):
         return _at(i, LANES), _at(i, LANES)
 
-    def level_small(w, c_ref, lev):
+    def merge_tile(w, i, low_part):
+        cur = xm[(w, *tile(i))]
+        xm[(w, *tile(i))] = cur - _dot_nn(_dot_nn(cur, low_part), cur)
+
+    def level_l(lev):
         pick = jnp.logical_and(
             lax.shift_right_logical(r_i, lev) % 2 == 1,
             lax.shift_right_logical(c_i, lev) + 1 == lax.shift_right_logical(r_i, lev),
         )
-
-        def one(i):
-            at = tile(i)
-            cur = xm[(w, *at)]
-            low_part = jnp.where(pick, c_ref[at], 0.0)
-            xm[(w, *at)] = cur - _dot_nn(_dot_nn(cur, low_part), cur)
-
-        _loop(0, n128, one)
-
-    def level_big(w, c_ref):
-        width_ = LANES
-        while width_ < size:
-            for i in range(size // (2 * width_)):
-                d1 = pl.ds(2 * i * width_, width_)
-                d2 = pl.ds((2 * i + 1) * width_, width_)
-                xm[w, d2, d1] = -_dot_nn(_dot_nn(xm[w, d2, d2], c_ref[d2, d1]), xm[w, d1, d1])
-            width_ *= 2
+        _loop(0, n128, lambda i: merge_tile(1, i, jnp.where(pick, gm[tile(i)], 0.0)))
+
+    def level_big(w, corner):
+        for w_ in reversed(widths[:-1]):
+            for i in range(hsize // w_):
+                d1 = pl.ds(2 * i * w_, w_)
+                d2 = pl.ds((2 * i + 1) * w_, w_)
+                xm[w, d2, d1] = -_dot_nn(_dot_nn(xm[w, d2, d2], corner(w_, i)), xm[w, d1, d1])
+
+    def pack_factor(w):
+        for i in range(n128):
+            pm[w, :, pl.ds(LANES * (i * (i + 1) // 2), LANES * (i + 1))] = xm[
+                w, pl.ds(pl.multiple_of(i * LANES + k * EDGE, EDGE), EDGE), pl.ds(0, LANES * (i + 1))
+            ]
 
     xm[...] = jnp.zeros_like(xm)
     ins[3].wait()
@@ -450,17 +466,22 @@
         )
         xm[0, pl.ds(p * EDGE, LANES), pl.ds(p * EDGE, LANES)] = both
     await_(ga.at[theirs], gx_sem.at[3])
-    level_small(0, ga, 6)
-    level_big(0, ga)
-    tick(6)
+
+    def corner64(i):
+        block = ga[_at(i, EDGE), packed(EDGE)]
+        zero = jnp.zeros((EDGE, EDGE), jnp.float32)
+        low_part = jnp.concatenate([block, zero], axis=1)
+        merge_tile(0, i, jnp.concatenate([jnp.zeros_like(low_part), low_part], axis=0))
+
+    _loop(0, n128, corner64)
+    level_big(0, lambda w_, i: ga[pl.ds(i * w_, w_), packed(w_)])
+    pack_factor(0)
+    tick(4)
 
     fetch_blk(0)
     fetch_blk(1)
     for d in range(1, chips):
         await_(lx.at[peer(chips - d)], lx_r.at[d - 1])
-    to_mate.wait_send()
-    for d in range(1, chips):
-        r2_copy(d).wait_send()
     for i in range(chips):
         gm[_at(i, LANES), :] = lx[i].T
     same = r_i == c_i
@@ -471,13 +492,14 @@
 
     _loop(0, n128, diag)
     swapped(2)
+    tick(5)
+    _loop(0, 3, level_l)
+    tick(6)
+    _loop(3, 7, level_l)
     tick(7)
-    _loop(0, 3, lambda i: level_small(1, gm, i))
+    level_big(1, lambda w_, i: gm[pl.ds((2 * i + 1) * w_, w_), pl.ds(2 * i * w_, w_)])
+    pack_factor(1)
     tick(8)
-    _loop(3, 7, lambda i: level_small(1, gm, i))
-    tick(9)
-    level_big(1, gm)
-    tick(10)
     fetch_mat(0)
     fetch_mat(1)
 
@@ -591,6 +613,17 @@
         src = wb.at[g, pl.ds(0, sl), _at(peer(d), LANES)]
         return remote(src, xr.at[g, _at(x, sl)], ex_s.at[g, d - 1], ex_r.at[g, d - 1], at_peer(d))
 
+    for m in range(3):
+        _loop(0, pairs, lambda i, m=m: swaps(m, i)[1].wait_send())
+    over_v(sent)
+    over_l(sent)
+    to_mate.wait_send()
+    half_to_mate.wait_send()
+    for d in range(1, chips):
+        r2_copy(d).wait_send()
+        ga_copy(d).wait_send()
+        lx_copy(d).wait_send()
+
     wait_blk(nb)
     wait_mat(nb)
     for g in range(2):
@@ -644,31 +677,23 @@
 
     def fin_copy(i):
         return remote(
-            xs.at[:, _at(2 * i + 1 - k, LANES)], xf.at[_at(k, ncol), _at(i, LANES)], fin_s.at[i], fin_r.at[i], mate
+            xs.at[:, _at(2 * i + 1 - k, LANES)], zt.at[k, :, _at(i, LANES)], fin_s.at[i], fin_r.at[i], mate
         )
 
     _loop(0, pairs, lambda i: fin_copy(i).start())
 
     def own_cols(i):
-        xf[_at(k, ncol), _at(i, LANES)] = xs[:, _at(2 * i + k, LANES)]
+        zt[k, :, _at(i, LANES)] = xs[:, _at(2 * i + k, LANES)]
 
     _loop(0, pairs, own_cols)
 
     def give(i):
-        await_(xf.at[_at(1 - k, ncol), _at(i, LANES)], fin_r.at[i])
-        out_ref[_at(i, LANES), :] = xf[:, _at(i, LANES)].T
+        await_(zt.at[1 - k, :, _at(i, LANES)], fin_r.at[i])
+        out_ref[_at(i, LANES), :] = zt[:, :, _at(i, LANES)].reshape(2 * ncol, LANES).T
 
     _loop(0, pairs, give)
 
     _loop(0, pairs, lambda i: fin_copy(i).wait_send())
-    for m in range(3):
-        _loop(0, pairs, lambda i, m=m: swaps(m, i)[1].wait_send())
-    over_v(sent)
-    over_l(sent)
-    half_to_mate.wait_send()
-    for d in range(1, chips):
-        ga_copy(d).wait_send()
-        lx_copy(d).wait_send()
 
 
 def solution(mesh):
@@ -681,7 +706,8 @@
         slots, lanes, chips, size = n_col // EDGE, 2 * n_row, rows // 2, rows * EDGE
         nb, ncol = lanes // LANES, z_loc.shape[1] // 2
         pairs, gcol, peers = nb // 2, ncol // 2, max(chips - 1, 1)
-        sl, gathers = gcol // chips, len(_gathers(slots))
+        sl, gathers, n128 = gcol // chips, len(_gathers(slots)), size // LANES
+        tri = LANES * (n128 * (n128 + 1) // 2)
         dma = pltpu.SemaphoreType.DMA
         hbm, vmem = pl.BlockSpec(memory_space=pl.ANY), pl.BlockSpec(memory_space=pltpu.VMEM)
 
@@ -693,10 +719,9 @@
             out_shape=[
                 jax.ShapeDtypeStruct(z_loc.shape, jnp.float32),
                 jax.ShapeDtypeStruct((2, slots, RING, RING, HALF, lanes), jnp.float32),
-                jax.ShapeDtypeStruct((2, RING, RING, size // 2, size), jnp.float32),
             ],
             in_specs=[hbm] * 4,
-            out_specs=[vmem, hbm, hbm],
+            out_specs=[vmem, hbm],
             scratch_shapes=[
                 buf(3, n_row, n_col),
                 buf(2, slots, 2, HALF, n_row),
@@ -705,24 +730,26 @@
                 buf(2, slots, HALF, lanes),
                 buf(ncol, lanes),
                 buf(ncol, lanes),
-                buf(rows, EDGE, lanes // 2),
+                buf(pairs // 2, rows, EDGE, STEP),
                 buf(rows, EDGE, STEP),
                 buf(chips, size, LANES),
                 buf(size, size),
                 buf(size // 2, size),
-                buf(peers, size // 2 // chips, size),
-                buf(size, size),
+                buf(size // 4, size),
+                buf(peers, size // 4 // chips, size),
+                buf(size // 2, size),
                 buf(2, size, size),
+                buf(2, EDGE, tri),
+                buf(2, RING, RING, EDGE, tri),
                 buf(2, rows, EDGE, lanes),
                 buf(2, size, size),
                 buf(2, 2, gcol, size),
                 buf(2, peers, sl, size),
                 buf(2, gcol, size),
                 buf(2, gcol, LANES),
-                buf(2 * ncol, n_row),
                 dma((4,)),
                 dma((3, pairs)), dma((3, pairs)), dma((3, pairs)),
-                dma((slots, 2)), dma((rows, 2)),
+                dma((slots, pairs)), dma((pairs // 2, rows, 2)),
                 dma((slots, 2)), dma((rows, 2)),
                 dma((peers,)), dma((peers,)),
                 dma((4,)),
@@ -730,7 +757,7 @@
                 dma((pairs,)), dma((pairs,)),
                 dma((gathers,)), dma((gathers, 8)), dma((gathers, 8)),
                 dma((2, rows)), dma((2, rows)), dma((2, rows)),
-                dma((2,)), dma((2,)), dma((2,)),
+                dma((2, n128)), dma((2, n128)), dma((2, n128)),
                 pltpu.SemaphoreType.REGULAR((2,)),
                 dma((2, peers)), dma((2, peers)), dma((2, peers)), dma((2, peers)),
             ],

time: 760 us -> 671 us (0.88)
  Pallas kernels: 751 us -> 662 us
    pallas_call x1, Pallas kernels: 751 us -> 662 us  [local_work(): pl.pallas_call(functools.partial(_kernel, (rows, cols, slots, nb, ncol)),...]
where the time goes in v4:
time: 671 us
  Pallas kernels  662 us (99%)
  local copies, waits for them, and re-layouts  8.67 us (1%)
    pallas_call x1, Pallas kernels, local_work(): pl.pallas_call(functools.partial(_kernel, (rows, cols, slots, nb, ncol)),...  662 us

profile of v4, /device:TPU:1, one launch (start us, length us, event | category | flops | bytes accessed | tf_op | source)
XLA Modules:
  0.0 670.6 jit_solution(15710956686231986757)
XLA Ops:
  0.0 5.6 copy.5.t_in
  5.6 661.9 %eigvec.1 = (f32[1024,512]{1,0:T(8,128)}, f32[2,8,4,4,32,2048]{5,4,3,2,1,0:T(8,128)}) custom-call(f32[1024,512]{1,0:T(8,128)} %v_in.1, f32[128,64,64]{2,1,0:T(8,128)} %copy.5.t_in, f32[1024,512]{1,0:T(8,128)} %z_in.1, f32[1024,512]{1,0:T(8,128)} %l_in.1), custom_call_target="tpu_custom_call" | custom-call | tf_op jit(solution)/shard_map/eigvec/pallas_call | solution.py:717
  667.5 3.1 copy.7

commit v5 on v4

--- a/solution.py
+++ b/solution.py
@@ -15,6 +15,7 @@
 STEP = 256
 RING = 4
 LEAD = 9
+DEEP = 3
 
 
 def _dot_nt(a, b):
@@ -45,9 +46,10 @@
 
 
 def _kernel(dims, v_in, t_in, z_in, l_in, out_ref, gath, *scratch):
-    (stage, vt, zt, tb, own, ys, xs, vb, ld, lx, gm, pk, gx, r2, ga, xm, pm, mg, blk, mbuf, sbuf, rs, wb, xr,
+    (stage, vt, zt, tb, own, ys, xs, vb, ld, lx, gm, pk, gx, r2, ga, xm, pm, mg, blk, mbuf, sbuf, rs, wb, cm, rx,
      in_sem, swap_l, swap_s, swap_r, v_s, v_r, l_s, l_r, lx_s, lx_r, gx_sem, r2_s, r2_r, ga_s, ga_r, fin_s, fin_r,
-     ag_loc, ag_s, ag_r, blk_loc, blk_s, blk_r, mat_loc, mat_s, mat_r, free, rs_s, rs_r, ex_s, ex_r) = scratch
+     ag_loc, ag_s, ag_r, blk_loc, blk_s, blk_r, mat_loc, mat_s, mat_r, free_b, free_m, rs_s, rs_r, ex_s, ex_r, cm_s, cm_r,
+     rx_s, rx_r) = scratch
     rows, cols, slots, nb, ncol = dims
     row, col = lax.axis_index("row"), lax.axis_index("col")
     x, k = row // 2, row % 2
@@ -182,15 +184,15 @@
         return n // nb, j, j // groups, j % groups, n % 2
 
     def blk_copies(n, q, p):
-        w, _, _, h, s = block_of(n)
-        c = h * rows + p
+        w, _, _, h, _ = block_of(n)
+        s, c = n % DEEP, h * rows + p
         at = pl.ds(low(q), lanes - low(q))
         src = gath.at[w, q, (c // s_b) % RING, (c // s_a) % RING, :, at]
         dst = blk.at[s, p, k_half, at]
         return pltpu.make_async_copy(src, dst, blk_loc.at[s, p]), remote(src, dst, blk_s.at[s, p], blk_r.at[s, p], mate)
 
     def from_mate(n, q, p):
-        await_(blk.at[n % 2, p, m_half, pl.ds(low(q), lanes - low(q))], blk_r.at[n % 2, p])
+        await_(blk.at[n % DEEP, p, m_half, pl.ds(low(q), lanes - low(q))], blk_r.at[n % DEEP, p])
 
     def mat_copies(n, i):
         w, j, q, h, s = block_of(n)
@@ -235,23 +237,30 @@
             there = pl.ds(pl.multiple_of(i * LANES + (1 - k) * EDGE, EDGE), EDGE), pl.ds(0, LANES * (i + 1))
             await_(mbuf.at[(n % 2, *there)], mat_r.at[n % 2, i])
 
-    def release(n):
+    def release_blk(n):
         per_piece(n, lambda q, p: blk_copies(n, q, p)[1].wait_send())
+
+        @pl.when(n + DEEP < 2 * nb)
+        def _():
+            pl.semaphore_signal(free_b.at[n % DEEP], inc=1, device_id=mate, device_id_type=MESH)
+            pl.semaphore_wait(free_b.at[n % DEEP], 1)
+            fetch_blk(n + DEEP)
+
+    def release_mat(n):
         for i in range(n128):
             mat_copies(n, i)[1].wait_send()
 
         @pl.when(n + 2 < 2 * nb)
         def _():
-            pl.semaphore_signal(free.at[n % 2], inc=1, device_id=mate, device_id_type=MESH)
-            pl.semaphore_wait(free.at[n % 2], 1)
-            fetch_blk(n + 2)
+            pl.semaphore_signal(free_m.at[n % 2], inc=1, device_id=mate, device_id_type=MESH)
+            pl.semaphore_wait(free_m.at[n % 2], 1)
             fetch_mat(n + 2)
 
     ins = [
-        pltpu.make_async_copy(src, stage.at[i], in_sem.at[i]) for i, src in enumerate((v_in, l_in, z_in))
+        pltpu.make_async_copy(src, stage.at[i % 2], in_sem.at[i]) for i, src in enumerate((v_in, l_in, z_in))
     ] + [pltpu.make_async_copy(t_in.at[_at(groups * part + grp, rows)], tb, in_sem.at[3])]
-    for c in ins:
-        c.start()
+    for i in (0, 1, 3):
+        ins[i].start()
 
     def swaps(m, i):
         there = _at(2 * i + k, LANES)
@@ -274,7 +283,7 @@
         ins[m].wait()
 
         def one(i):
-            block = stage[m, _at(i, LANES), :].T
+            block = stage[m % 2, _at(i, LANES), :].T
             if m < 2:
                 vt[m, :, :, :, _at(i, LANES)] = block.reshape(slots, 2, HALF, LANES)
             else:
@@ -338,6 +347,7 @@
         _loop(0, slots, one)
 
     turn(0)
+    ins[2].start()
     swapped(0)
     over_v(send)
     turn(1)
@@ -502,87 +512,131 @@
     tick(8)
     fetch_mat(0)
     fetch_mat(1)
-
-    def cut(s, i):
-        return blk[s, :, :, _at(i, STEP)].reshape(size, STEP)
-
-    def rs_copy(par, g, d):
-        return remote(sbuf.at[par, g, _at(peer(d), sl)], rs.at[g, d - 1], rs_s.at[g, d - 1], rs_r.at[g, d - 1], at_peer(d))
-
-    def send_partial(par, g):
-        for d in range(1, chips):
-            rs_copy(par, g, d).start()
-
-    def gather_sum(par, g):
-        for d in range(1, chips):
-            rs_copy(par, g, d).wait_recv()
-        total = sbuf[par, g, _at(x, sl)]
-        for d in range(1, chips):
-            total = total + rs[g, d - 1]
-        for d in range(1, chips):
-            rs_copy(par, g, d).wait_send()
-        return total
+    fetch_blk(2)
+
+    def over(first, body):
+        pl.when(first % 2 == 1)(lambda: body(first * STEP, STEP))
+        _loop((first + 1) // 2, whole // 2, lambda i: body(i * 2 * STEP, 2 * STEP))
+
+    def rows_at(off, width):
+        return pl.ds(pl.multiple_of(off, STEP), width)
+
+    def cut(n, off, width):
+        return blk[n % DEEP, :, :, rows_at(off, width)].reshape(size, width)
+
+    def project(dst, ref, n, first):
+        dst[...] = jnp.zeros((ncol, size), jnp.float32)
+
+        def one(off, width):
+            dst[...] += _dot_nt(ref[:, rows_at(off, width)], cut(n, off, width))
+
+        over(first, one)
+
+    def slice_of(g, x2):
+        return pl.ds(pl.multiple_of(g * gcol + x2 * sl, sl), sl)
 
     def cols_of(g):
         return pl.ds(g * gcol, gcol)
 
-    def project(par, g, s, ref, first):
-        sbuf[par, g] = jnp.zeros((gcol, size), jnp.float32)
-
-        def one(i):
-            sbuf[par, g] += _dot_nt(ref[cols_of(g), _at(i, STEP)], cut(s, i))
-
-        _loop(first, whole, one)
-
-    def ex_wait(g, d, ref):
-        await_(ref.at[g, _at(peer(chips - d), sl)], ex_r.at[g, d - 1])
-
-    def w_copy(g, d):
-        mine = wb.at[g, _at(x, sl)]
+    def rs_copy(par, g, d):
+        return remote(sbuf.at[par, slice_of(g, peer(d))], rs.at[g, d - 1], rs_s.at[g, d - 1], rs_r.at[g, d - 1], at_peer(d))
+
+    def w_copy(par, g, d):
+        mine = wb.at[par, slice_of(g, x)]
         return remote(mine, mine, ex_s.at[g, d - 1], ex_r.at[g, d - 1], at_peer(d))
 
+    c_half = pl.ds(pl.multiple_of(k * (rows // 2), rows // 2), rows // 2)
+
+    def c_copy(par):
+        return remote(cm.at[par, _at(k, hsize)], cm.at[par, _at(k, hsize)], cm_s.at[par], cm_r.at[par], mate)
+
+    def apply(n):
+        def one(off, width):
+            ys[:, rows_at(off, width)] = ys[:, rows_at(off, width)] - _dot_nn(wb[n % 2], cut(n, off, width))
+
+        over((top - n) // 2, one)
+
     wait_blk(0)
+    project(sbuf.at[0], ys, 0, top // 2)
     for g in range(2):
-        project(0, g, 0, ys, top // 2)
-        send_partial(0, g)
+        for d in range(1, chips):
+            rs_copy(0, g, d).start()
     wait_mat(0)
 
     def reflect(n):
-        j, s = top - n, n % 2
-        for g in range(2):
-            wb[g, _at(x, sl)] = _dot_nn(gather_sum(0, g), mbuf[s])
-            for d in range(1, chips):
-                w_copy(g, d).start()
-
-        @pl.when(s == 0)
-        def _():
-            tick(LEAD + n // 2)
+        j, par, nxt = top - n, n % 2, (n + 1) % 2
+
+        @pl.when(n > 0)
+        def _():
+            apply(n - 1)
+            release_blk(n - 1)
 
         @pl.when(j > 0)
         def _():
             wait_blk(n + 1)
-            wait_mat(n + 1)
+            project(sbuf.at[nxt], ys, n + 1, (j - 1) // 2)
 
         for g in range(2):
             for d in range(1, chips):
-                ex_wait(g, d, wb)
-
-            def apply(i, g=g):
-                at = cols_of(g), _at(i, STEP)
-                ys[at] = ys[at] - _dot_nn(wb[g], cut(s, i))
-
-            _loop(j // 2, whole, apply)
+                rs_copy(par, g, d).wait_recv()
+            total = sbuf[par, slice_of(g, x)]
             for d in range(1, chips):
-                w_copy(g, d).wait_send()
+                total = total + rs[g, d - 1]
+            wb[par, slice_of(g, x)] = _dot_nn(total, mbuf[par])
+            for d in range(1, chips):
+                w_copy(par, g, d).start()
+
+        release_mat(n)
+
+        @pl.when(j > 0)
+        def _():
+            cm[par, _at(k, hsize)] = jnp.zeros((hsize, size), jnp.float32)
+
+            def one(off, width):
+                here = blk[n % DEEP, c_half, :, rows_at(off, width)].reshape(hsize, width)
+                cm[par, _at(k, hsize)] += _dot_nt(here, cut(n + 1, off, width))
+
+            over(j // 2, one)
+            c_copy(par).start()
+
+        @pl.when(jnp.logical_and(n < 8, par == 0))
+        def _():
+            tick(LEAD + n // 2)
+
+        @pl.when(n >= 8)
+        def _():
+            tick(LEAD - 4 + n)
+
+        for g in range(2):
+            for d in range(1, chips):
+                rs_copy(par, g, d).wait_send()
+
+        @pl.when(j > 0)
+        def _():
+            wait_mat(n + 1)
+            await_(cm.at[par, _at(1 - k, hsize)], cm_r.at[par])
+
+        for g in range(2):
+            for d in range(1, chips):
+                await_(wb.at[par, slice_of(g, peer(chips - d))], ex_r.at[g, d - 1])
 
             @pl.when(j > 0)
             def _(g=g):
-                project(0, g, 1 - s, ys, (j - 1) // 2)
-                send_partial(0, g)
-
-        release(n)
+                sbuf[nxt, cols_of(g)] = sbuf[nxt, cols_of(g)] - _dot_nn(wb[par, cols_of(g)], cm[par])
+                for d in range(1, chips):
+                    rs_copy(nxt, g, d).start()
+
+        for g in range(2):
+            for d in range(1, chips):
+                w_copy(par, g, d).wait_send()
+
+        @pl.when(j > 0)
+        def _():
+            c_copy(par).wait_send()
 
     _loop(0, nb, reflect)
+    apply(top)
+    release_blk(top)
 
     xs[...] = jnp.zeros_like(xs)
     first_half = lax.broadcasted_iota(jnp.int32, (gcol, LANES), 1) < EDGE
@@ -605,13 +659,17 @@
         hi = jnp.where(even, jnp.where(first_half, other, zero), jnp.where(first_half, zero, val))
         return jnp.concatenate([lo, hi], axis=1)
 
-    def right_side(par, g, j):
-        sbuf[par, g] = -sbuf[par, g]
-        sbuf[par, g, :, _at(x, LANES)] += take(ys, g, j)
-
-    def x_copy(g, d):
-        src = wb.at[g, pl.ds(0, sl), _at(peer(d), LANES)]
-        return remote(src, xr.at[g, _at(x, sl)], ex_s.at[g, d - 1], ex_r.at[g, d - 1], at_peer(d))
+    def x_copy(par, g, d):
+        src = sbuf.at[par, cols_of(g), _at(peer(d), LANES)]
+        return remote(src, rx.at[par, g, d - 1], rx_s.at[par, g, d - 1], rx_r.at[par, g, d - 1], at_peer(d))
+
+    def solve_partial(n, g, j):
+        par = n % 2
+        wb[0, cols_of(g)] = -wb[0, cols_of(g)]
+        wb[0, cols_of(g), _at(x, LANES)] += take(ys, g, j)
+        sbuf[par, cols_of(g)] = _dot_nn(wb[0, cols_of(g)], mbuf[par])
+        for d in range(1, chips):
+            x_copy(par, g, d).start()
 
     for m in range(3):
         _loop(0, pairs, lambda i, m=m: swaps(m, i)[1].wait_send())
@@ -626,52 +684,46 @@
 
     wait_blk(nb)
     wait_mat(nb)
+    wb[0] = jnp.zeros((ncol, size), jnp.float32)
     for g in range(2):
-        sbuf[0, g] = jnp.zeros((gcol, size), jnp.float32)
-        right_side(0, g, top)
-        send_partial(0, g)
+        solve_partial(nb, g, top)
+    release_blk(nb)
+    release_mat(nb)
 
     def solve(i):
         n = nb + i
-        j = top - i
-        par, nxt = n % 2, (n + 1) % 2
+        j, par, nxt = top - i, n % 2, (n + 1) % 2
 
         @pl.when(j > 0)
         def _():
             wait_blk(n + 1)
             wait_mat(n + 1)
-
-        for g in range(2):
-
-            @pl.when(j > 0)
-            def _(g=g):
-                project(nxt, g, nxt, xs, (j + 1) // 2)
-
-            wb[g, pl.ds(0, sl)] = _dot_nn(gather_sum(par, g), mbuf[par])
-            for d in range(1, chips):
-                x_copy(g, d).start()
-            xr[g, _at(x, sl)] = wb[g, pl.ds(0, sl), _at(x, LANES)]
-
-        @pl.when(par == 0)
-        def _():
-            tick(LEAD + n // 2)
+            project(wb.at[0], xs, n + 1, (j + 1) // 2)
 
         for g in range(2):
             for d in range(1, chips):
-                ex_wait(g, d, xr)
-            solved = spread(xr[g], j)
+                x_copy(par, g, d).wait_recv()
+            val = sbuf[par, cols_of(g), _at(x, LANES)]
+            for d in range(1, chips):
+                val = val + rx[par, g, d - 1]
+            solved = spread(val, j)
             xs[cols_of(g), _at(j // 2, STEP)] += solved
 
             @pl.when(j > 0)
             def _(g=g, solved=solved):
-                sbuf[nxt, g] += _dot_nt(solved, cut(nxt, j // 2))
-                right_side(nxt, g, j - 1)
-                send_partial(nxt, g)
-
+                wb[0, cols_of(g)] += _dot_nt(solved, cut(n + 1, (j // 2) * STEP, STEP))
+                solve_partial(n + 1, g, j - 1)
+
+        for g in range(2):
             for d in range(1, chips):
-                x_copy(g, d).wait_send()
-
-        release(n)
+                x_copy(par, g, d).wait_send()
+
+        @pl.when(j > 0)
+        def _():
+            release_blk(n + 1)
+            release_mat(n + 1)
+
+        tick(LEAD - 4 + n)
 
     _loop(0, nb, solve)
 
@@ -723,7 +775,7 @@
             in_specs=[hbm] * 4,
             out_specs=[vmem, hbm],
             scratch_shapes=[
-                buf(3, n_row, n_col),
+                buf(2, n_row, n_col),
                 buf(2, slots, 2, HALF, n_row),
                 buf(2, ncol, n_row),
                 buf(rows, EDGE, EDGE),
@@ -741,12 +793,13 @@
                 buf(2, size, size),
                 buf(2, EDGE, tri),
                 buf(2, RING, RING, EDGE, tri),
-                buf(2, rows, EDGE, lanes),
+                buf(DEEP, rows, EDGE, lanes),
                 buf(2, size, size),
-                buf(2, 2, gcol, size),
+                buf(2, ncol, size),
                 buf(2, peers, sl, size),
-                buf(2, gcol, size),
-                buf(2, gcol, LANES),
+                buf(2, ncol, size),
+                buf(2, size, size),
+                buf(2, 2, peers, gcol, LANES),
                 dma((4,)),
                 dma((3, pairs)), dma((3, pairs)), dma((3, pairs)),
                 dma((slots, pairs)), dma((pairs // 2, rows, 2)),
@@ -756,12 +809,14 @@
                 dma((peers,)), dma((peers,)), dma((peers,)), dma((peers,)),
                 dma((pairs,)), dma((pairs,)),
                 dma((gathers,)), dma((gathers, 8)), dma((gathers, 8)),
-                dma((2, rows)), dma((2, rows)), dma((2, rows)),
+                dma((DEEP, rows)), dma((DEEP, rows)), dma((DEEP, rows)),
                 dma((2, n128)), dma((2, n128)), dma((2, n128)),
-                pltpu.SemaphoreType.REGULAR((2,)),
+                pltpu.SemaphoreType.REGULAR((DEEP,)), pltpu.SemaphoreType.REGULAR((2,)),
                 dma((2, peers)), dma((2, peers)), dma((2, peers)), dma((2, peers)),
+                dma((2,)), dma((2,)),
+                dma((2, 2, peers)), dma((2, 2, peers)),
             ],
-            compiler_params=pltpu.CompilerParams(has_side_effects=True, vmem_limit_bytes=60 * 1024 * 1024),
+            compiler_params=pltpu.CompilerParams(has_side_effects=True, vmem_limit_bytes=63 * 1024 * 1024),
             name="eigvec",
         )(v_loc, t_loc, z_loc, l_loc)[0]
 

time: 671 us -> 526 us (0.78)
  Pallas kernels: 662 us -> 518 us
    pallas_call x1, Pallas kernels: 662 us -> 518 us  [local_work(): pl.pallas_call(functools.partial(_kernel, (rows, cols, slots, nb, ncol)),...]
where the time goes in v5:
time: 526 us
  Pallas kernels  518 us (98%)
  local copies, waits for them, and re-layouts  8.67 us (2%)
    pallas_call x1, Pallas kernels, local_work(): pl.pallas_call(functools.partial(_kernel, (rows, cols, slots, nb, ncol)),...  518 us

profile of v5, /device:TPU:1, one launch (start us, length us, event | category | flops | bytes accessed | tf_op | source)
XLA Modules:
  0.0 526.3 jit_solution(10569460700351824653)
XLA Ops:
  0.0 5.6 %copy.5.t_in = f32[128,64,64]{2,1,0:T(8,128)} copy(f32[128,64,64]{0,2,1:T(8,128)} %param.5) | data formatting | bytes 4194304 | tf_op args[1]
  5.6 517.6 %eigvec.1 = (f32[1024,512]{1,0:T(8,128)}, f32[2,8,4,4,32,2048]{5,4,3,2,1,0:T(8,128)}) custom-call(f32[1024,512]{1,0:T(8,128)} %v_in.1, f32[128,64,64]{2,1,0:T(8,128)} %copy.5.t_in, f32[1024,512]{1,0:T(8,128)} %z_in.1, f32[1024,512]{1,0:T(8,128)} %l_in.1), custom_call_target="tpu_custom_call" | custom-call | tf_op jit(solution)/shard_map/eigvec/pallas_call | solution.py:769
  523.2 3.1 copy.7

commit v6 on v5

--- a/solution.py
+++ b/solution.py
@@ -256,11 +256,28 @@
             pl.semaphore_wait(free_m.at[n % 2], 1)
             fetch_mat(n + 2)
 
+    barrier = pltpu.get_barrier_semaphore()
+
+    def here_i_am(device):
+        pl.semaphore_signal(barrier, inc=1, device_id=device, device_id_type=MESH)
+
+    def group_member(d):
+        n = lax.rem(2 * part + k + d, 2 * rows)
+        here_i_am({"col": grp * rows + n // 2, "row": 2 * x + n % 2})
+
+    _loop(1, 2 * rows, group_member)
+    for d in range(1, chips):
+        here_i_am(at_peer(d))
+    for d in (1, RING - 1):
+        here_i_am(plane(d, 0))
+        here_i_am(plane(0, d))
+
     ins = [
         pltpu.make_async_copy(src, stage.at[i % 2], in_sem.at[i]) for i, src in enumerate((v_in, l_in, z_in))
-    ] + [pltpu.make_async_copy(t_in.at[_at(groups * part + grp, rows)], tb, in_sem.at[3])]
+    ] + [pltpu.make_async_copy(t_in, tb, in_sem.at[3])]
     for i in (0, 1, 3):
         ins[i].start()
+    pl.semaphore_wait(barrier, 2 * rows - 1 + chips - 1 + 4)
 
     def swaps(m, i):
         there = _at(2 * i + k, LANES)
@@ -279,7 +296,7 @@
         there = _at(2 * i + 1 - k, LANES)
         await_(own.at[m, :, :, there] if m < 2 else ys.at[:, there], swap_r.at[m, i])
 
-    def turn(m):
+    def turn(m, then=None):
         ins[m].wait()
 
         def one(i):
@@ -290,8 +307,12 @@
                 zt[:, :, _at(i, LANES)] = block.reshape(2, ncol, LANES)
             for c in swaps(m, i):
                 c.start()
+            if then is not None:
+                pl.when(i > 0)(lambda: then(i - 1))
 
         _loop(0, pairs, one)
+        if then is not None:
+            then(pairs - 1)
 
     def swapped(m):
         def one(i):
@@ -346,10 +367,13 @@
 
         _loop(0, slots, one)
 
-    turn(0)
+    def deal_chunk(t):
+        swaps(0, t)[0].wait()
+        arriving(0, t)
+        _loop(0, (2 * t + 1 - grp + groups) // groups, lambda q: deal_v(q, t, send))
+
+    turn(0, deal_chunk)
     ins[2].start()
-    swapped(0)
-    over_v(send)
     turn(1)
     swapped(1)
     over_l(send)
@@ -565,16 +589,19 @@
 
     def reflect(n):
         j, par, nxt = top - n, n % 2, (n + 1) % 2
-
-        @pl.when(n > 0)
-        def _():
-            apply(n - 1)
-            release_blk(n - 1)
+        pl.when(n > 0)(lambda: apply(n - 1))
 
         @pl.when(j > 0)
         def _():
             wait_blk(n + 1)
-            project(sbuf.at[nxt], ys, n + 1, (j - 1) // 2)
+            cm[par, _at(k, hsize)] = jnp.zeros((hsize, size), jnp.float32)
+
+            def one(off, width):
+                here = blk[n % DEEP, c_half, :, rows_at(off, width)].reshape(hsize, width)
+                cm[par, _at(k, hsize)] += _dot_nt(here, cut(n + 1, off, width))
+
+            over(j // 2, one)
+            c_copy(par).start()
 
         for g in range(2):
             for d in range(1, chips):
@@ -586,18 +613,9 @@
             for d in range(1, chips):
                 w_copy(par, g, d).start()
 
-        release_mat(n)
-
-        @pl.when(j > 0)
-        def _():
-            cm[par, _at(k, hsize)] = jnp.zeros((hsize, size), jnp.float32)
-
-            def one(off, width):
-                here = blk[n % DEEP, c_half, :, rows_at(off, width)].reshape(hsize, width)
-                cm[par, _at(k, hsize)] += _dot_nt(here, cut(n + 1, off, width))
-
-            over(j // 2, one)
-            c_copy(par).start()
+        for g in range(2):
+            for d in range(1, chips):
+                rs_copy(par, g, d).wait_send()
 
         @pl.when(jnp.logical_and(n < 8, par == 0))
         def _():
@@ -607,12 +625,12 @@
         def _():
             tick(LEAD - 4 + n)
 
-        for g in range(2):
-            for d in range(1, chips):
-                rs_copy(par, g, d).wait_send()
+        pl.when(n > 0)(lambda: release_blk(n - 1))
+        release_mat(n)
 
         @pl.when(j > 0)
         def _():
+            project(sbuf.at[nxt], ys, n + 1, (j - 1) // 2)
             wait_mat(n + 1)
             await_(cm.at[par, _at(1 - k, hsize)], cm_r.at[par])
 
@@ -670,6 +688,16 @@
         sbuf[par, cols_of(g)] = _dot_nn(wb[0, cols_of(g)], mbuf[par])
         for d in range(1, chips):
             x_copy(par, g, d).start()
+
+    def fin_copy(i):
+        return remote(
+            xs.at[:, _at(2 * i + 1 - k, LANES)], zt.at[k, :, _at(i, LANES)], fin_s.at[i], fin_r.at[i], mate
+        )
+
+    def give(i):
+        await_(zt.at[1 - k, :, _at(i, LANES)], fin_r.at[i])
+        zt[k, :, _at(i, LANES)] = xs[:, _at(2 * i + k, LANES)]
+        out_ref[_at(i, LANES), :] = zt[:, :, _at(i, LANES)].reshape(2 * ncol, LANES).T
 
     for m in range(3):
         _loop(0, pairs, lambda i, m=m: swaps(m, i)[1].wait_send())
@@ -714,6 +742,9 @@
                 wb[0, cols_of(g)] += _dot_nt(solved, cut(n + 1, (j // 2) * STEP, STEP))
                 solve_partial(n + 1, g, j - 1)
 
+        pl.when(j % 2 == 0)(lambda: fin_copy(j // 2).start())
+        pl.when(jnp.logical_and(j % 2 == 1, j < top))(lambda: give(j // 2 + 1))
+
         for g in range(2):
             for d in range(1, chips):
                 x_copy(par, g, d).wait_send()
@@ -727,24 +758,7 @@
 
     _loop(0, nb, solve)
 
-    def fin_copy(i):
-        return remote(
-            xs.at[:, _at(2 * i + 1 - k, LANES)], zt.at[k, :, _at(i, LANES)], fin_s.at[i], fin_r.at[i], mate
-        )
-
-    _loop(0, pairs, lambda i: fin_copy(i).start())
-
-    def own_cols(i):
-        zt[k, :, _at(i, LANES)] = xs[:, _at(2 * i + k, LANES)]
-
-    _loop(0, pairs, own_cols)
-
-    def give(i):
-        await_(zt.at[1 - k, :, _at(i, LANES)], fin_r.at[i])
-        out_ref[_at(i, LANES), :] = zt[:, :, _at(i, LANES)].reshape(2 * ncol, LANES).T
-
-    _loop(0, pairs, give)
-
+    give(0)
     _loop(0, pairs, lambda i: fin_copy(i).wait_send())
 
 
@@ -766,6 +780,8 @@
         def buf(*shape):
             return pltpu.VMEM(shape, jnp.float32)
 
+        col = lax.axis_index("col")
+        t_mine = lax.dynamic_slice_in_dim(t_loc, (cols // rows * (col % rows) + col // rows) * rows, rows, axis=0)
         return pl.pallas_call(
             functools.partial(_kernel, (rows, cols, slots, nb, ncol)),
             out_shape=[
@@ -816,8 +832,8 @@
                 dma((2,)), dma((2,)),
                 dma((2, 2, peers)), dma((2, 2, peers)),
             ],
-            compiler_params=pltpu.CompilerParams(has_side_effects=True, vmem_limit_bytes=63 * 1024 * 1024),
+            compiler_params=pltpu.CompilerParams(collective_id=0, has_side_effects=True, vmem_limit_bytes=63 * 1024 * 1024),
             name="eigvec",
-        )(v_loc, t_loc, z_loc, l_loc)[0]
+        )(v_loc, t_mine, z_loc, l_loc)[0]
 
     return jax.shard_map(local_work, mesh=mesh, in_specs=(mat_spec, fac_spec, mat_spec, mat_spec), out_specs=mat_spec, check_vma=False)

time: 526 us -> 497 us (0.945)
  Pallas kernels: 518 us -> 491 us
    pallas_call x1, Pallas kernels: 518 us -> 491 us  [local_work(): pl.pallas_call(functools.partial(_kernel, (rows, cols, slots, nb, ncol)),...]
where the time goes in v6:
time: 497 us
  Pallas kernels  491 us (99%)
  local copies, waits for them, and re-layouts  6.57 us (1%)
    pallas_call x1, Pallas kernels, local_work(): pl.pallas_call(functools.partial(_kernel, (rows, cols, slots, nb, ncol)),...  491 us

profile of v6, /device:TPU:1, one launch (start us, length us, event | category | flops | bytes accessed | tf_op | source)
XLA Modules:
  0.0 497.1 jit_solution(4797886822079710780)
XLA Ops:
  0.0 2.2 constant_dynamic-slice_fusion
  2.2 1.3 copy.6.t_in
  3.5 490.5 %eigvec.1 = (f32[1024,512]{1,0:T(8,128)}, f32[2,8,4,4,32,2048]{5,4,3,2,1,0:T(8,128)}) custom-call(f32[1024,512]{1,0:T(8,128)} %v_in.1, f32[8,64,64]{2,1,0:T(8,128)} %copy.6.t_in, f32[1024,512]{1,0:T(8,128)} %z_in.1, f32[1024,512]{1,0:T(8,128)} %l_in.1), custom_call_target="tpu_custom_call" | custom-call | tf_op jit(solution)/shard_map/eigvec/pallas_call | solution.py:785
  494.1 3.1 copy.8

commit v7 on v6

--- a/solution.py
+++ b/solution.py
@@ -183,16 +183,14 @@
         j = top - n % nb
         return n // nb, j, j // groups, j % groups, n % 2
 
-    def blk_copies(n, q, p):
-        w, _, _, h, _ = block_of(n)
-        s, c = n % DEEP, h * rows + p
-        at = pl.ds(low(q), lanes - low(q))
-        src = gath.at[w, q, (c // s_b) % RING, (c // s_a) % RING, :, at]
-        dst = blk.at[s, p, k_half, at]
-        return pltpu.make_async_copy(src, dst, blk_loc.at[s, p]), remote(src, dst, blk_s.at[s, p], blk_r.at[s, p], mate)
-
-    def from_mate(n, q, p):
-        await_(blk.at[n % DEEP, p, m_half, pl.ds(low(q), lanes - low(q))], blk_r.at[n % DEEP, p])
+    run = min(rows, RING)
+    runs = rows // run
+
+    def in_blk(n, q, i, half):
+        return blk.at[n % DEEP, pl.ds(i * run, run), half, pl.ds(low(q), lanes - low(q))]
+
+    def from_mate(n, q, i):
+        await_(in_blk(n, q, i, m_half), blk_r.at[n % DEEP, i])
 
     def mat_copies(n, i):
         w, j, q, h, s = block_of(n)
@@ -210,12 +208,25 @@
 
             @pl.when(q_now == q)
             def _(q=q):
-                _loop(0, rows, functools.partial(act, q))
+                for i in range(runs):
+                    act(q, i)
 
     def fetch_blk(n):
-        def go(q, p):
-            for c in blk_copies(n, q, p):
-                c.start()
+        w, _, _, h, _ = block_of(n)
+        s = n % DEEP
+
+        def go(q, i):
+            c = h * rows + i * run
+            z_now, y_run = c // RING, pl.ds(c % RING, run)
+            at = pl.ds(low(q), lanes - low(q))
+            dst = in_blk(n, q, i, k_half)
+
+            def both(src):
+                pltpu.make_async_copy(src, dst, blk_loc.at[s, i]).start()
+                remote(src, dst, blk_s.at[s, i], blk_r.at[s, i], mate).start()
+
+            pl.when(k == 0)(lambda: both(gath.at[w, q, z_now, y_run, :, at]))
+            pl.when(k == 1)(lambda: both(gath.at[w, q, y_run, z_now, :, at]))
 
         per_piece(n, go)
 
@@ -225,9 +236,9 @@
                 c.start()
 
     def wait_blk(n):
-        def one(q, p):
-            blk_copies(n, q, p)[0].wait()
-            from_mate(n, q, p)
+        def one(q, i):
+            await_(in_blk(n, q, i, k_half), blk_loc.at[n % DEEP, i])
+            from_mate(n, q, i)
 
         per_piece(n, one)
 
@@ -238,7 +249,7 @@
             await_(mbuf.at[(n % 2, *there)], mat_r.at[n % 2, i])
 
     def release_blk(n):
-        per_piece(n, lambda q, p: blk_copies(n, q, p)[1].wait_send())
+        per_piece(n, lambda q, i: await_(in_blk(n, q, i, k_half), blk_s.at[n % DEEP, i]))
 
         @pl.when(n + DEEP < 2 * nb)
         def _():
@@ -574,11 +585,23 @@
     def c_copy(par):
         return remote(cm.at[par, _at(k, hsize)], cm.at[par, _at(k, hsize)], cm_s.at[par], cm_r.at[par], mate)
 
-    def apply(n):
-        def one(off, width):
-            ys[:, rows_at(off, width)] = ys[:, rows_at(off, width)] - _dot_nn(wb[n % 2], cut(n, off, width))
-
-        over((top - n) // 2, one)
+    def apply(n, off, width):
+        ys[:, rows_at(off, width)] = ys[:, rows_at(off, width)] - _dot_nn(wb[n % 2], cut(n, off, width))
+
+    def cross(n, off, width):
+        here = blk[n % DEEP, c_half, :, rows_at(off, width)].reshape(hsize, width)
+        cm[n % 2, _at(k, hsize)] += _dot_nt(here, cut(n + 1, off, width))
+
+    def by_half(j, act):
+        @pl.when(j >= nb // 2)
+        def _():
+            act((0,))
+            act((1,))
+
+        pl.when(j < nb // 2)(lambda: act((0, 1)))
+
+    def cols_in(gs):
+        return pl.ds(gs[0] * gcol, len(gs) * gcol)
 
     wait_blk(0)
     project(sbuf.at[0], ys, 0, top // 2)
@@ -589,29 +612,38 @@
 
     def reflect(n):
         j, par, nxt = top - n, n % 2, (n + 1) % 2
-        pl.when(n > 0)(lambda: apply(n - 1))
 
         @pl.when(j > 0)
         def _():
             wait_blk(n + 1)
             cm[par, _at(k, hsize)] = jnp.zeros((hsize, size), jnp.float32)
+            pl.when(j % 2 == 1)(lambda: cross(n, (j // 2) * STEP, STEP))
 
             def one(off, width):
-                here = blk[n % DEEP, c_half, :, rows_at(off, width)].reshape(hsize, width)
-                cm[par, _at(k, hsize)] += _dot_nt(here, cut(n + 1, off, width))
-
-            over(j // 2, one)
+                apply(n - 1, off, width)
+                cross(n, off, width)
+
+            over((j + 1) // 2, one)
             c_copy(par).start()
 
-        for g in range(2):
-            for d in range(1, chips):
-                rs_copy(par, g, d).wait_recv()
-            total = sbuf[par, slice_of(g, x)]
-            for d in range(1, chips):
-                total = total + rs[g, d - 1]
-            wb[par, slice_of(g, x)] = _dot_nn(total, mbuf[par])
-            for d in range(1, chips):
-                w_copy(par, g, d).start()
+        pl.when(j == 0)(lambda: over(0, functools.partial(apply, n - 1)))
+
+        def factor(gs):
+            totals = []
+            for g in gs:
+                for d in range(1, chips):
+                    rs_copy(par, g, d).wait_recv()
+                total = sbuf[par, slice_of(g, x)]
+                for d in range(1, chips):
+                    total = total + rs[g, d - 1]
+                totals.append(total)
+            got = _dot_nn(jnp.concatenate(totals, axis=0), mbuf[par])
+            for i, g in enumerate(gs):
+                wb[par, slice_of(g, x)] = got[i * sl : (i + 1) * sl]
+                for d in range(1, chips):
+                    w_copy(par, g, d).start()
+
+        by_half(j, factor)
 
         for g in range(2):
             for d in range(1, chips):
@@ -634,15 +666,19 @@
             wait_mat(n + 1)
             await_(cm.at[par, _at(1 - k, hsize)], cm_r.at[par])
 
-        for g in range(2):
-            for d in range(1, chips):
-                await_(wb.at[par, slice_of(g, peer(chips - d))], ex_r.at[g, d - 1])
+        def correct(gs):
+            for g in gs:
+                for d in range(1, chips):
+                    await_(wb.at[par, slice_of(g, peer(chips - d))], ex_r.at[g, d - 1])
 
             @pl.when(j > 0)
-            def _(g=g):
-                sbuf[nxt, cols_of(g)] = sbuf[nxt, cols_of(g)] - _dot_nn(wb[par, cols_of(g)], cm[par])
-                for d in range(1, chips):
-                    rs_copy(nxt, g, d).start()
+            def _():
+                sbuf[nxt, cols_in(gs)] = sbuf[nxt, cols_in(gs)] - _dot_nn(wb[par, cols_in(gs)], cm[par])
+                for g in gs:
+                    for d in range(1, chips):
+                        rs_copy(nxt, g, d).start()
+
+        by_half(j, correct)
 
         for g in range(2):
             for d in range(1, chips):
@@ -653,41 +689,44 @@
             c_copy(par).wait_send()
 
     _loop(0, nb, reflect)
-    apply(top)
+    over(0, functools.partial(apply, top))
     release_blk(top)
 
     xs[...] = jnp.zeros_like(xs)
-    first_half = lax.broadcasted_iota(jnp.int32, (gcol, LANES), 1) < EDGE
-
-    def take(ref, g, j):
-        lo = ref[cols_of(g), pl.ds(pl.multiple_of((j // 2) * STEP, LANES), LANES)]
-        hi = ref[cols_of(g), pl.ds(pl.multiple_of((j // 2) * STEP + LANES, LANES), LANES)]
+    def first_half(val):
+        return lax.broadcasted_iota(jnp.int32, val.shape, 1) < EDGE
+
+
+    def take(ref, cols_, j):
+        lo = ref[cols_, pl.ds(pl.multiple_of((j // 2) * STEP, LANES), LANES)]
+        hi = ref[cols_, pl.ds(pl.multiple_of((j // 2) * STEP + LANES, LANES), LANES)]
         even = j % 2 == 0
         return jnp.where(
-            first_half,
+            first_half(lo),
             jnp.where(even, lo, pltpu.roll(lo, EDGE, 1)),
             jnp.where(even, pltpu.roll(hi, EDGE, 1), hi),
         )
 
     def spread(val, j):
-        even = j % 2 == 0
+        even, first = j % 2 == 0, first_half(val)
         other = pltpu.roll(val, EDGE, 1)
         zero = jnp.zeros_like(val)
-        lo = jnp.where(even, jnp.where(first_half, val, zero), jnp.where(first_half, zero, other))
-        hi = jnp.where(even, jnp.where(first_half, other, zero), jnp.where(first_half, zero, val))
+        lo = jnp.where(even, jnp.where(first, val, zero), jnp.where(first, zero, other))
+        hi = jnp.where(even, jnp.where(first, other, zero), jnp.where(first, zero, val))
         return jnp.concatenate([lo, hi], axis=1)
 
     def x_copy(par, g, d):
         src = sbuf.at[par, cols_of(g), _at(peer(d), LANES)]
         return remote(src, rx.at[par, g, d - 1], rx_s.at[par, g, d - 1], rx_r.at[par, g, d - 1], at_peer(d))
 
-    def solve_partial(n, g, j):
-        par = n % 2
-        wb[0, cols_of(g)] = -wb[0, cols_of(g)]
-        wb[0, cols_of(g), _at(x, LANES)] += take(ys, g, j)
-        sbuf[par, cols_of(g)] = _dot_nn(wb[0, cols_of(g)], mbuf[par])
-        for d in range(1, chips):
-            x_copy(par, g, d).start()
+    def solve_partial(n, gs, j):
+        par, cols_ = n % 2, cols_in(gs)
+        wb[0, cols_] = -wb[0, cols_]
+        wb[0, cols_, _at(x, LANES)] += take(ys, cols_, j)
+        sbuf[par, cols_] = _dot_nn(wb[0, cols_], mbuf[par])
+        for g in gs:
+            for d in range(1, chips):
+                x_copy(par, g, d).start()
 
     def fin_copy(i):
         return remote(
@@ -714,7 +753,7 @@
     wait_mat(nb)
     wb[0] = jnp.zeros((ncol, size), jnp.float32)
     for g in range(2):
-        solve_partial(nb, g, top)
+        solve_partial(nb, (g,), top)
     release_blk(nb)
     release_mat(nb)
 
@@ -728,19 +767,25 @@
             wait_mat(n + 1)
             project(wb.at[0], xs, n + 1, (j + 1) // 2)
 
-        for g in range(2):
-            for d in range(1, chips):
-                x_copy(par, g, d).wait_recv()
-            val = sbuf[par, cols_of(g), _at(x, LANES)]
-            for d in range(1, chips):
-                val = val + rx[par, g, d - 1]
-            solved = spread(val, j)
-            xs[cols_of(g), _at(j // 2, STEP)] += solved
+        def finish(gs):
+            cols_ = cols_in(gs)
+            vals = []
+            for g in gs:
+                for d in range(1, chips):
+                    x_copy(par, g, d).wait_recv()
+                val = sbuf[par, cols_of(g), _at(x, LANES)]
+                for d in range(1, chips):
+                    val = val + rx[par, g, d - 1]
+                vals.append(val)
+            solved = spread(jnp.concatenate(vals, axis=0), j)
+            xs[cols_, _at(j // 2, STEP)] += solved
 
             @pl.when(j > 0)
-            def _(g=g, solved=solved):
-                wb[0, cols_of(g)] += _dot_nt(solved, cut(n + 1, (j // 2) * STEP, STEP))
-                solve_partial(n + 1, g, j - 1)
+            def _():
+                wb[0, cols_] += _dot_nt(solved, cut(n + 1, (j // 2) * STEP, STEP))
+                solve_partial(n + 1, gs, j - 1)
+
+        by_half(j, finish)
 
         pl.when(j % 2 == 0)(lambda: fin_copy(j // 2).start())
         pl.when(jnp.logical_and(j % 2 == 1, j < top))(lambda: give(j // 2 + 1))

time: 497 us -> 501 us (level)
  no operation moved by 1% of the time
where the time goes in v7:
time: 501 us; the launch traced here: 500 us
  Pallas kernels  493 us (98%)
  local copies, waits for them, and re-layouts  6.57 us (1%)
    pallas_call x1, Pallas kernels, local_work(): pl.pallas_call(functools.partial(_kernel, (rows, cols, slots, nb, ncol)),...  493 us

profile of v7, /device:TPU:1, one launch (start us, length us, event | category | flops | bytes accessed | tf_op | source)
XLA Modules:
  0.0 499.6 jit_solution(12421236812266457485)
XLA Ops:
  0.0 2.2 constant_dynamic-slice_fusion
  2.2 1.3 copy.6.t_in
  3.5 493.0 %eigvec.1 = (f32[1024,512]{1,0:T(8,128)}, f32[2,8,4,4,32,2048]{5,4,3,2,1,0:T(8,128)}) custom-call(f32[1024,512]{1,0:T(8,128)} %v_in.1, f32[8,64,64]{2,1,0:T(8,128)} %copy.6.t_in, f32[1024,512]{1,0:T(8,128)} %z_in.1, f32[1024,512]{1,0:T(8,128)} %l_in.1), custom_call_target="tpu_custom_call" | custom-call | tf_op jit(solution)/shard_map/eigvec/pallas_call | solution.py:830
  496.6 3.1 copy.8

commit v8 on v7

--- a/solution.py
+++ b/solution.py
@@ -592,14 +592,6 @@
         here = blk[n % DEEP, c_half, :, rows_at(off, width)].reshape(hsize, width)
         cm[n % 2, _at(k, hsize)] += _dot_nt(here, cut(n + 1, off, width))
 
-    def by_half(j, act):
-        @pl.when(j >= nb // 2)
-        def _():
-            act((0,))
-            act((1,))
-
-        pl.when(j < nb // 2)(lambda: act((0, 1)))
-
     def cols_in(gs):
         return pl.ds(gs[0] * gcol, len(gs) * gcol)
 
@@ -643,7 +635,8 @@
                 for d in range(1, chips):
                     w_copy(par, g, d).start()
 
-        by_half(j, factor)
+        factor((0,))
+        factor((1,))
 
         for g in range(2):
             for d in range(1, chips):
@@ -678,7 +671,8 @@
                     for d in range(1, chips):
                         rs_copy(nxt, g, d).start()
 
-        by_half(j, correct)
+        correct((0,))
+        correct((1,))
 
         for g in range(2):
             for d in range(1, chips):
@@ -785,7 +779,8 @@
                 wb[0, cols_] += _dot_nt(solved, cut(n + 1, (j // 2) * STEP, STEP))
                 solve_partial(n + 1, gs, j - 1)
 
-        by_half(j, finish)
+        finish((0,))
+        finish((1,))
 
         pl.when(j % 2 == 0)(lambda: fin_copy(j // 2).start())
         pl.when(jnp.logical_and(j % 2 == 1, j < top))(lambda: give(j // 2 + 1))
@@ -877,7 +872,7 @@
                 dma((2,)), dma((2,)),
                 dma((2, 2, peers)), dma((2, 2, peers)),
             ],
-            compiler_params=pltpu.CompilerParams(collective_id=0, has_side_effects=True, vmem_limit_bytes=63 * 1024 * 1024),
+            compiler_params=pltpu.CompilerParams(collective_id=0, has_side_effects=True, vmem_limit_bytes=67_043_328),
             name="eigvec",
         )(v_loc, t_mine, z_loc, l_loc)[0]
 

time: 501 us -> 488 us (0.974)
  Pallas kernels: 493 us -> 481 us
    pallas_call x1, Pallas kernels: 493 us -> 481 us  [local_work(): pl.pallas_call(functools.partial(_kernel, (rows, cols, slots, nb, ncol)),...]
where the time goes in v8:
time: 488 us
  Pallas kernels  481 us (99%)
  local copies, waits for them, and re-layouts  6.57 us (1%)
    pallas_call x1, Pallas kernels, local_work(): pl.pallas_call(functools.partial(_kernel, (rows, cols, slots, nb, ncol)),...  481 us

profile of v8, /device:TPU:1, one launch (start us, length us, event | category | flops | bytes accessed | tf_op | source)
XLA Modules:
  0.0 487.8 jit_solution(4621974830406664851)
XLA Ops:
  0.0 2.2 constant_dynamic-slice_fusion
  2.2 1.3 copy.6.t_in
  3.5 481.2 %eigvec.1 = (f32[1024,512]{1,0:T(8,128)}, f32[2,8,4,4,32,2048]{5,4,3,2,1,0:T(8,128)}) custom-call(f32[1024,512]{1,0:T(8,128)} %v_in.1, f32[8,64,64]{2,1,0:T(8,128)} %copy.6.t_in, f32[1024,512]{1,0:T(8,128)} %z_in.1, f32[1024,512]{1,0:T(8,128)} %l_in.1), custom_call_target="tpu_custom_call" | custom-call | tf_op jit(solution)/shard_map/eigvec/pallas_call | solution.py:825
  484.7 3.1 copy.8

commit v9 on v8

--- a/solution.py
+++ b/solution.py
@@ -49,7 +49,7 @@
     (stage, vt, zt, tb, own, ys, xs, vb, ld, lx, gm, pk, gx, r2, ga, xm, pm, mg, blk, mbuf, sbuf, rs, wb, cm, rx,
      in_sem, swap_l, swap_s, swap_r, v_s, v_r, l_s, l_r, lx_s, lx_r, gx_sem, r2_s, r2_r, ga_s, ga_r, fin_s, fin_r,
      ag_loc, ag_s, ag_r, blk_loc, blk_s, blk_r, mat_loc, mat_s, mat_r, free_b, free_m, rs_s, rs_r, ex_s, ex_r, cm_s, cm_r,
-     rx_s, rx_r) = scratch
+     rx_s, rx_r, eg_s, eg_r) = scratch
     rows, cols, slots, nb, ncol = dims
     row, col = lax.axis_index("row"), lax.axis_index("col")
     x, k = row // 2, row % 2
@@ -165,17 +165,70 @@
                 for i in range(8):
                     self.copy(i).wait_send()
 
+    class Eager(Slot):
+        def spot(self, db, da, part=None):
+            return self.piece(lax.rem(b + db, RING), lax.rem(a + da, RING), part)
+
+        def copy(self, i):
+            back = RING - 1
+            db, da, part, to_b, to_a = (
+                (0, 0, None, 0, 1), (0, 0, None, 0, back), (0, 0, None, 1, 0), (0, 0, None, back, 0),
+                (0, back, 0, 0, 1), (0, 1, 1, 0, back),
+                (0, back, None, 1, 0), (0, back, None, back, 0), (0, 1, None, 1, 0), (0, 1, None, back, 0),
+                (0, 2, None, 1, 0), (0, 2, None, back, 0),
+                (back, 0, None, 1, 0), (back, back, None, 1, 0), (1, 1, None, back, 0), (1, 2, None, back, 0),
+            )[i]
+            dst = self.spot(db, da, part)
+            src = self.own() if db == 0 and da == 0 else dst
+            sent_ = remote(src, dst, eg_s.at[i], eg_r.at[i], plane(to_a, to_b))
+            return sent_, self.spot(db + RING - to_b, da + RING - to_a, part)
+
+        def go(self, *which):
+            for i in which:
+                self.copy(i)[0].start()
+
+        def got(self, *which):
+            for i in which:
+                await_(self.copy(i)[1], eg_r.at[i])
+
+        def stage(self, s):
+            if s == 0:
+                self.go(0, 1, 2, 3)
+                self.kept().start()
+            elif s == 1:
+                self.got(0)
+                self.go(4, 6, 7)
+                self.got(1)
+                self.go(5, 8, 9)
+                self.got(2)
+                self.go(12)
+            elif s == 2:
+                self.got(4, 5)
+                self.go(10, 11)
+                self.got(6)
+                self.go(13)
+            elif s == 3:
+                self.got(9)
+                self.go(14)
+                self.got(11)
+                self.go(15)
+            elif s == 4:
+                self.got(3, 7, 8, 10, 12, 13, 14, 15)
+                self.kept().wait()
+                for i in range(16):
+                    self.copy(i)[0].wait_send()
+
     def tick(t):
         for s in (4, 3, 2, 1, 0, 5):
             n = t - s
             if isinstance(n, int):
                 if 0 <= n < len(order) and order[n] is not None:
-                    Slot(*order[n], n).stage(s)
+                    (Eager if order[n] == ("m", 0) else Slot)(*order[n], n).stage(s)
                 continue
             for kind in list(range(slots)) + ["m"]:
                 at_v, at_l = order.index((kind, 0)), order.index((kind, 1))
 
-                @pl.when(jnp.logical_or(n == at_v, n == at_l))
+                @pl.when(n == at_l if kind == "m" else jnp.logical_or(n == at_v, n == at_l))
                 def _(s=s, n=n, kind=kind, at_l=at_l):
                     Slot(kind, jnp.where(n == at_l, 1, 0), n).stage(s)
 
@@ -266,6 +319,52 @@
             pl.semaphore_signal(free_m.at[n % 2], inc=1, device_id=mate, device_id_type=MESH)
             pl.semaphore_wait(free_m.at[n % 2], 1)
             fetch_mat(n + 2)
+
+    def over(first, body):
+        pl.when(first % 2 == 1)(lambda: body(first * STEP, STEP))
+        _loop((first + 1) // 2, whole // 2, lambda i: body(i * 2 * STEP, 2 * STEP))
+
+    def rows_at(off, width):
+        return pl.ds(pl.multiple_of(off, STEP), width)
+
+    def cut(n, off, width):
+        return blk[n % DEEP, :, :, rows_at(off, width)].reshape(size, width)
+
+    def project(dst, ref, n, first):
+        dst[...] = jnp.zeros((ncol, size), jnp.float32)
+
+        def one(off, width):
+            dst[...] += _dot_nt(ref[:, rows_at(off, width)], cut(n, off, width))
+
+        over(first, one)
+
+    def slice_of(g, x2):
+        return pl.ds(pl.multiple_of(g * gcol + x2 * sl, sl), sl)
+
+    def cols_of(g):
+        return pl.ds(g * gcol, gcol)
+
+    def rs_copy(par, g, d):
+        return remote(sbuf.at[par, slice_of(g, peer(d))], rs.at[g, d - 1], rs_s.at[g, d - 1], rs_r.at[g, d - 1], at_peer(d))
+
+    def w_copy(par, g, d):
+        mine = wb.at[par, slice_of(g, x)]
+        return remote(mine, mine, ex_s.at[g, d - 1], ex_r.at[g, d - 1], at_peer(d))
+
+    c_half = pl.ds(pl.multiple_of(k * (rows // 2), rows // 2), rows // 2)
+
+    def c_copy(par):
+        return remote(cm.at[par, _at(k, hsize)], cm.at[par, _at(k, hsize)], cm_s.at[par], cm_r.at[par], mate)
+
+    def apply(n, off, width):
+        ys[:, rows_at(off, width)] = ys[:, rows_at(off, width)] - _dot_nn(wb[n % 2], cut(n, off, width))
+
+    def cross(n, off, width):
+        here = blk[n % DEEP, c_half, :, rows_at(off, width)].reshape(hsize, width)
+        cm[n % 2, _at(k, hsize)] += _dot_nt(here, cut(n + 1, off, width))
+
+    def cols_in(gs):
+        return pl.ds(gs[0] * gcol, len(gs) * gcol)
 
     barrier = pltpu.get_barrier_semaphore()
 
@@ -540,6 +639,11 @@
     tick(5)
     _loop(0, 3, level_l)
     tick(6)
+    wait_blk(0)
+    project(sbuf.at[0], ys, 0, top // 2)
+    for g in range(2):
+        for d in range(1, chips):
+            rs_copy(0, g, d).start()
     _loop(3, 7, level_l)
     tick(7)
     level_big(1, lambda w_, i: gm[pl.ds((2 * i + 1) * w_, w_), pl.ds(2 * i * w_, w_)])
@@ -549,57 +653,6 @@
     fetch_mat(1)
     fetch_blk(2)
 
-    def over(first, body):
-        pl.when(first % 2 == 1)(lambda: body(first * STEP, STEP))
-        _loop((first + 1) // 2, whole // 2, lambda i: body(i * 2 * STEP, 2 * STEP))
-
-    def rows_at(off, width):
-        return pl.ds(pl.multiple_of(off, STEP), width)
-
-    def cut(n, off, width):
-        return blk[n % DEEP, :, :, rows_at(off, width)].reshape(size, width)
-
-    def project(dst, ref, n, first):
-        dst[...] = jnp.zeros((ncol, size), jnp.float32)
-
-        def one(off, width):
-            dst[...] += _dot_nt(ref[:, rows_at(off, width)], cut(n, off, width))
-
-        over(first, one)
-
-    def slice_of(g, x2):
-        return pl.ds(pl.multiple_of(g * gcol + x2 * sl, sl), sl)
-
-    def cols_of(g):
-        return pl.ds(g * gcol, gcol)
-
-    def rs_copy(par, g, d):
-        return remote(sbuf.at[par, slice_of(g, peer(d))], rs.at[g, d - 1], rs_s.at[g, d - 1], rs_r.at[g, d - 1], at_peer(d))
-
-    def w_copy(par, g, d):
-        mine = wb.at[par, slice_of(g, x)]
-        return remote(mine, mine, ex_s.at[g, d - 1], ex_r.at[g, d - 1], at_peer(d))
-
-    c_half = pl.ds(pl.multiple_of(k * (rows // 2), rows // 2), rows // 2)
-
-    def c_copy(par):
-        return remote(cm.at[par, _at(k, hsize)], cm.at[par, _at(k, hsize)], cm_s.at[par], cm_r.at[par], mate)
-
-    def apply(n, off, width):
-        ys[:, rows_at(off, width)] = ys[:, rows_at(off, width)] - _dot_nn(wb[n % 2], cut(n, off, width))
-
-    def cross(n, off, width):
-        here = blk[n % DEEP, c_half, :, rows_at(off, width)].reshape(hsize, width)
-        cm[n % 2, _at(k, hsize)] += _dot_nt(here, cut(n + 1, off, width))
-
-    def cols_in(gs):
-        return pl.ds(gs[0] * gcol, len(gs) * gcol)
-
-    wait_blk(0)
-    project(sbuf.at[0], ys, 0, top // 2)
-    for g in range(2):
-        for d in range(1, chips):
-            rs_copy(0, g, d).start()
     wait_mat(0)
 
     def reflect(n):
@@ -871,6 +924,7 @@
                 dma((2, peers)), dma((2, peers)), dma((2, peers)), dma((2, peers)),
                 dma((2,)), dma((2,)),
                 dma((2, 2, peers)), dma((2, 2, peers)),
+                dma((16,)), dma((16,)),
             ],
             compiler_params=pltpu.CompilerParams(collective_id=0, has_side_effects=True, vmem_limit_bytes=67_043_328),
             name="eigvec",

time: 488 us -> 484 us (level)
  no operation moved by 1% of the time
where the time goes in v9:
time: 484 us
  Pallas kernels  477 us (99%)
  local copies, waits for them, and re-layouts  6.57 us (1%)
    pallas_call x1, Pallas kernels, local_work(): pl.pallas_call(functools.partial(_kernel, (rows, cols, slots, nb, ncol)),...  477 us

profile of v9, /device:TPU:1, one launch (start us, length us, event | category | flops | bytes accessed | tf_op | source)
XLA Modules:
  0.0 483.8 jit_solution(8472790345724396506)
XLA Ops:
  0.0 2.2 constant_dynamic-slice_fusion
  2.2 1.3 copy.6.t_in
  3.5 477.3 %eigvec.1 = (f32[1024,512]{1,0:T(8,128)}, f32[2,8,4,4,32,2048]{5,4,3,2,1,0:T(8,128)}) custom-call(f32[1024,512]{1,0:T(8,128)} %v_in.1, f32[8,64,64]{2,1,0:T(8,128)} %copy.6.t_in, f32[1024,512]{1,0:T(8,128)} %z_in.1, f32[1024,512]{1,0:T(8,128)} %l_in.1), custom_call_target="tpu_custom_call" | custom-call | tf_op jit(solution)/shard_map/eigvec/pallas_call | solution.py:878
  480.8 3.1 copy.8

commit v10 on v9

--- a/solution.py
+++ b/solution.py
@@ -46,10 +46,11 @@
 
 
 def _kernel(dims, v_in, t_in, z_in, l_in, out_ref, gath, *scratch):
-    (stage, vt, zt, tb, own, ys, xs, vb, ld, lx, gm, pk, gx, r2, ga, xm, pm, mg, blk, mbuf, sbuf, rs, wb, cm, rx,
+    (stage, vt, zt, tb, own, ys, xs, vb, ld, lx, gm, pk, gx, r2, ga, pm, mg, blk, mbuf, sbuf, rs, wb, cm, rx,
      in_sem, swap_l, swap_s, swap_r, v_s, v_r, l_s, l_r, lx_s, lx_r, gx_sem, r2_s, r2_r, ga_s, ga_r, fin_s, fin_r,
      ag_loc, ag_s, ag_r, blk_loc, blk_s, blk_r, mat_loc, mat_s, mat_r, free_b, free_m, rs_s, rs_r, ex_s, ex_r, cm_s, cm_r,
      rx_s, rx_r, eg_s, eg_r) = scratch
+    xm = cm
     rows, cols, slots, nb, ncol = dims
     row, col = lax.axis_index("row"), lax.axis_index("col")
     x, k = row // 2, row % 2
@@ -336,7 +337,13 @@
         def one(off, width):
             dst[...] += _dot_nt(ref[:, rows_at(off, width)], cut(n, off, width))
 
-        over(first, one)
+        if whole % 4 or isinstance(first, int):
+            over(first, one)
+            return
+        half = (first + 1) // 2
+        pl.when(first % 2 == 1)(lambda: one(first * STEP, STEP))
+        pl.when(half % 2 == 1)(lambda: one(half * 2 * STEP, 2 * STEP))
+        _loop((half + 1) // 2, whole // 4, lambda i: one(i * 4 * STEP, 4 * STEP))
 
     def slice_of(g, x2):
         return pl.ds(pl.multiple_of(g * gcol + x2 * sl, sl), sl)
@@ -695,20 +702,19 @@
             for d in range(1, chips):
                 rs_copy(par, g, d).wait_send()
 
-        @pl.when(jnp.logical_and(n < 8, par == 0))
-        def _():
-            tick(LEAD + n // 2)
-
-        @pl.when(n >= 8)
-        def _():
-            tick(LEAD - 4 + n)
-
         pl.when(n > 0)(lambda: release_blk(n - 1))
         release_mat(n)
 
         @pl.when(j > 0)
         def _():
             project(sbuf.at[nxt], ys, n + 1, (j - 1) // 2)
+
+        @pl.when(jnp.logical_or(n >= 8, par == 0))
+        def _():
+            tick(jnp.where(n < 8, LEAD + n // 2, LEAD - 4 + n))
+
+        @pl.when(j > 0)
+        def _():
             wait_mat(n + 1)
             await_(cm.at[par, _at(1 - k, hsize)], cm_r.at[par])
 
@@ -899,7 +905,6 @@
                 buf(size // 4, size),
                 buf(peers, size // 4 // chips, size),
                 buf(size // 2, size),
-                buf(2, size, size),
                 buf(2, EDGE, tri),
                 buf(2, RING, RING, EDGE, tri),
                 buf(DEEP, rows, EDGE, lanes),

time: 484 us -> 484 us (level)
  no operation moved by 1% of the time
where the time goes in v10:
time: 484 us
  Pallas kernels  477 us (99%)
  local copies, waits for them, and re-layouts  6.57 us (1%)
    pallas_call x1, Pallas kernels, local_work(): pl.pallas_call(functools.partial(_kernel, (rows, cols, slots, nb, ncol)),...  477 us

profile of v10, /device:TPU:1, one launch (start us, length us, event | category | flops | bytes accessed | tf_op | source)
XLA Modules:
  0.0 483.9 jit_solution(7247078284472311558)
XLA Ops:
  0.0 2.2 constant_dynamic-slice_fusion
  2.2 1.3 copy.6.t_in
  3.5 477.3 %eigvec.1 = (f32[1024,512]{1,0:T(8,128)}, f32[2,8,4,4,32,2048]{5,4,3,2,1,0:T(8,128)}) custom-call(f32[1024,512]{1,0:T(8,128)} %v_in.1, f32[8,64,64]{2,1,0:T(8,128)} %copy.6.t_in, f32[1024,512]{1,0:T(8,128)} %z_in.1, f32[1024,512]{1,0:T(8,128)} %l_in.1), custom_call_target="tpu_custom_call" | custom-call | tf_op jit(solution)/shard_map/eigvec/pallas_call | solution.py:884
  480.8 3.1 copy.8

commit v11 on v10

--- a/solution.py
+++ b/solution.py
@@ -709,9 +709,9 @@
         def _():
             project(sbuf.at[nxt], ys, n + 1, (j - 1) // 2)
 
-        @pl.when(jnp.logical_or(n >= 8, par == 0))
+        @pl.when(jnp.where(n < 9, par == 0, par == 1))
         def _():
-            tick(jnp.where(n < 8, LEAD + n // 2, LEAD - 4 + n))
+            tick(LEAD + (n + 1) // 2)
 
         @pl.when(j > 0)
         def _():
@@ -848,12 +848,14 @@
             for d in range(1, chips):
                 x_copy(par, g, d).wait_send()
 
+        @pl.when(jnp.logical_or(i == 0, i % 2 == 1))
+        def _():
+            tick(LEAD + 9 + (i + 1) // 2)
+
         @pl.when(j > 0)
         def _():
             release_blk(n + 1)
             release_mat(n + 1)
-
-        tick(LEAD - 4 + n)
 
     _loop(0, nb, solve)
 

time: 484 us -> 482 us (level)
  no operation moved by 1% of the time
where the time goes in v11:
time: 482 us
  Pallas kernels  475 us (99%)
  local copies, waits for them, and re-layouts  6.57 us (1%)
    pallas_call x1, Pallas kernels, local_work(): pl.pallas_call(functools.partial(_kernel, (rows, cols, slots, nb, ncol)),...  475 us

profile of v11, /device:TPU:1, one launch (start us, length us, event | category | flops | bytes accessed | tf_op | source)
XLA Modules:
  0.0 482.1 jit_solution(754756505885250241)
XLA Ops:
  0.0 2.2 constant_dynamic-slice_fusion
  2.2 1.3 copy.6.t_in
  3.5 475.5 %eigvec.1 = (f32[1024,512]{1,0:T(8,128)}, f32[2,8,4,4,32,2048]{5,4,3,2,1,0:T(8,128)}) custom-call(f32[1024,512]{1,0:T(8,128)} %v_in.1, f32[8,64,64]{2,1,0:T(8,128)} %copy.6.t_in, f32[1024,512]{1,0:T(8,128)} %z_in.1, f32[1024,512]{1,0:T(8,128)} %l_in.1), custom_call_target="tpu_custom_call" | custom-call | tf_op jit(solution)/shard_map/eigvec/pallas_call | solution.py:886
  479.0 3.1 copy.8

commit v12 on v11

--- a/solution.py
+++ b/solution.py
@@ -360,15 +360,22 @@
 
     c_half = pl.ds(pl.multiple_of(k * (rows // 2), rows // 2), rows // 2)
 
-    def c_copy(par):
-        return remote(cm.at[par, _at(k, hsize)], cm.at[par, _at(k, hsize)], cm_s.at[par], cm_r.at[par], mate)
+    def c_copy(n):
+        mine = cm.at[n % 3, _at(k, hsize)]
+        return remote(mine, mine, cm_s.at[n % 3], cm_r.at[n % 3], mate)
 
     def apply(n, off, width):
         ys[:, rows_at(off, width)] = ys[:, rows_at(off, width)] - _dot_nn(wb[n % 2], cut(n, off, width))
 
     def cross(n, off, width):
         here = blk[n % DEEP, c_half, :, rows_at(off, width)].reshape(hsize, width)
-        cm[n % 2, _at(k, hsize)] += _dot_nt(here, cut(n + 1, off, width))
+        cm[n % 3, _at(k, hsize)] += _dot_nt(here, cut(n + 1, off, width))
+
+    def cross_all(n):
+        wait_blk(n + 1)
+        cm[n % 3, _at(k, hsize)] = jnp.zeros((hsize, size), jnp.float32)
+        over((top - n) // 2, functools.partial(cross, n))
+        c_copy(n).start()
 
     def cols_in(gs):
         return pl.ds(gs[0] * gcol, len(gs) * gcol)
@@ -661,24 +668,15 @@
     fetch_blk(2)
 
     wait_mat(0)
+    wait_blk(1)
+    cm[0, _at(k, hsize)] = jnp.zeros((hsize, size), jnp.float32)
+    cross(0, (whole - 1) * STEP, STEP)
+    c_copy(0).start()
 
     def reflect(n):
         j, par, nxt = top - n, n % 2, (n + 1) % 2
 
-        @pl.when(j > 0)
-        def _():
-            wait_blk(n + 1)
-            cm[par, _at(k, hsize)] = jnp.zeros((hsize, size), jnp.float32)
-            pl.when(j % 2 == 1)(lambda: cross(n, (j // 2) * STEP, STEP))
-
-            def one(off, width):
-                apply(n - 1, off, width)
-                cross(n, off, width)
-
-            over((j + 1) // 2, one)
-            c_copy(par).start()
-
-        pl.when(j == 0)(lambda: over(0, functools.partial(apply, n - 1)))
+        pl.when(n > 0)(lambda: over((j + 1) // 2, functools.partial(apply, n - 1)))
 
         def factor(gs):
             totals = []
@@ -716,7 +714,7 @@
         @pl.when(j > 0)
         def _():
             wait_mat(n + 1)
-            await_(cm.at[par, _at(1 - k, hsize)], cm_r.at[par])
+            await_(cm.at[n % 3, _at(1 - k, hsize)], cm_r.at[n % 3])
 
         def correct(gs):
             for g in gs:
@@ -725,12 +723,13 @@
 
             @pl.when(j > 0)
             def _():
-                sbuf[nxt, cols_in(gs)] = sbuf[nxt, cols_in(gs)] - _dot_nn(wb[par, cols_in(gs)], cm[par])
+                sbuf[nxt, cols_in(gs)] = sbuf[nxt, cols_in(gs)] - _dot_nn(wb[par, cols_in(gs)], cm[n % 3])
                 for g in gs:
                     for d in range(1, chips):
                         rs_copy(nxt, g, d).start()
 
         correct((0,))
+        pl.when(j > 1)(lambda: cross_all(n + 1))
         correct((1,))
 
         for g in range(2):
@@ -739,7 +738,7 @@
 
         @pl.when(j > 0)
         def _():
-            c_copy(par).wait_send()
+            c_copy(n).wait_send()
 
     _loop(0, nb, reflect)
     over(0, functools.partial(apply, top))
@@ -914,7 +913,7 @@
                 buf(2, ncol, size),
                 buf(2, peers, sl, size),
                 buf(2, ncol, size),
-                buf(2, size, size),
+                buf(3, size, size),
                 buf(2, 2, peers, gcol, LANES),
                 dma((4,)),
                 dma((3, pairs)), dma((3, pairs)), dma((3, pairs)),
@@ -929,7 +928,7 @@
                 dma((2, n128)), dma((2, n128)), dma((2, n128)),
                 pltpu.SemaphoreType.REGULAR((DEEP,)), pltpu.SemaphoreType.REGULAR((2,)),
                 dma((2, peers)), dma((2, peers)), dma((2, peers)), dma((2, peers)),
-                dma((2,)), dma((2,)),
+                dma((3,)), dma((3,)),
                 dma((2, 2, peers)), dma((2, 2, peers)),
                 dma((16,)), dma((16,)),
             ],

time: 482 us -> 487 us (1.010)
  Pallas kernels: 475 us -> 481 us
    pallas_call x1, Pallas kernels: 475 us -> 481 us  [local_work(): pl.pallas_call(functools.partial(_kernel, (rows, cols, slots, nb, ncol)),...]
where the time goes in v12:
time: 487 us
  Pallas kernels  481 us (99%)
  local copies, waits for them, and re-layouts  6.57 us (1%)
    pallas_call x1, Pallas kernels, local_work(): pl.pallas_call(functools.partial(_kernel, (rows, cols, slots, nb, ncol)),...  481 us

profile of v12, /device:TPU:1, one launch (start us, length us, event | category | flops | bytes accessed | tf_op | source)
XLA Modules:
  0.0 487.3 jit_solution(8520861881919166219)
XLA Ops:
  0.0 2.2 constant_dynamic-slice_fusion
  2.2 1.3 copy.6.t_in
  3.5 480.7 %eigvec.1 = (f32[1024,512]{1,0:T(8,128)}, f32[2,8,4,4,32,2048]{5,4,3,2,1,0:T(8,128)}) custom-call(f32[1024,512]{1,0:T(8,128)} %v_in.1, f32[8,64,64]{2,1,0:T(8,128)} %copy.6.t_in, f32[1024,512]{1,0:T(8,128)} %z_in.1, f32[1024,512]{1,0:T(8,128)} %l_in.1), custom_call_target="tpu_custom_call" | custom-call | tf_op jit(solution)/shard_map/eigvec/pallas_call | solution.py:885
  484.2 3.1 copy.8

commit v13 on v11

--- a/solution.py
+++ b/solution.py
@@ -363,6 +363,14 @@
     def c_copy(par):
         return remote(cm.at[par, _at(k, hsize)], cm.at[par, _at(k, hsize)], cm_s.at[par], cm_r.at[par], mate)
 
+    def summed(par, g):
+        for d in range(1, chips):
+            rs_copy(par, g, d).wait_recv()
+        total = sbuf[par, slice_of(g, x)]
+        for d in range(1, chips):
+            total = total + rs[g, d - 1]
+        return total
+
     def apply(n, off, width):
         ys[:, rows_at(off, width)] = ys[:, rows_at(off, width)] - _dot_nn(wb[n % 2], cut(n, off, width))
 
@@ -653,14 +661,24 @@
             rs_copy(0, g, d).start()
     _loop(3, 7, level_l)
     tick(7)
+    for g in range(2):
+        wb[1, slice_of(g, x)] = summed(0, g)
+        for d in range(1, chips):
+            w_copy(1, g, d).start()
     level_big(1, lambda w_, i: gm[pl.ds((2 * i + 1) * w_, w_), pl.ds(2 * i * w_, w_)])
     pack_factor(1)
     tick(8)
     fetch_mat(0)
     fetch_mat(1)
     fetch_blk(2)
+    for g in range(2):
+        for d in range(1, chips):
+            await_(wb.at[1, slice_of(g, peer(chips - d))], ex_r.at[g, d - 1])
+            w_copy(1, g, d).wait_send()
+            rs_copy(0, g, d).wait_send()
 
     wait_mat(0)
+    wb[0] = _dot_nn(wb[1], mbuf[0])
 
     def reflect(n):
         j, par, nxt = top - n, n % 2, (n + 1) % 2
@@ -681,26 +699,24 @@
         pl.when(j == 0)(lambda: over(0, functools.partial(apply, n - 1)))
 
         def factor(gs):
-            totals = []
-            for g in gs:
-                for d in range(1, chips):
-                    rs_copy(par, g, d).wait_recv()
-                total = sbuf[par, slice_of(g, x)]
-                for d in range(1, chips):
-                    total = total + rs[g, d - 1]
-                totals.append(total)
-            got = _dot_nn(jnp.concatenate(totals, axis=0), mbuf[par])
+            got = _dot_nn(jnp.concatenate([summed(par, g) for g in gs], axis=0), mbuf[par])
             for i, g in enumerate(gs):
                 wb[par, slice_of(g, x)] = got[i * sl : (i + 1) * sl]
                 for d in range(1, chips):
                     w_copy(par, g, d).start()
 
-        factor((0,))
-        factor((1,))
-
-        for g in range(2):
-            for d in range(1, chips):
-                rs_copy(par, g, d).wait_send()
+        @pl.when(jnp.logical_and(n > 0, j >= 7))
+        def _():
+            factor((0,))
+            factor((1,))
+
+        pl.when(jnp.logical_and(n > 0, j < 7))(lambda: factor((0, 1)))
+
+        @pl.when(n > 0)
+        def _():
+            for g in range(2):
+                for d in range(1, chips):
+                    rs_copy(par, g, d).wait_send()
 
         pl.when(n > 0)(lambda: release_blk(n - 1))
         release_mat(n)
@@ -719,9 +735,11 @@
             await_(cm.at[par, _at(1 - k, hsize)], cm_r.at[par])
 
         def correct(gs):
-            for g in gs:
-                for d in range(1, chips):
-                    await_(wb.at[par, slice_of(g, peer(chips - d))], ex_r.at[g, d - 1])
+            @pl.when(n > 0)
+            def _():
+                for g in gs:
+                    for d in range(1, chips):
+                        await_(wb.at[par, slice_of(g, peer(chips - d))], ex_r.at[g, d - 1])
 
             @pl.when(j > 0)
             def _():
@@ -733,9 +751,11 @@
         correct((0,))
         correct((1,))
 
-        for g in range(2):
-            for d in range(1, chips):
-                w_copy(par, g, d).wait_send()
+        @pl.when(n > 0)
+        def _():
+            for g in range(2):
+                for d in range(1, chips):
+                    w_copy(par, g, d).wait_send()
 
         @pl.when(j > 0)
         def _():

time: 482 us -> 484 us (level)
  no operation moved by 1% of the time
where the time goes in v13:
time: 484 us
  Pallas kernels  477 us (99%)
  local copies, waits for them, and re-layouts  6.57 us (1%)
    pallas_call x1, Pallas kernels, local_work(): pl.pallas_call(functools.partial(_kernel, (rows, cols, slots, nb, ncol)),...  477 us

profile of v13, /device:TPU:1, one launch (start us, length us, event | category | flops | bytes accessed | tf_op | source)
XLA Modules:
  0.0 483.7 jit_solution(14014915700119897161)
XLA Ops:
  0.0 2.2 constant_dynamic-slice_fusion
  2.2 1.3 copy.6.t_in
  3.5 477.1 %eigvec.1 = (f32[1024,512]{1,0:T(8,128)}, f32[2,8,4,4,32,2048]{5,4,3,2,1,0:T(8,128)}) custom-call(f32[1024,512]{1,0:T(8,128)} %v_in.1, f32[8,64,64]{2,1,0:T(8,128)} %copy.6.t_in, f32[1024,512]{1,0:T(8,128)} %z_in.1, f32[1024,512]{1,0:T(8,128)} %l_in.1), custom_call_target="tpu_custom_call" | custom-call | tf_op jit(solution)/shard_map/eigvec/pallas_call | solution.py:906
  480.6 3.1 copy.8

commit v14 on v13

--- a/solution.py
+++ b/solution.py
@@ -39,7 +39,7 @@
 
 
 def _gathers(slots):
-    early = [(slots - 1, 0), (slots - 2, 0), None, None, ("m", 0)]
+    early = [(slots - 1, 0), (slots - 2, 0), None, None, ("m", 0), None]
     first = early + [(q, 0) for q in range(slots - 3, -1, -1)]
     rest = [(slots - 1, 1), ("m", 1)] + [(q, 1) for q in range(slots - 2, -1, -1)]
     return first + [None] * (LEAD - len(first)) + rest
@@ -725,9 +725,9 @@
         def _():
             project(sbuf.at[nxt], ys, n + 1, (j - 1) // 2)
 
-        @pl.when(jnp.where(n < 9, par == 0, par == 1))
-        def _():
-            tick(LEAD + (n + 1) // 2)
+        @pl.when(jnp.logical_or(par == 1, jnp.logical_or(n == 0, n == 12)))
+        def _():
+            tick(LEAD + (n + 1) // 2 + jnp.where(n >= 12, 1, 0))
 
         @pl.when(j > 0)
         def _():
@@ -870,7 +870,7 @@
 
         @pl.when(jnp.logical_or(i == 0, i % 2 == 1))
         def _():
-            tick(LEAD + 9 + (i + 1) // 2)
+            tick(LEAD + 10 + (i + 1) // 2)
 
         @pl.when(j > 0)
         def _():

time: 484 us -> 479 us (0.990)
  no operation moved by 1% of the time
where the time goes in v14:
time: 479 us
  Pallas kernels  473 us (99%)
  local copies, waits for them, and re-layouts  6.57 us (1%)
    pallas_call x1, Pallas kernels, local_work(): pl.pallas_call(functools.partial(_kernel, (rows, cols, slots, nb, ncol)),...  473 us

profile of v14, /device:TPU:1, one launch (start us, length us, event | category | flops | bytes accessed | tf_op | source)
XLA Modules:
  0.0 479.3 jit_solution(15744260940335297816)
XLA Ops:
  0.0 2.2 constant_dynamic-slice_fusion
  2.2 1.3 copy.6.t_in
  3.5 472.7 %eigvec.1 = (f32[1024,512]{1,0:T(8,128)}, f32[2,8,4,4,32,2048]{5,4,3,2,1,0:T(8,128)}) custom-call(f32[1024,512]{1,0:T(8,128)} %v_in.1, f32[8,64,64]{2,1,0:T(8,128)} %copy.6.t_in, f32[1024,512]{1,0:T(8,128)} %z_in.1, f32[1024,512]{1,0:T(8,128)} %l_in.1), custom_call_target="tpu_custom_call" | custom-call | tf_op jit(solution)/shard_map/eigvec/pallas_call | solution.py:906
  476.2 3.1 copy.8

commit v15 on v14

--- a/solution.py
+++ b/solution.py
@@ -725,7 +725,7 @@
         def _():
             project(sbuf.at[nxt], ys, n + 1, (j - 1) // 2)
 
-        @pl.when(jnp.logical_or(par == 1, jnp.logical_or(n == 0, n == 12)))
+        @pl.when(jnp.logical_or(par == 1, n == 12))
         def _():
             tick(LEAD + (n + 1) // 2 + jnp.where(n >= 12, 1, 0))
 
@@ -750,6 +750,7 @@
 
         correct((0,))
         correct((1,))
+        pl.when(n == 0)(lambda: tick(LEAD))
 
         @pl.when(n > 0)
         def _():

time: 479 us -> 477 us (level)
  no operation moved by 1% of the time
where the time goes in v15:
time: 477 us
  Pallas kernels  470 us (99%)
  local copies, waits for them, and re-layouts  6.57 us (1%)
    pallas_call x1, Pallas kernels, local_work(): pl.pallas_call(functools.partial(_kernel, (rows, cols, slots, nb, ncol)),...  470 us

profile of v15, /device:TPU:1, one launch (start us, length us, event | category | flops | bytes accessed | tf_op | source)
XLA Modules:
  0.0 476.7 jit_solution(15214064444175188627)
XLA Ops:
  0.0 2.2 constant_dynamic-slice_fusion
  2.2 1.3 copy.6.t_in
  3.5 470.1 %eigvec.1 = (f32[1024,512]{1,0:T(8,128)}, f32[2,8,4,4,32,2048]{5,4,3,2,1,0:T(8,128)}) custom-call(f32[1024,512]{1,0:T(8,128)} %v_in.1, f32[8,64,64]{2,1,0:T(8,128)} %copy.6.t_in, f32[1024,512]{1,0:T(8,128)} %z_in.1, f32[1024,512]{1,0:T(8,128)} %l_in.1), custom_call_target="tpu_custom_call" | custom-call | tf_op jit(solution)/shard_map/eigvec/pallas_call | solution.py:907
  473.6 3.1 copy.8

commit v16 on v15

--- a/solution.py
+++ b/solution.py
@@ -219,8 +219,8 @@
                 for i in range(16):
                     self.copy(i)[0].wait_send()
 
-    def tick(t):
-        for s in (4, 3, 2, 1, 0, 5):
+    def tick(t, stages=(4, 3, 2, 1, 0, 5)):
+        for s in stages:
             n = t - s
             if isinstance(n, int):
                 if 0 <= n < len(order) and order[n] is not None:
@@ -667,7 +667,7 @@
             w_copy(1, g, d).start()
     level_big(1, lambda w_, i: gm[pl.ds((2 * i + 1) * w_, w_), pl.ds(2 * i * w_, w_)])
     pack_factor(1)
-    tick(8)
+    tick(8, (4,))
     fetch_mat(0)
     fetch_mat(1)
     fetch_blk(2)
@@ -727,7 +727,7 @@
 
         @pl.when(jnp.logical_or(par == 1, n == 12))
         def _():
-            tick(LEAD + (n + 1) // 2 + jnp.where(n >= 12, 1, 0))
+            tick(LEAD + (n + 1) // 2 + jnp.where(n >= 12, 1, 0) - jnp.where(n == 1, 1, 0))
 
         @pl.when(j > 0)
         def _():
@@ -750,7 +750,8 @@
 
         correct((0,))
         correct((1,))
-        pl.when(n == 0)(lambda: tick(LEAD))
+        pl.when(n == 0)(lambda: tick(8, (3, 2, 1, 0, 5)))
+        pl.when(n == 1)(lambda: tick(10))
 
         @pl.when(n > 0)
         def _():

time: 477 us -> 481 us (level)
  no operation moved by 1% of the time
where the time goes in v16:
time: 481 us
  Pallas kernels  474 us (99%)
  local copies, waits for them, and re-layouts  6.57 us (1%)
    pallas_call x1, Pallas kernels, local_work(): pl.pallas_call(functools.partial(_kernel, (rows, cols, slots, nb, ncol)),...  474 us

profile of v16, /device:TPU:1, one launch (start us, length us, event | category | flops | bytes accessed | tf_op | source)
XLA Modules:
  0.0 481.0 jit_solution(8713682129010585530)
XLA Ops:
  0.0 2.2 constant_dynamic-slice_fusion
  2.2 1.3 copy.6.t_in
  3.5 474.5 %eigvec.1 = (f32[1024,512]{1,0:T(8,128)}, f32[2,8,4,4,32,2048]{5,4,3,2,1,0:T(8,128)}) custom-call(f32[1024,512]{1,0:T(8,128)} %v_in.1, f32[8,64,64]{2,1,0:T(8,128)} %copy.6.t_in, f32[1024,512]{1,0:T(8,128)} %z_in.1, f32[1024,512]{1,0:T(8,128)} %l_in.1), custom_call_target="tpu_custom_call" | custom-call | tf_op jit(solution)/shard_map/eigvec/pallas_call | solution.py:908
  478.0 3.1 copy.8
